TPU v7x, 256 devices: a whole 4x4x8 slice. The times are simulated.
256 devices in a mesh: ens: 8 (over y_hi, x), lon: 32 (over z, y_lo, core).
Axes of the slice: x: 4, y: 4 (y_hi: 2, y_lo: 2; y = y_hi * 2 + y_lo), z: 8, core: 2. Of those that a mesh axis runs over, the one named last changes fastest.
Arguments:
- control: float32 [16, 1024, 2048], P('ens', None, 'lon'), may hold values from -6 to 6
- residual: float32 [16, 1024, 2048], P('ens', None, 'lon'), may hold values from -6 to 6
- direction: float32 [16, 1024, 2048], P('ens', None, 'lon'), may hold values from -6 to 6
- ens_perturb: bfloat16 [16, 3, 1024, 2048], P('ens', None, None, 'lon'), may hold values from -1.5 to 1.5
- localize: float32 [1024, 1024], replicated, may hold values from -0.5 to 1.5
- obs_cell: int32 [131072], P('lon'), may hold values from 0 to 65535
- obs_slot: int32 [131072], P('lon'), may hold values from 0 to 3
- obs_weight: float32 [131072], P('lon'), may hold values from 0.5 to 4
Outputs:
- control_new: float32 [16, 1024, 2048], P('ens', None, 'lon')
- residual_new: float32 [16, 1024, 2048], P('ens', None, 'lon')
- direction_new: float32 [16, 1024, 2048], P('ens', None, 'lon')
Inputs may be any that keep to these rules, and one draw needn't show every extreme that they name: `obs_cell`: row-major cell within the entry's own longitude tile: row times 64 plus column. `obs_slot`: slot n < 3 observes the height after model step n + 1; slot 3 marks a padding entry that observes nothing.
All inputs are finite; a program needn't handle non-finite values.
Results may differ from a plain program's by a relative error of at most 0.0003.
Values sent between devices are 32-bit elements; how exact they have to be, the bound alone decides.
No kernel may reach another device: no remote copies, remote signals or barrier semaphores. Data moves between devices by JAX's collectives and lax.ppermute only.
A program may use at most 64 MiB of HBM per device.

v0:
```python
import jax
import jax.numpy as jnp
from jax import lax
from jax.sharding import Mesh
from jax.sharding import PartitionSpec as P

STEPS = 3
LON = ("lon_0", "lon_1", "lon_2")
ENS = ("ens_0", "ens_1")
ENS_LON = ("ens_0", "ens_1", "lon_0", "lon_1", "lon_2")


wave_speed = 0.35
rotation = 0.2


def extended(block, sides, width, periodic):
    for axis, dim in sides:
        count = lax.axis_size(axis)
        forward = [(i, i + 1) for i in range(count - 1)]
        if periodic:
            forward.append((count - 1, 0))
        backward = [(target, source) for source, target in forward]
        low = lax.ppermute(
            lax.slice_in_dim(block, block.shape[dim] - width, None, axis=dim), axis, forward
        )
        high = lax.ppermute(lax.slice_in_dim(block, 0, width, axis=dim), axis, backward)
        block = jnp.concatenate([low, block, high], axis=dim)
    return block


def cut_along(value, dim, devices):
    dims = value.shape
    pieces = value.reshape(*dims[:dim], devices, dims[dim] // devices, *dims[dim + 1 :])
    return jnp.moveaxis(pieces, dim, 0)


def sent_and_summed(value, axis, dim):
    devices = lax.axis_size(axis)
    pieces = lax.all_to_all(cut_along(value, dim, devices), axis, 0, 0, tiled=True)
    return jnp.sum(pieces, axis=0)


def copy_for_each(value, axis):
    devices = lax.axis_size(axis)
    return lax.all_to_all(
        jnp.broadcast_to(value[None], (devices, *value.shape)), axis, 0, 0, tiled=True
    )


def joined_along(pieces, dim):
    pieces = jnp.moveaxis(pieces, 0, dim)
    dims = pieces.shape
    return pieces.reshape(*dims[:dim], dims[dim] * dims[dim + 1], *dims[dim + 2 :])


def gathered_copies(value, axis, dim):
    pieces = copy_for_each(value, axis)
    return joined_along(pieces, dim)


def by_axis(value, axes):
    for axis in axes:
        value = lax.psum(value, axis)
    return value


def grid_factors(row_ids, lat_total):
    latitude = (-1.0 / 3.0 + 2.0 / 3.0 * (row_ids + 0.5) / lat_total) * jnp.pi
    return (1.0 / jnp.cos(latitude), jnp.sin(latitude))


def model_step(fields, orient, metric, coriolis):
    lon_wide = extended(fields, ((LON, 2),), 1, True)
    lat_wide = extended(fields, ((ENS, 1),), 1, False)
    lon_diff = 0.5 * metric[:, None] * (lon_wide[:, :, 2:] - lon_wide[:, :, :-2])
    lat_diff = 0.5 * (lat_wide[:, 2:] - lat_wide[:, :-2])
    height, zonal, meridional = (fields[0], fields[1], fields[2])
    speed = orient * wave_speed
    turning = orient * rotation * coriolis[:, None]
    return jnp.stack(
        [
            height - speed * (lon_diff[1] + lat_diff[2]),
            zonal - speed * lon_diff[0] + turning * meridional,
            meridional - speed * lat_diff[0] - turning * zonal,
        ]
    )


def body(control, residual, direction, ens_perturb, localize, obs_cell, obs_slot, obs_weight):
    hi = lax.Precision.HIGHEST
    lat_total = localize.shape[0]
    tile_cols = control.shape[2]
    localized = jnp.einsum("ij,mjc->mic", localize, direction, precision=hi)
    increment = jnp.sum(ens_perturb.astype(jnp.float32) * localized[:, None], axis=0)
    lat_slab = sent_and_summed(increment, ENS, 1)
    row_start = lax.axis_index(ENS) * lat_slab.shape[1]
    slab_rows = lat_slab.shape[1]
    cells = slab_rows * tile_cols
    row_ids = (row_start + jnp.arange(slab_rows, dtype=jnp.int32)).astype(jnp.float32)
    metric, coriolis = grid_factors(row_ids, lat_total)
    local_row = obs_cell // tile_cols - row_start
    inside = (local_row >= 0) & (local_row < slab_rows) & (obs_slot < STEPS)
    cell_index = jnp.clip(local_row, 0, slab_rows - 1) * tile_cols + obs_cell % tile_cols
    slot_index = obs_slot * cells + cell_index
    gather_index = jnp.clip(slot_index, 0, STEPS * cells - 1)
    tl_state = lat_slab
    heights = []
    for moment in range(STEPS):
        tl_state = model_step(tl_state, 1.0, metric, coriolis)
        heights.append(tl_state[0].reshape(-1))
    observed = jnp.concatenate(heights)[gather_index]
    weighted = jnp.where(inside, obs_weight * observed, 0.0)
    forcing = jnp.zeros(((STEPS + 1) * cells,), jnp.float32).at[slot_index].add(weighted)
    forcing = forcing.reshape(STEPS + 1, slab_rows, tile_cols)
    adjoint = jnp.zeros(lat_slab.shape, jnp.float32)
    for moment in reversed(range(STEPS)):
        adjoint = adjoint.at[0].add(forcing[moment])
        adjoint = model_step(adjoint, -1.0, metric, coriolis)
    adjoint = gathered_copies(adjoint, ENS, 1)
    projected = jnp.sum(ens_perturb.astype(jnp.float32) * adjoint[None], axis=1)
    pulled_back = jnp.einsum("ji,mjc->mic", localize, projected, precision=hi)
    image_vec = direction + pulled_back
    norm_old, curvature, cross_term, square = (
        by_axis(jnp.sum(residual * residual), ENS_LON),
        by_axis(jnp.sum(direction * image_vec), ENS_LON),
        by_axis(jnp.sum(residual * image_vec), ENS_LON),
        by_axis(jnp.sum(image_vec * image_vec), ENS_LON),
    )
    step_size = norm_old / curvature
    control_new = control + step_size * direction
    residual_new = residual - step_size * image_vec
    norm_new = norm_old - 2.0 * step_size * cross_term + step_size * step_size * square
    direction_new = residual_new + norm_new / norm_old * direction
    return (control_new, residual_new, direction_new)


def solution(mesh):
    split = Mesh(mesh.devices.reshape(2, 4, 8, 2, 2), ("ens_0", "ens_1", "lon_0", "lon_1", "lon_2"))
    placed = (
        P(ENS, None, LON),
        P(ENS, None, LON),
        P(ENS, None, LON),
        P(ENS, None, None, LON),
        P(),
        P(LON),
        P(LON),
        P(LON),
    )
    return jax.shard_map(
        body,
        mesh=split,
        in_specs=placed,
        out_specs=(P(ENS, None, LON), P(ENS, None, LON), P(ENS, None, LON)),
        check_vma=False,
    )
```

profile of v0, /device:TPU:1, one launch (start us, length us, event | category | flops | bytes accessed | tf_op | source)
XLA Modules:
  0.0 240.7 jit_solution(2650219843363851633)
XLA Ops:
  0.6 6.8 %fusion.6 = f32[2,1024,64]{1,2,0:T(8,128)S(1)} fusion(f32[2,1024,64]{1,2,0:T(8,128)} %param.16, f32[1024,1024]{1,0:T(8,128)} %param.18), kind=kOutput, calls=%fused_computation.10 | convolution fusion | flops 1610612736 | bytes 5242880 | tf_op jit(solution)/shard_map/ij,mjc->mic/dot_general | solution.py:94
  7.5 0.2 fusion.4
  7.7 1.0 bitcast_bitcast_fusion
  8.7 7.5 %all-to-all-start = ((f32[8,3,128,64]{2,3,1,0:T(8,128)}), f32[8,3,128,64]{2,3,1,0:T(8,128)S(1)}, u32[]{:S(2)}, u32[]{:S(2)}) async-start(f32[8,3,128,64]{2,3,1,0:T(8,128)} %bitcast_bitcast_fusion), calls=%async_computation | async-start | bytes 1572864 | tf_op jit(solution)/shard_map/all_to_all | solution.py:40
  16.2 14.6 %all-to-all-done = f32[8,3,128,64]{2,3,1,0:T(8,128)S(1)} async-done(((f32[8,3,128,64]{2,3,1,0:T(8,128)}), f32[8,3,128,64]{2,3,1,0:T(8,128)S(1)}, u32[]{:S(2)}, u32[]{:S(2)}) %all-to-all-start) | async-done | bytes 786464 | tf_op jit(solution)/shard_map/all_to_all | solution.py:40
  30.9 0.9 collective-permute-start
  31.7 1.0 collective-permute-start.1
  32.7 1.3 collective-permute-start.2
  34.0 4.0 %collective-permute-start.3 = (f32[3,1,64]{1,2,0:T(8,128)S(1)}, f32[3,1,64]{1,2,0:T(8,128)S(1)}, u32[]{:S(2)}, u32[]{:S(2)}) collective-permute-start(f32[3,1,64]{1,2,0:T(8,128)S(1)} %get-tuple-element.122), channel_id=1, source_target_pairs={{0,32},{32,64},{64,96},{96,128},{128,160},{160,192},{192,224},{1,3... | collective-permute-start | bytes 2312 | tf_op jit(solution)/shard_map/ppermute | solution.py:24
  38.0 1.6 collective-permute-done.3
  39.6 0.1 fusion.34
  39.8 5.6 %collective-permute-start.4 = (f32[3,128,1]{1,2,0:T(1,128)S(1)}, f32[3,128,1]{1,2,0:T(1,128)S(1)}, u32[]{:S(2)}, u32[]{:S(2)}) collective-permute-start(f32[3,128,1]{1,2,0:T(1,128)S(1)} %get-tuple-element.113), channel_id=1, source_target_pairs={{1,0},{2,1},{3,2},{4,3},{5,4},{6,5},{7,6},{8,7},{9,8},{10,9},{11,1... | collective-permute-start | bytes 4616 | tf_op jit(solution)/shard_map/ppermute | solution.py:27
  45.5 1.3 collective-permute-start.6
  46.8 4.7 %collective-permute-start.7 = (f32[3,1,64]{1,2,0:T(8,128)S(1)}, f32[3,1,64]{1,2,0:T(8,128)S(1)}, u32[]{:S(2)}, u32[]{:S(2)}) collective-permute-start(f32[3,1,64]{1,2,0:T(8,128)S(1)} %get-tuple-element.116), channel_id=1, source_target_pairs={{0,32},{32,64},{64,96},{96,128},{128,160},{160,192},{192,224},{1,3... | collective-permute-start | bytes 2312 | tf_op jit(solution)/shard_map/ppermute | solution.py:24
  51.5 0.3 collective-permute-done.6
  51.8 1.3 collective-permute-done.7
  53.3 3.4 %collective-permute-start.8 = (f32[3,128,1]{1,2,0:T(1,128)S(1)}, f32[3,128,1]{1,2,0:T(1,128)S(1)}, u32[]{:S(2)}, u32[]{:S(2)}) collective-permute-start(f32[3,128,1]{1,2,0:T(1,128)S(1)} %get-tuple-element.106), channel_id=1, source_target_pairs={{1,0},{2,1},{3,2},{4,3},{5,4},{6,5},{7,6},{8,7},{9,8},{10,9},{11,1... | collective-permute-start | bytes 4616 | tf_op jit(solution)/shard_map/ppermute | solution.py:27
  56.8 4.0 %collective-permute-start.11 = (f32[3,1,64]{1,2,0:T(8,128)S(1)}, f32[3,1,64]{1,2,0:T(8,128)S(1)}, u32[]{:S(2)}, u32[]{:S(2)}) collective-permute-start(f32[3,1,64]{1,2,0:T(8,128)S(1)} %get-tuple-element.107), channel_id=1, source_target_pairs={{0,32},{32,64},{64,96},{96,128},{128,160},{160,192},{192,224},{1,3... | collective-permute-start | bytes 2312 | tf_op jit(solution)/shard_map/ppermute | solution.py:24
  60.8 1.3 collective-permute-start.10
  62.5 4.0 %collective-permute-done.10 = f32[3,1,64]{1,2,0:T(8,128)S(1)} collective-permute-done((f32[3,1,64]{1,2,0:T(8,128)S(1)}, f32[3,1,64]{1,2,0:T(8,128)S(1)}, u32[]{:S(2)}, u32[]{:S(2)}) %collective-permute-start.10) | collective-permute-done | bytes 800 | tf_op jit(solution)/shard_map/ppermute | solution.py:27
  66.8 23.0 %gather_fusion = f32[4096]{0:T(1024)S(1)} fusion(f32[24576]{0:T(1024)S(1)} %pad_maximum_fusion.30, s32[4096]{0:T(1024)S(1)} %get-tuple-element.69), kind=kCustom, calls=%fused_computation | custom fusion | bytes 49152 | tf_op jit(solution)/shard_map/gather | solution.py:112
  89.9 21.9 %scatter_custom_fusion = f32[32768]{0:T(1024)S(1)} fusion(s32[4096]{0:T(1024)S(1)} %compare_select_fusion.1, f32[4096]{0:T(1024)S(1)} %multiply_select_fusion, f32[]{:T(128)} %constant.129.clone.1), kind=kCustom, calls=%fused_computation.80 | custom fusion | flops 4096 | bytes 131076 | tf_op jit(solution)/shard_map/scatter-add | solution.py:114
  112.1 5.1 %collective-permute-start.12 = (f32[3,128,1]{1,2,0:T(1,128)S(1)}, f32[3,128,1]{1,2,0:T(1,128)S(1)}, u32[]{:S(2)}, u32[]{:S(2)}) collective-permute-start(f32[3,128,1]{1,2,0:T(1,128)S(1)} %get-tuple-element.123), channel_id=1, source_target_pairs={{1,0},{2,1},{3,2},{4,3},{5,4},{6,5},{7,6},{8,7},{9,8},{10,9},{11,1... | collective-permute-start | bytes 4616 | tf_op jit(solution)/shard_map/ppermute | solution.py:27
  117.2 1.3 collective-permute-start.14
  118.5 6.7 %collective-permute-start.15 = (f32[3,1,64]{1,2,0:T(8,128)S(1)}, f32[3,1,64]{1,2,0:T(8,128)S(1)}, u32[]{:S(2)}, u32[]{:S(2)}) collective-permute-start(f32[3,1,64]{1,2,0:T(8,128)S(1)} %get-tuple-element.126), channel_id=1, source_target_pairs={{0,32},{32,64},{64,96},{96,128},{128,160},{160,192},{192,224},{1,3... | collective-permute-start | bytes 2312 | tf_op jit(solution)/shard_map/ppermute | solution.py:24
  125.4 0.5 collective-permute-done.14
  125.9 0.9 collective-permute-done.15
  126.8 0.1 fusion.26
  127.2 1.4 collective-permute-start.16
  128.6 0.4 collective-permute-start.17
  129.0 1.3 collective-permute-start.18
  130.3 8.3 %collective-permute-start.19 = (f32[3,1,64]{1,2,0:T(8,128)S(1)}, f32[3,1,64]{1,2,0:T(8,128)S(1)}, u32[]{:S(2)}, u32[]{:S(2)}) collective-permute-start(f32[3,1,64]{1,2,0:T(8,128)S(1)} %get-tuple-element.99), channel_id=1, source_target_pairs={{0,32},{32,64},{64,96},{96,128},{128,160},{160,192},{192,224},{1,3... | collective-permute-start | bytes 2312 | tf_op jit(solution)/shard_map/ppermute | solution.py:24
  138.8 1.4 collective-permute-done.19
  140.2 0.1 fusion.22
  140.4 3.1 %collective-permute-start.20 = (f32[3,128,1]{1,2,0:T(1,128)S(1)}, f32[3,128,1]{1,2,0:T(1,128)S(1)}, u32[]{:S(2)}, u32[]{:S(2)}) collective-permute-start(f32[3,128,1]{1,2,0:T(1,128)S(1)} %get-tuple-element.90), channel_id=1, source_target_pairs={{1,0},{2,1},{3,2},{4,3},{5,4},{6,5},{7,6},{8,7},{9,8},{10,9},{11,1... | collective-permute-start | bytes 4616 | tf_op jit(solution)/shard_map/ppermute | solution.py:27
  143.7 1.3 collective-permute-start.22
  145.0 7.9 %collective-permute-start.23 = (f32[3,1,64]{1,2,0:T(8,128)S(1)}, f32[3,1,64]{1,2,0:T(8,128)S(1)}, u32[]{:S(2)}, u32[]{:S(2)}) collective-permute-start(f32[3,1,64]{1,2,0:T(8,128)S(1)} %get-tuple-element.93), channel_id=1, source_target_pairs={{0,32},{32,64},{64,96},{96,128},{128,160},{160,192},{192,224},{1,3... | collective-permute-start | bytes 2312 | tf_op jit(solution)/shard_map/ppermute | solution.py:24
  152.9 1.6 collective-permute-done.23
  154.5 0.1 fusion.18
  154.8 30.9 %all_to_all.10 = f32[8,3,128,64]{2,3,1,0:T(8,128)S(1)} all-to-all(f32[8,3,128,64]{2,3,1,0:T(8,128)S(1)} %broadcast_in_dim.16), channel_id=1, replica_groups=mesh['ens_0'=2,'ens_1'=4,'lon_0'=8,'lon_1'=2,'lon_2'=2] {'ens_0','ens_1'}, dimensions={0} | all-to-all | bytes 1572864 | tf_op jit(solution)/shard_map/all_to_all | solution.py:46
  185.7 0.2 fusion.5
  186.0 3.2 %multiply_reduce_fusion = (f32[]{:T(128)}, f32[]{:T(128)}, f32[]{:T(128)}, f32[]{:T(128)}, f32[2,1024,64]{1,2,0:T(8,128)S(1)}) fusion(f32[2,1024,64]{1,2,0:T(8,128)S(1)} %copy-done.3, f32[2,1024,64]{1,2,0:T(8,128)S(1)} %copy-done.1, f32[2,1024,64]{1,2,0:T(8,128)S(1)} %fusion.5, f32[1024,1024]{1,0:T(8,128)S(1)} %copy-done), kind=kOutput, calls=%fused_computation.16 | convolution fusion | flops 1611792384 | bytes 6291472 | tf_op jit(solution)/shard_map/ji,mjc->mic/dot_general | solution.py:122
  189.1 5.9 %all-reduce.5 = (f32[]{:T(128)}, f32[]{:T(128)}, f32[]{:T(128)}, f32[]{:T(128)}) all-reduce(f32[]{:T(128)} %get-tuple-element.41, f32[]{:T(128)} %get-tuple-element.42, f32[]{:T(128)} %get-tuple-element.40, f32[]{:T(128)} %get-tuple-element.39), channel_id=1, replica_groups=mesh['ens_0'=2,'ens_1'=4,'lon_0'=8,'lon_1'=2,'lon_2'=2] {'ens_0'}, use_global_device_ids=true, to_apply=%region_1.0 | all-reduce | flops 4 | bytes 32 | tf_op jit(solution)/shard_map/psum | solution.py:64
  195.1 7.6 %all-reduce.2 = (f32[]{:T(128)}, f32[]{:T(128)}, f32[]{:T(128)}, f32[]{:T(128)}) all-reduce(f32[]{:T(128)} %get-tuple-element.59, f32[]{:T(128)} %get-tuple-element.60, f32[]{:T(128)} %get-tuple-element.61, f32[]{:T(128)} %get-tuple-element.62), channel_id=1, replica_groups=mesh['ens_0'=2,'ens_1'=4,'lon_0'=8,'lon_1'=2,'lon_2'=2] {'ens_1'}, use_global_device_ids=true, to_apply=%region_2.3 | all-reduce | flops 4 | bytes 32 | tf_op jit(solution)/shard_map/psum | solution.py:64
  202.7 15.4 %all-reduce.1 = (f32[]{:T(128)}, f32[]{:T(128)}, f32[]{:T(128)}, f32[]{:T(128)}) all-reduce(f32[]{:T(128)} %get-tuple-element.47, f32[]{:T(128)} %get-tuple-element.48, f32[]{:T(128)} %get-tuple-element.49, f32[]{:T(128)} %get-tuple-element.50), channel_id=1, replica_groups=mesh['ens_0'=2,'ens_1'=4,'lon_0'=8,'lon_1'=2,'lon_2'=2] {'lon_0'}, use_global_device_ids=true, to_apply=%region_3.4 | all-reduce | flops 4 | bytes 32 | tf_op jit(solution)/shard_map/psum | solution.py:64
  218.1 7.4 %all-reduce.4 = (f32[]{:T(128)}, f32[]{:T(128)}, f32[]{:T(128)}, f32[]{:T(128)}) all-reduce(f32[]{:T(128)} %get-tuple-element.43, f32[]{:T(128)} %get-tuple-element.44, f32[]{:T(128)} %get-tuple-element.45, f32[]{:T(128)} %get-tuple-element.46), channel_id=1, replica_groups=mesh['ens_0'=2,'ens_1'=4,'lon_0'=8,'lon_1'=2,'lon_2'=2] {'lon_1'}, use_global_device_ids=true, to_apply=%region_4.5 | all-reduce | flops 4 | bytes 32 | tf_op jit(solution)/shard_map/psum | solution.py:64
  225.5 10.0 %all-reduce.3 = (f32[]{:T(128)}, f32[]{:T(128)}, f32[]{:T(128)}, f32[]{:T(128)}) all-reduce(f32[]{:T(128)} %get-tuple-element.55, f32[]{:T(128)} %get-tuple-element.56, f32[]{:T(128)} %get-tuple-element.57, f32[]{:T(128)} %get-tuple-element.58), channel_id=1, replica_groups=mesh['ens_0'=2,'ens_1'=4,'lon_0'=8,'lon_1'=2,'lon_2'=2] {'lon_2'}, use_global_device_ids=true, to_apply=%region_5.6 | all-reduce | flops 4 | bytes 32 | tf_op jit(solution)/shard_map/psum | solution.py:64
  239.4 1.3 multiply_add_fusion
  (87 shorter events, 2.6 us)
Async XLA Ops:
  0.6 6.8 %copy-start.2 = (bf16[2,3,1024,64]{2,3,1,0:T(8,128)(2,1)S(1)}, bf16[2,3,1024,64]{2,3,1,0:T(8,128)(2,1)}, u32[]{:S(2)}) copy-start(bf16[2,3,1024,64]{2,3,1,0:T(8,128)(2,1)} %param.17) | copy-start | bytes 2359300
  7.5 44.0 %copy-start.5 = (s32[4096]{0:T(1024)S(1)}, s32[4096]{0:T(1024)}, u32[]{:S(2)}) copy-start(s32[4096]{0:T(1024)} %param.19) | copy-start | bytes 49156
  7.5 44.0 %copy-start.6 = (s32[4096]{0:T(1024)S(1)}, s32[4096]{0:T(1024)}, u32[]{:S(2)}) copy-start(s32[4096]{0:T(1024)} %param.20) | copy-start | bytes 49156
  8.7 22.0 %all-to-all-start = ((f32[8,3,128,64]{2,3,1,0:T(8,128)}), f32[8,3,128,64]{2,3,1,0:T(8,128)S(1)}, u32[]{:S(2)}, u32[]{:S(2)}) async-start(f32[8,3,128,64]{2,3,1,0:T(8,128)} %bitcast_bitcast_fusion), calls=%async_computation | async-start | bytes 1572864 | tf_op jit(solution)/shard_map/all_to_all | solution.py:40
  30.9 8.7 %collective-permute-start = (f32[3,128,1]{1,2,0:T(1,128)S(1)}, f32[3,128,1]{1,2,0:T(1,128)S(1)}, u32[]{:S(2)}, u32[]{:S(2)}) collective-permute-start(f32[3,128,1]{1,2,0:T(1,128)S(1)} %get-tuple-element.119), channel_id=1, source_target_pairs={{1,0},{2,1},{3,2},{4,3},{5,4},{6,5},{7,6},{8,7},{9,8},{10,9},{11,1... | collective-permute-start | bytes 4616 | tf_op jit(solution)/shard_map/ppermute | solution.py:27
  31.7 7.9 %collective-permute-start.1 = (f32[3,128,1]{1,2,0:T(1,128)S(1)}, f32[3,128,1]{1,2,0:T(1,128)S(1)}, u32[]{:S(2)}, u32[]{:S(2)}) collective-permute-start(f32[3,128,1]{1,2,0:T(1,128)S(1)} %get-tuple-element.120), channel_id=1, source_target_pairs={{0,1},{1,2},{2,3},{3,4},{4,5},{5,6},{6,7},{7,8},{8,9},{9,10},{10,1... | collective-permute-start | bytes 4616 | tf_op jit(solution)/shard_map/ppermute | solution.py:24
  32.7 5.3 %collective-permute-start.2 = (f32[3,1,64]{1,2,0:T(8,128)S(1)}, f32[3,1,64]{1,2,0:T(8,128)S(1)}, u32[]{:S(2)}, u32[]{:S(2)}) collective-permute-start(f32[3,1,64]{1,2,0:T(8,128)S(1)} %get-tuple-element.121), channel_id=1, source_target_pairs={{32,0},{64,32},{96,64},{128,96},{160,128},{192,160},{224,192},{33,... | collective-permute-start | bytes 2312 | tf_op jit(solution)/shard_map/ppermute | solution.py:27
  34.0 5.6 %collective-permute-start.3 = (f32[3,1,64]{1,2,0:T(8,128)S(1)}, f32[3,1,64]{1,2,0:T(8,128)S(1)}, u32[]{:S(2)}, u32[]{:S(2)}) collective-permute-start(f32[3,1,64]{1,2,0:T(8,128)S(1)} %get-tuple-element.122), channel_id=1, source_target_pairs={{0,32},{32,64},{64,96},{96,128},{128,160},{160,192},{192,224},{1,3... | collective-permute-start | bytes 2312 | tf_op jit(solution)/shard_map/ppermute | solution.py:24
  39.8 13.2 %collective-permute-start.4 = (f32[3,128,1]{1,2,0:T(1,128)S(1)}, f32[3,128,1]{1,2,0:T(1,128)S(1)}, u32[]{:S(2)}, u32[]{:S(2)}) collective-permute-start(f32[3,128,1]{1,2,0:T(1,128)S(1)} %get-tuple-element.113), channel_id=1, source_target_pairs={{1,0},{2,1},{3,2},{4,3},{5,4},{6,5},{7,6},{8,7},{9,8},{10,9},{11,1... | collective-permute-start | bytes 4616 | tf_op jit(solution)/shard_map/ppermute | solution.py:27
  45.4 7.7 %collective-permute-start.5 = (f32[3,128,1]{1,2,0:T(1,128)S(1)}, f32[3,128,1]{1,2,0:T(1,128)S(1)}, u32[]{:S(2)}, u32[]{:S(2)}) collective-permute-start(f32[3,128,1]{1,2,0:T(1,128)S(1)} %get-tuple-element.114), channel_id=1, source_target_pairs={{0,1},{1,2},{2,3},{3,4},{4,5},{5,6},{6,7},{7,8},{8,9},{9,10},{10,1... | collective-permute-start | bytes 4616 | tf_op jit(solution)/shard_map/ppermute | solution.py:24
  45.5 6.3 %collective-permute-start.6 = (f32[3,1,64]{1,2,0:T(8,128)S(1)}, f32[3,1,64]{1,2,0:T(8,128)S(1)}, u32[]{:S(2)}, u32[]{:S(2)}) collective-permute-start(f32[3,1,64]{1,2,0:T(8,128)S(1)} %get-tuple-element.115), channel_id=1, source_target_pairs={{32,0},{64,32},{96,64},{128,96},{160,128},{192,160},{224,192},{33,... | collective-permute-start | bytes 2312 | tf_op jit(solution)/shard_map/ppermute | solution.py:27
  46.8 6.3 %collective-permute-start.7 = (f32[3,1,64]{1,2,0:T(8,128)S(1)}, f32[3,1,64]{1,2,0:T(8,128)S(1)}, u32[]{:S(2)}, u32[]{:S(2)}) collective-permute-start(f32[3,1,64]{1,2,0:T(8,128)S(1)} %get-tuple-element.116), channel_id=1, source_target_pairs={{0,32},{32,64},{64,96},{96,128},{128,160},{160,192},{192,224},{1,3... | collective-permute-start | bytes 2312 | tf_op jit(solution)/shard_map/ppermute | solution.py:24
  53.3 13.2 %collective-permute-start.9 = (f32[3,128,1]{1,2,0:T(1,128)S(1)}, f32[3,128,1]{1,2,0:T(1,128)S(1)}, u32[]{:S(2)}, u32[]{:S(2)}) collective-permute-start(f32[3,128,1]{1,2,0:T(1,128)S(1)} %get-tuple-element.105), channel_id=1, source_target_pairs={{0,1},{1,2},{2,3},{3,4},{4,5},{5,6},{6,7},{7,8},{8,9},{9,10},{10,1... | collective-permute-start | bytes 4616 | tf_op jit(solution)/shard_map/ppermute | solution.py:24
  53.3 13.1 %collective-permute-start.8 = (f32[3,128,1]{1,2,0:T(1,128)S(1)}, f32[3,128,1]{1,2,0:T(1,128)S(1)}, u32[]{:S(2)}, u32[]{:S(2)}) collective-permute-start(f32[3,128,1]{1,2,0:T(1,128)S(1)} %get-tuple-element.106), channel_id=1, source_target_pairs={{1,0},{2,1},{3,2},{4,3},{5,4},{6,5},{7,6},{8,7},{9,8},{10,9},{11,1... | collective-permute-start | bytes 4616 | tf_op jit(solution)/shard_map/ppermute | solution.py:27
  56.8 5.7 %collective-permute-start.11 = (f32[3,1,64]{1,2,0:T(8,128)S(1)}, f32[3,1,64]{1,2,0:T(8,128)S(1)}, u32[]{:S(2)}, u32[]{:S(2)}) collective-permute-start(f32[3,1,64]{1,2,0:T(8,128)S(1)} %get-tuple-element.107), channel_id=1, source_target_pairs={{0,32},{32,64},{64,96},{96,128},{128,160},{160,192},{192,224},{1,3... | collective-permute-start | bytes 2312 | tf_op jit(solution)/shard_map/ppermute | solution.py:24
  60.8 5.6 %collective-permute-start.10 = (f32[3,1,64]{1,2,0:T(8,128)S(1)}, f32[3,1,64]{1,2,0:T(8,128)S(1)}, u32[]{:S(2)}, u32[]{:S(2)}) collective-permute-start(f32[3,1,64]{1,2,0:T(8,128)S(1)} %get-tuple-element.108), channel_id=1, source_target_pairs={{32,0},{64,32},{96,64},{128,96},{160,128},{192,160},{224,192},{33,... | collective-permute-start | bytes 2312 | tf_op jit(solution)/shard_map/ppermute | solution.py:27
  66.8 23.1 %copy-start.7 = (f32[4096]{0:T(1024)S(1)}, f32[4096]{0:T(1024)}, u32[]{:S(2)}) copy-start(f32[4096]{0:T(1024)} %param.21) | copy-start | bytes 49156
  112.1 14.8 %collective-permute-start.12 = (f32[3,128,1]{1,2,0:T(1,128)S(1)}, f32[3,128,1]{1,2,0:T(1,128)S(1)}, u32[]{:S(2)}, u32[]{:S(2)}) collective-permute-start(f32[3,128,1]{1,2,0:T(1,128)S(1)} %get-tuple-element.123), channel_id=1, source_target_pairs={{1,0},{2,1},{3,2},{4,3},{5,4},{6,5},{7,6},{8,7},{9,8},{10,9},{11,1... | collective-permute-start | bytes 4616 | tf_op jit(solution)/shard_map/ppermute | solution.py:27
  117.2 9.6 %collective-permute-start.13 = (f32[3,128,1]{1,2,0:T(1,128)S(1)}, f32[3,128,1]{1,2,0:T(1,128)S(1)}, u32[]{:S(2)}, u32[]{:S(2)}) collective-permute-start(f32[3,128,1]{1,2,0:T(1,128)S(1)} %get-tuple-element.124), channel_id=1, source_target_pairs={{0,1},{1,2},{2,3},{3,4},{4,5},{5,6},{6,7},{7,8},{8,9},{9,10},{10,1... | collective-permute-start | bytes 4616 | tf_op jit(solution)/shard_map/ppermute | solution.py:24
  117.2 8.7 %collective-permute-start.14 = (f32[3,1,64]{1,2,0:T(8,128)S(1)}, f32[3,1,64]{1,2,0:T(8,128)S(1)}, u32[]{:S(2)}, u32[]{:S(2)}) collective-permute-start(f32[3,1,64]{1,2,0:T(8,128)S(1)} %get-tuple-element.125), channel_id=1, source_target_pairs={{32,0},{64,32},{96,64},{128,96},{160,128},{192,160},{224,192},{33,... | collective-permute-start | bytes 2312 | tf_op jit(solution)/shard_map/ppermute | solution.py:27
  118.5 8.3 %collective-permute-start.15 = (f32[3,1,64]{1,2,0:T(8,128)S(1)}, f32[3,1,64]{1,2,0:T(8,128)S(1)}, u32[]{:S(2)}, u32[]{:S(2)}) collective-permute-start(f32[3,1,64]{1,2,0:T(8,128)S(1)} %get-tuple-element.126), channel_id=1, source_target_pairs={{0,32},{32,64},{64,96},{96,128},{128,160},{160,192},{192,224},{1,3... | collective-permute-start | bytes 2312 | tf_op jit(solution)/shard_map/ppermute | solution.py:24
  127.2 13.0 %collective-permute-start.16 = (f32[3,128,1]{1,2,0:T(1,128)S(1)}, f32[3,128,1]{1,2,0:T(1,128)S(1)}, u32[]{:S(2)}, u32[]{:S(2)}) collective-permute-start(f32[3,128,1]{1,2,0:T(1,128)S(1)} %get-tuple-element.96), channel_id=1, source_target_pairs={{1,0},{2,1},{3,2},{4,3},{5,4},{6,5},{7,6},{8,7},{9,8},{10,9},{11,1... | collective-permute-start | bytes 4616 | tf_op jit(solution)/shard_map/ppermute | solution.py:27
  128.6 11.6 %collective-permute-start.17 = (f32[3,128,1]{1,2,0:T(1,128)S(1)}, f32[3,128,1]{1,2,0:T(1,128)S(1)}, u32[]{:S(2)}, u32[]{:S(2)}) collective-permute-start(f32[3,128,1]{1,2,0:T(1,128)S(1)} %get-tuple-element.97), channel_id=1, source_target_pairs={{0,1},{1,2},{2,3},{3,4},{4,5},{5,6},{6,7},{7,8},{8,9},{9,10},{10,1... | collective-permute-start | bytes 4616 | tf_op jit(solution)/shard_map/ppermute | solution.py:24
  129.0 9.8 %collective-permute-start.18 = (f32[3,1,64]{1,2,0:T(8,128)S(1)}, f32[3,1,64]{1,2,0:T(8,128)S(1)}, u32[]{:S(2)}, u32[]{:S(2)}) collective-permute-start(f32[3,1,64]{1,2,0:T(8,128)S(1)} %get-tuple-element.98), channel_id=1, source_target_pairs={{32,0},{64,32},{96,64},{128,96},{160,128},{192,160},{224,192},{33,... | collective-permute-start | bytes 2312 | tf_op jit(solution)/shard_map/ppermute | solution.py:27
  130.3 9.9 %collective-permute-start.19 = (f32[3,1,64]{1,2,0:T(8,128)S(1)}, f32[3,1,64]{1,2,0:T(8,128)S(1)}, u32[]{:S(2)}, u32[]{:S(2)}) collective-permute-start(f32[3,1,64]{1,2,0:T(8,128)S(1)} %get-tuple-element.99), channel_id=1, source_target_pairs={{0,32},{32,64},{64,96},{96,128},{128,160},{160,192},{192,224},{1,3... | collective-permute-start | bytes 2312 | tf_op jit(solution)/shard_map/ppermute | solution.py:24
  140.3 45.6 %copy-start = (f32[1024,1024]{1,0:T(8,128)S(1)}, f32[1024,1024]{1,0:T(8,128)}, u32[]{:S(2)}) copy-start(f32[1024,1024]{1,0:T(8,128)} %param.18) | copy-start | bytes 12582916
  140.3 45.6 %copy-start.1 = (f32[2,1024,64]{1,2,0:T(8,128)S(1)}, f32[2,1024,64]{1,2,0:T(8,128)}, u32[]{:S(2)}) copy-start(f32[2,1024,64]{1,2,0:T(8,128)} %param.16) | copy-start | bytes 1572868
  140.4 45.6 %copy-start.3 = (f32[2,1024,64]{1,2,0:T(8,128)S(1)}, f32[2,1024,64]{1,2,0:T(8,128)}, u32[]{:S(2)}) copy-start(f32[2,1024,64]{1,2,0:T(8,128)} %param.15) | copy-start | bytes 1572868
  140.4 14.0 %collective-permute-start.20 = (f32[3,128,1]{1,2,0:T(1,128)S(1)}, f32[3,128,1]{1,2,0:T(1,128)S(1)}, u32[]{:S(2)}, u32[]{:S(2)}) collective-permute-start(f32[3,128,1]{1,2,0:T(1,128)S(1)} %get-tuple-element.90), channel_id=1, source_target_pairs={{1,0},{2,1},{3,2},{4,3},{5,4},{6,5},{7,6},{8,7},{9,8},{10,9},{11,1... | collective-permute-start | bytes 4616 | tf_op jit(solution)/shard_map/ppermute | solution.py:27
  143.6 10.9 %collective-permute-start.21 = (f32[3,128,1]{1,2,0:T(1,128)S(1)}, f32[3,128,1]{1,2,0:T(1,128)S(1)}, u32[]{:S(2)}, u32[]{:S(2)}) collective-permute-start(f32[3,128,1]{1,2,0:T(1,128)S(1)} %get-tuple-element.91), channel_id=1, source_target_pairs={{0,1},{1,2},{2,3},{3,4},{4,5},{5,6},{6,7},{7,8},{8,9},{9,10},{10,1... | collective-permute-start | bytes 4616 | tf_op jit(solution)/shard_map/ppermute | solution.py:24
  143.7 9.3 %collective-permute-start.22 = (f32[3,1,64]{1,2,0:T(8,128)S(1)}, f32[3,1,64]{1,2,0:T(8,128)S(1)}, u32[]{:S(2)}, u32[]{:S(2)}) collective-permute-start(f32[3,1,64]{1,2,0:T(8,128)S(1)} %get-tuple-element.92), channel_id=1, source_target_pairs={{32,0},{64,32},{96,64},{128,96},{160,128},{192,160},{224,192},{33,... | collective-permute-start | bytes 2312 | tf_op jit(solution)/shard_map/ppermute | solution.py:27
  145.0 9.5 %collective-permute-start.23 = (f32[3,1,64]{1,2,0:T(8,128)S(1)}, f32[3,1,64]{1,2,0:T(8,128)S(1)}, u32[]{:S(2)}, u32[]{:S(2)}) collective-permute-start(f32[3,1,64]{1,2,0:T(8,128)S(1)} %get-tuple-element.93), channel_id=1, source_target_pairs={{0,32},{32,64},{64,96},{96,128},{128,160},{160,192},{192,224},{1,3... | collective-permute-start | bytes 2312 | tf_op jit(solution)/shard_map/ppermute | solution.py:24
  185.7 53.7 %copy-start.4 = (f32[2,1024,64]{1,2,0:T(8,128)S(1)}, f32[2,1024,64]{1,2,0:T(8,128)}, u32[]{:S(2)}) copy-start(f32[2,1024,64]{1,2,0:T(8,128)} %param.14) | copy-start | bytes 1572868
where the time goes:
time: 241 us
  blocking collectives  77.2 us (32%)
  starting transfers between devices  71.6 us (30%)
  waiting for transfers between devices  26.1 us (11%)
  local copies, waits for them, and re-layouts  25.7 us (11%)
  other arithmetic  24.9 us (10%)
  matrix products  9.98 us (4%)
  between operations  5.13 us (2%)
    psum x5, blocking collectives, by_axis(): value = lax.psum(value, axis)  46.4 us
    ppermute x12, starting transfers between devices, extended(): lax.ppermute(lax.slice_in_dim(block, block.shape[dim] - width, None, axis...  37 us
    all_to_all x1, blocking collectives, copy_for_each(): lax.all_to_all(jnp.broadcast_to(value[None], (devices, *value.shape)), ax...  30.9 us
    ppermute x12, starting transfers between devices, extended(): lax.ppermute(lax.slice_in_dim(block, 0, width, axis=dim), axis, backward)  27.2 us
    gather x1, local copies, waits for them, and re-layouts, body(): observed = jnp.concatenate(heights)[gather_index]  23 us
    scatter-add x1, other arithmetic, body(): jnp.zeros(((STEPS + 1) * cells,), jnp.float32).at[slot_index].add(weighted)  21.9 us
    all_to_all x1, waiting for transfers between devices, sent_and_summed(): lax.all_to_all(cut_along(value, dim, devices), axis, 0, 0, tiled=True)  14.6 us
    all_to_all x1, starting transfers between devices, sent_and_summed(): lax.all_to_all(cut_along(value, dim, devices), axis, 0, 0, tiled=True)  7.47 us
  transfers between devices with their start and end apart: 25, of which 10 were waited for; matrix products, arithmetic and copies ran while one was open for 0% of the time, Pallas kernels for 0%

commit v1 on v0

v1 whole, which is shorter than its diff:
```python
import functools

import jax
import jax.numpy as jnp
import numpy as np
from jax import lax
from jax.experimental import pallas as pl
from jax.experimental.pallas import tpu as pltpu
from jax.sharding import Mesh
from jax.sharding import PartitionSpec as P

STEPS = 3
HALO = 3
PAD = 8
LON = ("lon_0", "lon_1", "lon_2")
ENS = ("ens_0", "ens_1")
ENS_LON = ("ens_0", "ens_1", "lon_0", "lon_1", "lon_2")

wave_speed = 0.35
rotation = 0.2

F32 = jnp.float32
BF16 = jnp.bfloat16
NT = (((1,), (1,)), ((), ()))
NN = (((1,), (0,)), ((), ()))


def split_two(x):
    high = x.astype(BF16)
    low = (x - high.astype(F32)).astype(BF16)
    return high, low


def dot(a, b, dims):
    return lax.dot_general(a, b, dims, preferred_element_type=F32)


def grid_factors(lat_total):
    row_ids = np.arange(lat_total).astype(np.float32)
    latitude = (-1.0 / 3.0 + 2.0 / 3.0 * (row_ids + 0.5) / lat_total) * np.pi
    return np.stack([1.0 / np.cos(latitude), np.sin(latitude)]).astype(np.float32)


def model_step(h, u, v, orient, metric, coriolis):
    wide, rows = h.shape
    lane = lax.broadcasted_iota(jnp.int32, (1, rows), 1)
    lon_scale = (orient * wave_speed * 0.5) * metric
    lat_scale = orient * wave_speed * 0.5
    turn = (orient * rotation) * coriolis
    keep_next = jnp.where(lane == rows - 1, 0.0, lat_scale)
    keep_last = jnp.where(lane == 0, 0.0, lat_scale)

    def lon_diff(x):
        return lon_scale * (pltpu.roll(x, wide - 1, 0) - pltpu.roll(x, 1, 0))

    def lat_diff(x):
        return keep_next * pltpu.roll(x, rows - 1, 1) - keep_last * pltpu.roll(x, 1, 1)

    return (
        h - (lon_diff(u) + lat_diff(v)),
        u - lon_diff(h) + turn * v,
        v - lat_diff(h) - turn * u,
    )


def increment_kernel(loc_ref, dir_ref, pert_ref, inc_ref, left_ref, right_ref, parts_ref):
    members, cols, rows = dir_ref.shape
    lines = members * cols

    @pl.when(pl.program_id(0) == 0)
    def _():
        high, low = split_two(dir_ref[...].reshape(lines, rows))
        parts_ref[0:lines] = high
        parts_ref[lines : 2 * lines] = low

    loc_high, loc_low = split_two(loc_ref[...])
    both = dot(parts_ref[...], loc_high, NT)
    rest = dot(parts_ref[0:lines], loc_low, NT)
    localized = both[0:lines] + both[lines : 2 * lines] + rest
    for field in range(3):
        total = None
        for m in range(members):
            term = pert_ref[m, field].astype(F32) * localized[m * cols : (m + 1) * cols]
            total = term if total is None else total + term
        inc_ref[field] = total
        left_ref[HALO * field : HALO * (field + 1)] = total[0:HALO]
        right_ref[HALO * field : HALO * (field + 1)] = total[cols - HALO : cols]


def partial_increment(localize, direction, pert):
    members, cols, rows = direction.shape
    block = 256
    edge = jax.ShapeDtypeStruct((3 * HALO, rows), F32)
    edge_spec = pl.BlockSpec((3 * HALO, block), lambda i: (0, i))
    return pl.pallas_call(
        increment_kernel,
        grid=(rows // block,),
        in_specs=[
            pl.BlockSpec((block, rows), lambda i: (i, 0)),
            pl.BlockSpec((members, cols, rows), lambda i: (0, 0, 0)),
            pl.BlockSpec((members, 3, cols, block), lambda i: (0, 0, 0, i)),
        ],
        out_specs=[pl.BlockSpec((3, cols, block), lambda i: (0, 0, i)), edge_spec, edge_spec],
        out_shape=[jax.ShapeDtypeStruct((3, cols, rows), F32), edge, edge],
        scratch_shapes=[pltpu.VMEM((2 * members * cols, rows), BF16)],
        name="increment",
    )(localize, direction, pert)


def forward_kernel(
    inc_ref, west_ref, east_ref, factor_ref, row_ref, spot_ref, out_ref, state_ref, parts_ref
):
    _, cols, rows = inc_ref.shape
    nobs = row_ref.shape[1]
    wide = cols + 2 * PAD
    state_ref[...] = jnp.zeros(state_ref.shape, F32)
    for field in range(3):
        lines = slice(HALO * field, HALO * (field + 1))
        state_ref[field, PAD : PAD + cols] = inc_ref[field]
        state_ref[field, PAD - HALO : PAD] = west_ref[lines]
        state_ref[field, PAD + cols : PAD + cols + HALO] = east_ref[lines]
    metric = factor_ref[0:1]
    coriolis = factor_ref[1:2]
    spots = STEPS * cols
    for moment in range(STEPS):
        h, u, v = model_step(state_ref[0], state_ref[1], state_ref[2], 1.0, metric, coriolis)
        state_ref[0] = h
        state_ref[1] = u
        state_ref[2] = v
        high, low = split_two(h[PAD : PAD + cols])
        parts_ref[moment * cols : (moment + 1) * cols] = high
        parts_ref[spots + moment * cols : spots + (moment + 1) * cols] = low
    chunk = 512
    for start in range(0, nobs, chunk):
        here = slice(start, start + chunk)
        row_hot = lax.broadcasted_iota(jnp.int32, (rows, chunk), 0) == row_ref[:, here]
        picked = dot(parts_ref[...], row_hot.astype(F32).astype(BF16), NN)
        picked = picked[0:spots] + picked[spots : 2 * spots]
        spot_hot = lax.broadcasted_iota(jnp.int32, (spots, chunk), 0) == spot_ref[:, here]
        value = jnp.sum(jnp.where(spot_hot, picked, 0.0), axis=0, keepdims=True)
        out_ref[:, here] = jnp.broadcast_to(value, (out_ref.shape[0], chunk))


def observed_parts(inc, west, east, factors, obs_row, obs_spot, copies):
    _, cols, rows = inc.shape
    nobs = obs_row.shape[1]
    return pl.pallas_call(
        forward_kernel,
        out_shape=jax.ShapeDtypeStruct((copies, nobs), F32),
        scratch_shapes=[
            pltpu.VMEM((3, cols + 2 * PAD, rows), F32),
            pltpu.VMEM((2 * STEPS * cols, rows), BF16),
        ],
        name="forward",
    )(inc, west, east, factors, obs_row, obs_spot)


def adjoint_kernel(
    seen_ref, weight_ref, row_ref, spot_ref, factor_ref, adj_ref, left_ref, right_ref,
    state_ref, force_ref,
):
    _, cols, rows = adj_ref.shape
    nobs = row_ref.shape[1]
    spots = STEPS * cols
    chunk = 512
    for start in range(0, nobs, chunk):
        here = slice(start, start + chunk)
        weighted = weight_ref[:, here] * jnp.sum(seen_ref[:, here], axis=0, keepdims=True)
        spot_hot = lax.broadcasted_iota(jnp.int32, (spots, chunk), 0) == spot_ref[:, here]
        high, low = split_two(jnp.where(spot_hot, weighted, 0.0))
        row_hot = lax.broadcasted_iota(jnp.int32, (rows, chunk), 0) == row_ref[:, here]
        part = dot(
            jnp.concatenate([high, low], axis=0), row_hot.astype(F32).astype(BF16), NT
        )
        part = part[0:spots] + part[spots : 2 * spots]
        if start == 0:
            force_ref[...] = part
        else:
            force_ref[...] += part
    metric = factor_ref[0:1]
    coriolis = factor_ref[1:2]
    state_ref[...] = jnp.zeros(state_ref.shape, F32)
    for moment in reversed(range(STEPS)):
        state_ref[0, PAD : PAD + cols] += force_ref[moment * cols : (moment + 1) * cols]
        h, u, v = model_step(state_ref[0], state_ref[1], state_ref[2], -1.0, metric, coriolis)
        state_ref[0] = h
        state_ref[1] = u
        state_ref[2] = v
    for field in range(3):
        lines = slice(HALO * field, HALO * (field + 1))
        adj_ref[field] = state_ref[field, PAD : PAD + cols]
        left_ref[lines] = state_ref[field, PAD - HALO : PAD]
        right_ref[lines] = state_ref[field, PAD + cols : PAD + cols + HALO]


def tile_adjoint(seen, weight, obs_row, obs_spot, factors, cols):
    rows = factors.shape[1]
    edge = jax.ShapeDtypeStruct((3 * HALO, rows), F32)
    return pl.pallas_call(
        adjoint_kernel,
        out_shape=[jax.ShapeDtypeStruct((3, cols, rows), F32), edge, edge],
        scratch_shapes=[
            pltpu.VMEM((3, cols + 2 * PAD, rows), F32),
            pltpu.VMEM((STEPS * cols, rows), F32),
        ],
        name="adjoint",
    )(seen, weight, obs_row, obs_spot, factors)


def image_kernel(
    loc_ref, adj_ref, west_ref, east_ref, pert_ref, dir_ref, res_ref, img_ref, sums_ref,
    parts_ref, total_ref,
):
    members, cols, rows = pert_ref.shape[0], pert_ref.shape[2], pert_ref.shape[3]
    block = loc_ref.shape[1]
    lines = members * cols
    step = pl.program_id(0)

    @pl.when(step == 0)
    def _():
        total_ref[...] = jnp.zeros(total_ref.shape, F32)
        adj = []
        for field in range(3):
            edges = slice(HALO * field, HALO * (field + 1))
            middle = jnp.zeros((cols - 2 * HALO, rows), F32)
            extra = jnp.concatenate([west_ref[edges], middle, east_ref[edges]], axis=0)
            adj.append(adj_ref[field] + extra)
        for m in range(members):
            projected = pert_ref[m, 0].astype(F32) * adj[0]
            projected += pert_ref[m, 1].astype(F32) * adj[1]
            projected += pert_ref[m, 2].astype(F32) * adj[2]
            high, low = split_two(projected)
            parts_ref[m * cols : (m + 1) * cols] = high
            parts_ref[lines + m * cols : lines + (m + 1) * cols] = low

    loc_high, loc_low = split_two(loc_ref[...])
    both = dot(parts_ref[...], loc_high, NN)
    rest = dot(parts_ref[0:lines], loc_low, NN)
    pulled = both[0:lines] + both[lines : 2 * lines] + rest
    way = dir_ref[...].reshape(lines, block)
    left = res_ref[...].reshape(lines, block)
    image = way + pulled
    img_ref[...] = image.reshape(members, cols, block)

    def fold(x):
        x = jnp.sum(x.reshape(lines // 8, 8, block), axis=0)
        return sum(x[:, i : i + 128] for i in range(0, block, 128))

    total_ref[0] += fold(left * left)
    total_ref[1] += fold(way * image)
    total_ref[2] += fold(left * image)
    total_ref[3] += fold(image * image)

    @pl.when(step == pl.num_programs(0) - 1)
    def _():
        lane = lax.broadcasted_iota(jnp.int32, (1, 128), 1)
        packed = jnp.zeros((1, 128), F32)
        for i in range(4):
            packed = jnp.where(lane == i, jnp.sum(total_ref[i]), packed)
        sums_ref[...] = jnp.broadcast_to(packed, sums_ref.shape)


def image_and_sums(localize, adj, west, east, pert, direction, residual, copies):
    members, _, cols, rows = pert.shape
    block = 256
    whole = lambda *dims: pl.BlockSpec(dims, lambda i: (0,) * len(dims))
    part = pl.BlockSpec((members, cols, block), lambda i: (0, 0, i))
    return pl.pallas_call(
        image_kernel,
        grid=(rows // block,),
        in_specs=[
            pl.BlockSpec((rows, block), lambda i: (0, i)),
            whole(3, cols, rows),
            whole(3 * HALO, rows),
            whole(3 * HALO, rows),
            whole(members, 3, cols, rows),
            part,
            part,
        ],
        out_specs=[part, whole(copies, 128)],
        out_shape=[
            jax.ShapeDtypeStruct((members, cols, rows), F32),
            jax.ShapeDtypeStruct((copies, 128), F32),
        ],
        scratch_shapes=[
            pltpu.VMEM((2 * members * cols, rows), BF16),
            pltpu.VMEM((4, 8, 128), F32),
        ],
        name="image",
    )(localize, adj, west, east, pert, direction, residual)


def neighbours(to_west, to_east):
    count = lax.axis_size(LON)
    east = [(i, (i + 1) % count) for i in range(count)]
    west = [(target, source) for source, target in east]
    from_west = lax.ppermute(to_east, LON, east)
    from_east = lax.ppermute(to_west, LON, west)
    return from_west, from_east


def body(control, residual, direction, ens_perturb, localize, obs_cell, obs_slot, obs_weight):
    lat_total = localize.shape[0]
    cols = control.shape[2]
    factors = jnp.asarray(grid_factors(lat_total))
    turned = lambda x: jnp.swapaxes(x, 1, 2)
    control_t, residual_t, direction_t = turned(control), turned(residual), turned(direction)
    pert = jnp.swapaxes(ens_perturb, 2, 3)
    obs_row = (obs_cell // cols)[None]
    obs_spot = (obs_slot * cols + obs_cell % cols)[None]
    inc, left, right = partial_increment(localize, direction_t, pert)
    west, east = neighbours(left, right)
    copies = lax.axis_size(ENS)
    seen = observed_parts(inc, west, east, factors, obs_row, obs_spot, copies)
    seen = lax.all_to_all(seen, ENS, 0, 0, tiled=True)
    adj, left, right = tile_adjoint(seen, obs_weight[None], obs_row, obs_spot, factors, cols)
    west, east = neighbours(left, right)
    image, sums = image_and_sums(
        localize, adj, west, east, pert, direction_t, residual_t, lax.axis_size(ENS_LON)
    )
    sums = jnp.sum(lax.all_to_all(sums, ENS_LON, 0, 0, tiled=True), axis=0)
    norm_old, curvature, cross_term, square = sums[0], sums[1], sums[2], sums[3]
    step_size = norm_old / curvature
    norm_new = norm_old - 2.0 * step_size * cross_term + step_size * step_size * square
    control_new = control_t + step_size * direction_t
    residual_new = residual_t - step_size * image
    direction_new = residual_new + norm_new / norm_old * direction_t
    return (turned(control_new), turned(residual_new), turned(direction_new))


def solution(mesh):
    split = Mesh(mesh.devices.reshape(2, 4, 8, 2, 2), ("ens_0", "ens_1", "lon_0", "lon_1", "lon_2"))
    placed = (
        P(ENS, None, LON),
        P(ENS, None, LON),
        P(ENS, None, LON),
        P(ENS, None, None, LON),
        P(),
        P(LON),
        P(LON),
        P(LON),
    )
    return jax.shard_map(
        body,
        mesh=split,
        in_specs=placed,
        out_specs=(P(ENS, None, LON), P(ENS, None, LON), P(ENS, None, LON)),
        check_vma=False,
    )
```

time: 241 us -> 88 us (0.37)
  starting transfers between devices: 71.6 us -> 8.27 us
  blocking collectives: 77.2 us -> 39.4 us
  Pallas kernels: 0 us -> 24 us
  waiting for transfers between devices: 26.1 us -> 3.76 us
  local copies, waits for them, and re-layouts: 25.7 us -> 3.76 us
  other arithmetic: 24.9 us -> 3.9 us
  matrix products: 9.98 us -> 0 us
    ppermute x24 -> x4, starting transfers between devices: 64.2 us -> 8.27 us  [the longest x2 4.68 us: neighbours(): from_east = lax.ppermute(to_west, LON, west)]
    psum x5 -> x0, blocking collectives: 46.4 us -> none  [by_axis(): value = lax.psum(value, axis)]
    pallas_call x0 -> x4, Pallas kernels: none -> 24 us  [the longest x1 6.62 us: observed_parts(): pl.pallas_call(forward_kernel, out_shape=jax.ShapeDtypeStruct((copies, no...]
    gather x1 -> x0, local copies, waits for them, and re-layouts: 23 us -> none  [body(): observed = jnp.concatenate(heights)[gather_index]]
    scatter-add x3 -> x0, other arithmetic: 22 us -> none  [the longest x1 21.9 us: body(): jnp.zeros(((STEPS + 1) * cells,), jnp.float32).at[slot_index].add(weighted)]
    all_to_all x1 -> x0, waiting for transfers between devices: 14.6 us -> none  [sent_and_summed(): lax.all_to_all(cut_along(value, dim, devices), axis, 0, 0, tiled=True)]
    dot_general x2 -> x0, matrix products: 9.98 us -> none  [the longest x1 6.81 us: body(): localized = jnp.einsum('ij,mjc->mic', localize, direction, precision=hi)]
    all_to_all x1 -> x2, blocking collectives: 30.9 us -> 39.4 us  [the longest x1 26.4 us: body(): sums = jnp.sum(lax.all_to_all(sums, ENS_LON, 0, 0, tiled=True), axis=0)]
  transfers between devices with their start and end apart: 25 -> 4, of which waited for: 10 -> 4; matrix products, arithmetic and copies ran while one was open for 0% -> 1% of each run, Pallas kernels for 0% -> 0%
where the time goes in v1:
time: 88 us; the launch traced here: 87.5 us
  blocking collectives  39.4 us (45%)
  Pallas kernels  24 us (27%)
  starting transfers between devices  8.27 us (9%)
  between operations  4.34 us (5%)
  other arithmetic  3.9 us (4%)
  local copies, waits for them, and re-layouts  3.76 us (4%)
  waiting for transfers between devices  3.76 us (4%)
    all_to_all x1, blocking collectives, body(): sums = jnp.sum(lax.all_to_all(sums, ENS_LON, 0, 0, tiled=True), axis=0)  26.4 us
    all_to_all x1, blocking collectives, body(): seen = lax.all_to_all(seen, ENS, 0, 0, tiled=True)  13.1 us
    pallas_call x1, Pallas kernels, observed_parts(): pl.pallas_call(forward_kernel, out_shape=jax.ShapeDtypeStruct((copies, no...  6.62 us
    pallas_call x1, Pallas kernels, tile_adjoint(): pl.pallas_call(adjoint_kernel, out_shape=[jax.ShapeDtypeStruct((3, cols,...  6.38 us
    pallas_call x1, Pallas kernels, image_and_sums(): pl.pallas_call(image_kernel, grid=(rows // block,), in_specs=[pl.BlockSpe...  5.82 us
    pallas_call x1, Pallas kernels, partial_increment(): pl.pallas_call(increment_kernel, grid=(rows // block,), in_specs=[pl.Bloc...  5.22 us
    ppermute x2, starting transfers between devices, neighbours(): from_east = lax.ppermute(to_west, LON, west)  4.68 us
    ppermute x2, starting transfers between devices, neighbours(): from_west = lax.ppermute(to_east, LON, east)  3.59 us
  transfers between devices with their start and end apart: 4, of which 4 were waited for; matrix products, arithmetic and copies ran while one was open for 1% of the time, Pallas kernels for 0%

profile of v1, /device:TPU:1, one launch (start us, length us, event | category | flops | bytes accessed | tf_op | source)
XLA Modules:
  0.0 87.5 jit_solution(10764351204726548827)
XLA Ops:
  0.6 0.0 copy-start.7
  0.6 0.0 copy-start.8
  0.7 5.2 %increment.1 = (f32[3,64,1024]{2,1,0:T(8,128)}, f32[9,1024]{1,0:T(8,128)}, f32[9,1024]{1,0:T(8,128)}) custom-call(f32[1024,1024]{1,0:T(8,128)} %loc_ref.3, f32[2,64,1024]{2,1,0:T(8,128)} %bitcast.24, bf16[2,3,64,1024]{3,2,1,0:T(8,128)(2,1)} %bitcast.26), custom_call_target="tpu_custom_call" | custom-call | tf_op jit(solution)/shard_map/increment/pallas_call | solution.py:95
  5.9 2.7 %collective-permute-start = (f32[9,1024]{1,0:T(8,128)}, f32[9,1024]{1,0:T(8,128)S(1)}, u32[]{:S(2)}, u32[]{:S(2)}) collective-permute-start(f32[9,1024]{1,0:T(8,128)} %get-tuple-element.12), channel_id=1, source_target_pairs={{0,1},{1,2},{2,3},{3,4},{4,5},{5,6},{6,7},{7,8},{8,9},{9,10},{10,1... | collective-permute-start | bytes 110600 | tf_op jit(solution)/shard_map/ppermute | solution.py:297
  8.6 0.6 collective-permute-start.1
  9.2 0.0 copy-done.7
  9.2 0.0 copy-done.8
  9.2 0.6 fusion.1
  9.8 0.4 collective-permute-done.west_ref
  10.2 0.0 copy-start.5
  10.2 2.3 %collective-permute-done.1.east_ref = f32[9,1024]{1,0:T(8,128)S(1)} collective-permute-done((f32[9,1024]{1,0:T(8,128)}, f32[9,1024]{1,0:T(8,128)S(1)}, u32[]{:S(2)}, u32[]{:S(2)}) %collective-permute-start.1) | collective-permute-done | bytes 36896 | tf_op jit(solution)/shard_map/ppermute | solution.py:298
  12.5 0.0 copy-start.6
  12.5 0.0 copy-done.5
  12.5 0.6 copy-done.6
  13.1 6.6 %forward.1 = f32[8,4096]{1,0:T(8,128)} custom-call(f32[3,64,1024]{2,1,0:T(8,128)} %get-tuple-element.11.inc_ref, f32[9,1024]{1,0:T(8,128)} %copy-done.5, f32[9,1024]{1,0:T(8,128)} %copy-done.6, f32[2,1024]{1,0:T(2,128)} %constant.35.clone.factor_ref, s32[1,4096]{1,0:T(1,128)} %bitcast.33, s32[1,4096]{1,0:T(1,128)} %bitcast.31), custom_call_target="tpu_custom_call" | custom-call | tf_op jit(solution)/shard_map/forward/pallas_call | solution.py:147
  19.7 0.0 copy-start
  19.7 0.0 copy-start.2
  19.7 1.1 %copy.12 = f32[8,1,4096]{2,1,0:T(1,128)S(1)} copy(f32[8,1,4096]{2,0,1:T(8,128)} %bitcast.29) | data formatting | bytes 262144 | tf_op jit(solution)/shard_map/all_to_all | solution.py:315
  20.8 13.1 %all_to_all.20 = f32[8,1,4096]{2,1,0:T(1,128)S(1)} all-to-all(f32[8,1,4096]{2,1,0:T(1,128)S(1)} %copy.12), channel_id=1, replica_groups=mesh['ens_0'=2,'ens_1'=4,'lon_0'=8,'lon_1'=2,'lon_2'=2] {'ens_0','ens_1'}, dimensions={0} | all-to-all | bytes 262144 | tf_op jit(solution)/shard_map/all_to_all | solution.py:315
  33.9 0.7 copy.16
  34.7 6.4 %adjoint.1 = (f32[3,64,1024]{2,1,0:T(8,128)}, f32[9,1024]{1,0:T(8,128)}, f32[9,1024]{1,0:T(8,128)}) custom-call(f32[8,4096]{1,0:T(8,128)} %bitcast.30, f32[1,4096]{1,0:T(1,128)} %bitcast.36, s32[1,4096]{1,0:T(1,128)} %bitcast.34, s32[1,4096]{1,0:T(1,128)} %bitcast.32, f32[2,1024]{1,0:T(2,128)} %constant.35.clone.factor_ref), custom_call_target="tpu_custom_call" | custom-call | tf_op jit(solution)/shard_map/adjoint/pallas_call | solution.py:199
  41.0 0.9 %collective-permute-start.2 = (f32[9,1024]{1,0:T(8,128)}, f32[9,1024]{1,0:T(8,128)S(1)}, u32[]{:S(2)}, u32[]{:S(2)}) collective-permute-start(f32[9,1024]{1,0:T(8,128)} %get-tuple-element.15), channel_id=1, source_target_pairs={{0,1},{1,2},{2,3},{3,4},{4,5},{5,6},{6,7},{7,8},{8,9},{9,10},{10,1... | collective-permute-start | bytes 110600 | tf_op jit(solution)/shard_map/ppermute | solution.py:297
  41.9 4.1 %collective-permute-start.3 = (f32[9,1024]{1,0:T(8,128)}, f32[9,1024]{1,0:T(8,128)S(1)}, u32[]{:S(2)}, u32[]{:S(2)}) collective-permute-start(f32[9,1024]{1,0:T(8,128)} %get-tuple-element.16), channel_id=1, source_target_pairs={{1,0},{2,1},{3,2},{4,3},{5,4},{6,5},{7,6},{8,7},{9,8},{10,9},{11,1... | collective-permute-start | bytes 110600 | tf_op jit(solution)/shard_map/ppermute | solution.py:298
  46.0 1.0 %collective-permute-done.2.west_ref = f32[9,1024]{1,0:T(8,128)S(1)} collective-permute-done((f32[9,1024]{1,0:T(8,128)}, f32[9,1024]{1,0:T(8,128)S(1)}, u32[]{:S(2)}, u32[]{:S(2)}) %collective-permute-start.2) | collective-permute-done | bytes 36896 | tf_op jit(solution)/shard_map/ppermute | solution.py:297
  47.0 0.0 copy-start.3
  47.0 0.2 collective-permute-done.3.east_ref
  47.1 0.0 copy-start.4
  47.1 0.5 copy-done.3
  47.6 0.2 copy-done.4
  47.8 0.0 copy-start.1
  47.8 5.8 %image.1 = (f32[2,64,1024]{2,1,0:T(8,128)}, f32[256,128]{1,0:T(8,128)}) custom-call(f32[1024,1024]{1,0:T(8,128)} %loc_ref.3, f32[3,64,1024]{2,1,0:T(8,128)} %get-tuple-element.14.adj_ref, f32[9,1024]{1,0:T(8,128)} %copy-done.3, f32[9,1024]{1,0:T(8,128)} %copy-done.4, bf16[2,3,64,1024]{3,2,1,0:T(8,128)(2,1)} %bitcast.27, f32[2,64,1024]{2,1,0:T(8,128)} %bitcast.25, ...), custom_call_target="tpu_custom_call" | custom-call | tf_op jit(solution)/shard_map/image/pallas_call | solution.py:268
  53.6 26.4 %all_to_all.21 = f32[256,1,128]{2,1,0:T(1,128)S(1)} all-to-all(f32[256,1,128]{2,1,0:T(1,128)} %bitcast.35), channel_id=1, replica_groups=mesh['ens_0'=2,'ens_1'=4,'lon_0'=8,'lon_1'=2,'lon_2'=2] {'ens_0','ens_1'..., dimensions={0} | all-to-all | bytes 262144 | tf_op jit(solution)/shard_map/all_to_all | solution.py:321
  79.9 0.3 reduce_sum.9
  80.2 0.6 fusion.4
  84.5 0.0 copy-done
  84.5 0.0 copy-done.2
  84.5 0.9 multiply_add_fusion
  85.4 0.0 copy-done.1
  85.4 2.1 %add_bitcast_fusion = (f32[2,1024,64]{1,2,0:T(8,128)}, f32[2,1024,64]{1,2,0:T(8,128)}) fusion(f32[]{:T(128)S(6)} %div.23, f32[2,64,1024]{2,1,0:T(8,128)} %get-tuple-element.18, f32[]{:T(128)S(6)} %div.22, f32[2,1024,64]{1,2,0:T(8,128)S(1)} %copy-done.1, f32[2,1024,64]{1,2,0:T(8,128)S(1)} %copy-done), kind=kLoop, calls=%fused_computation | loop fusion | flops 524288 | bytes 2621448 | tf_op jit(solution)/shard_map/transpose | solution.py:306
Async XLA Ops:
  0.6 8.5 %copy-start.7 = (s32[4096]{0:T(1024)S(1)}, s32[4096]{0:T(1024)}, u32[]{:S(2)}) copy-start(s32[4096]{0:T(1024)} %param.15) | copy-start | bytes 49156
  0.6 8.5 %copy-start.8 = (s32[4096]{0:T(1024)S(1)}, s32[4096]{0:T(1024)}, u32[]{:S(2)}) copy-start(s32[4096]{0:T(1024)} %param.14) | copy-start | bytes 49156
  5.9 4.3 %collective-permute-start = (f32[9,1024]{1,0:T(8,128)}, f32[9,1024]{1,0:T(8,128)S(1)}, u32[]{:S(2)}, u32[]{:S(2)}) collective-permute-start(f32[9,1024]{1,0:T(8,128)} %get-tuple-element.12), channel_id=1, source_target_pairs={{0,1},{1,2},{2,3},{3,4},{4,5},{5,6},{6,7},{7,8},{8,9},{9,10},{10,1... | collective-permute-start | bytes 110600 | tf_op jit(solution)/shard_map/ppermute | solution.py:297
  8.6 3.9 %collective-permute-start.1 = (f32[9,1024]{1,0:T(8,128)}, f32[9,1024]{1,0:T(8,128)S(1)}, u32[]{:S(2)}, u32[]{:S(2)}) collective-permute-start(f32[9,1024]{1,0:T(8,128)} %get-tuple-element.13), channel_id=1, source_target_pairs={{1,0},{2,1},{3,2},{4,3},{5,4},{6,5},{7,6},{8,7},{9,8},{10,9},{11,1... | collective-permute-start | bytes 110600 | tf_op jit(solution)/shard_map/ppermute | solution.py:298
  10.2 2.3 %copy-start.5 = (f32[9,1024]{1,0:T(8,128)}, f32[9,1024]{1,0:T(8,128)S(1)}, u32[]{:S(2)}) copy-start(f32[9,1024]{1,0:T(8,128)S(1)} %collective-permute-done.west_ref) | copy-start | bytes 110596
  12.5 0.6 copy-start.6
  19.7 64.8 %copy-start = (f32[2,1024,64]{1,2,0:T(8,128)S(1)}, f32[2,1024,64]{1,2,0:T(8,128)}, u32[]{:S(2)}) copy-start(f32[2,1024,64]{1,2,0:T(8,128)} %param.11) | copy-start | bytes 1572868
  19.7 64.8 %copy-start.2 = (f32[2,1024,64]{1,2,0:T(8,128)S(1)}, f32[2,1024,64]{1,2,0:T(8,128)}, u32[]{:S(2)}) copy-start(f32[2,1024,64]{1,2,0:T(8,128)} %param.9) | copy-start | bytes 1572868
  41.0 5.9 %collective-permute-start.2 = (f32[9,1024]{1,0:T(8,128)}, f32[9,1024]{1,0:T(8,128)S(1)}, u32[]{:S(2)}, u32[]{:S(2)}) collective-permute-start(f32[9,1024]{1,0:T(8,128)} %get-tuple-element.15), channel_id=1, source_target_pairs={{0,1},{1,2},{2,3},{3,4},{4,5},{5,6},{6,7},{7,8},{8,9},{9,10},{10,1... | collective-permute-start | bytes 110600 | tf_op jit(solution)/shard_map/ppermute | solution.py:297
  41.9 5.2 %collective-permute-start.3 = (f32[9,1024]{1,0:T(8,128)}, f32[9,1024]{1,0:T(8,128)S(1)}, u32[]{:S(2)}, u32[]{:S(2)}) collective-permute-start(f32[9,1024]{1,0:T(8,128)} %get-tuple-element.16), channel_id=1, source_target_pairs={{1,0},{2,1},{3,2},{4,3},{5,4},{6,5},{7,6},{8,7},{9,8},{10,9},{11,1... | collective-permute-start | bytes 110600 | tf_op jit(solution)/shard_map/ppermute | solution.py:298
  47.0 0.6 copy-start.3
  47.1 0.6 copy-start.4
  47.8 37.6 %copy-start.1 = (f32[2,1024,64]{1,2,0:T(8,128)S(1)}, f32[2,1024,64]{1,2,0:T(8,128)}, u32[]{:S(2)}) copy-start(f32[2,1024,64]{1,2,0:T(8,128)} %param.10) | copy-start | bytes 1572868

commit v2 on v1

v2 whole, which is shorter than its diff:
```python
import functools

import jax
import jax.numpy as jnp
import numpy as np
from jax import lax
from jax.experimental import pallas as pl
from jax.experimental.pallas import tpu as pltpu
from jax.sharding import Mesh
from jax.sharding import PartitionSpec as P

STEPS = 3
HALO = 3
PAD = 8
LON = ("lon_0", "lon_1", "lon_2")
ENS = ("ens_0", "ens_1")
ENS_LON = ("ens_0", "ens_1", "lon_0", "lon_1", "lon_2")

wave_speed = 0.35
rotation = 0.2

F32 = jnp.float32
BF16 = jnp.bfloat16
NT = (((1,), (1,)), ((), ()))
NN = (((1,), (0,)), ((), ()))
HBM = pl.BlockSpec(memory_space=pltpu.HBM)


def split_two(x):
    high = x.astype(BF16)
    low = (x - high.astype(F32)).astype(BF16)
    return high, low


def dot(a, b, dims):
    return lax.dot_general(a, b, dims, preferred_element_type=F32)


def grid_factors(lat_total):
    row_ids = np.arange(lat_total).astype(np.float32)
    latitude = (-1.0 / 3.0 + 2.0 / 3.0 * (row_ids + 0.5) / lat_total) * np.pi
    return np.stack([1.0 / np.cos(latitude), np.sin(latitude)]).astype(np.float32)


def model_step(h, u, v, orient, metric, coriolis):
    wide, rows = h.shape
    lane = lax.broadcasted_iota(jnp.int32, (1, rows), 1)
    lon_scale = (orient * wave_speed * 0.5) * metric
    lat_scale = orient * wave_speed * 0.5
    turn = (orient * rotation) * coriolis
    keep_next = jnp.where(lane == rows - 1, 0.0, lat_scale)
    keep_last = jnp.where(lane == 0, 0.0, lat_scale)

    def lon_diff(x):
        return lon_scale * (pltpu.roll(x, wide - 1, 0) - pltpu.roll(x, 1, 0))

    def lat_diff(x):
        return keep_next * pltpu.roll(x, rows - 1, 1) - keep_last * pltpu.roll(x, 1, 1)

    return (
        h - (lon_diff(u) + lat_diff(v)),
        u - lon_diff(h) + turn * v,
        v - lat_diff(h) - turn * u,
    )


def call(kernel, name, out_shape, scratch, flops, limit_mib=24, **options):
    return pl.pallas_call(
        kernel,
        name=name,
        out_shape=out_shape,
        scratch_shapes=scratch,
        compiler_params=pltpu.CompilerParams(vmem_limit_bytes=limit_mib << 20),
        cost_estimate=pl.CostEstimate(flops=flops, bytes_accessed=1 << 20, transcendentals=0),
        **options,
    )


def floats(*dims):
    return jax.ShapeDtypeStruct(dims, F32)


def rows_and_spots(cell, slot, cols):
    bits = cols.bit_length() - 1
    assert cols == 1 << bits
    return lax.shift_right_logical(cell, bits), slot, cell & (cols - 1)


def one_hot_rows(row, rows):
    ids = lax.broadcasted_iota(jnp.int32, (rows, row.shape[1]), 0)
    return (ids == row).astype(F32).astype(BF16)


def edges_of(field):
    return slice(HALO * field, HALO * (field + 1))


def increment_kernel(
    loc_hbm, dir_hbm, pert_hbm, inc_ref, left_ref, right_ref, high_ref, low_ref,
    loc_ref, dir_ref, pert_ref, parts_ref, sems,
):
    members, cols, rows = dir_ref.shape
    lines = members * cols
    block = 256
    blocks = rows // block
    first = pltpu.make_async_copy(dir_hbm, dir_ref, sems.at[0])
    first.start()
    copies = []
    for i in range(blocks):
        here = slice(i * block, (i + 1) * block)
        copies.append(
            pltpu.make_async_copy(loc_hbm.at[here], loc_ref.at[here], sems.at[2 + i])
        )
    copies[0].start()
    second = pltpu.make_async_copy(pert_hbm, pert_ref, sems.at[1])
    second.start()
    for copy in copies[1:]:
        copy.start()
    first.wait()
    high, low = split_two(dir_ref[...].reshape(lines, rows))
    parts_ref[0:lines] = high
    parts_ref[lines : 2 * lines] = low
    for i in range(blocks):
        here = slice(i * block, (i + 1) * block)
        copies[i].wait()
        loc_high, loc_low = split_two(loc_ref[here])
        high_ref[here] = loc_high
        low_ref[here] = loc_low
        both = dot(parts_ref[...], loc_high, NT)
        rest = dot(parts_ref[0:lines], loc_low, NT)
        localized = both[0:lines] + both[lines : 2 * lines] + rest
        if i == 0:
            second.wait()
        for field in range(3):
            total = None
            for m in range(members):
                term = pert_ref[m, field, :, here].astype(F32) * localized[m * cols : (m + 1) * cols]
                total = term if total is None else total + term
            inc_ref[field, :, here] = total
            left_ref[edges_of(field), here] = total[0:HALO]
            right_ref[edges_of(field), here] = total[cols - HALO : cols]


def partial_increment(localize, direction, pert):
    members, cols, rows = direction.shape
    half = jax.ShapeDtypeStruct((rows, rows), BF16)
    return call(
        increment_kernel,
        "increment",
        [floats(3, cols, rows), floats(3 * HALO, rows), floats(3 * HALO, rows), half, half],
        [
            pltpu.VMEM((rows, rows), F32),
            pltpu.VMEM(direction.shape, F32),
            pltpu.VMEM(pert.shape, BF16),
            pltpu.VMEM((2 * members * cols, rows), BF16),
            pltpu.SemaphoreType.DMA((2 + rows // 256,)),
        ],
        10**9,
        in_specs=[HBM, HBM, HBM],
    )(*(pltpu.with_memory_space_constraint(x, pltpu.HBM) for x in (localize, direction, pert)))


def forward_kernel(inc_ref, factor_ref, cell_ref, slot_ref, out_ref, state_ref, parts_ref):
    _, cols, rows = inc_ref.shape
    nobs = cell_ref.shape[1]
    state_ref[...] = jnp.zeros(state_ref.shape, F32)
    for field in range(3):
        state_ref[field, PAD : PAD + cols] = inc_ref[field]
    metric = factor_ref[0:1]
    coriolis = factor_ref[1:2]
    spots = STEPS * cols
    for moment in range(STEPS):
        h, u, v = model_step(state_ref[0], state_ref[1], state_ref[2], 1.0, metric, coriolis)
        state_ref[0] = h
        state_ref[1] = u
        state_ref[2] = v
        high, low = split_two(h[PAD : PAD + cols])
        parts_ref[moment * cols : (moment + 1) * cols] = high
        parts_ref[spots + moment * cols : spots + (moment + 1) * cols] = low
    chunk = 512
    for start in range(0, nobs, chunk):
        here = slice(start, start + chunk)
        row, slot, col = rows_and_spots(cell_ref[:, here], slot_ref[:, here], cols)
        picked = dot(parts_ref[...], one_hot_rows(row, rows), NN)
        picked = picked[0:spots] + picked[spots : 2 * spots]
        spot_hot = lax.broadcasted_iota(jnp.int32, (spots, chunk), 0) == slot * cols + col
        out_ref[:, here] = jnp.sum(jnp.where(spot_hot, picked, 0.0), axis=0, keepdims=True)


def own_observed(inc, factors, cell, slot):
    _, cols, rows = inc.shape
    return call(
        forward_kernel,
        "forward",
        floats(1, cell.shape[1]),
        [
            pltpu.VMEM((3, cols + 2 * PAD, rows), F32),
            pltpu.VMEM((2 * STEPS * cols, rows), BF16),
        ],
        4 * 10**9,
    )(inc, factors, cell, slot)


def border_kernel(
    own_ref, west_ref, east_ref, factor_ref, cell_ref, slot_ref, out_ref, state_ref, parts_ref,
    *, cols,
):
    rows = west_ref.shape[1]
    nobs = cell_ref.shape[1]
    state_ref[...] = jnp.zeros(state_ref.shape, F32)
    for field in range(3):
        state_ref[field, PAD - HALO : PAD] = west_ref[edges_of(field)]
        state_ref[field, 3 * PAD : 3 * PAD + HALO] = east_ref[edges_of(field)]
    metric = factor_ref[0:1]
    coriolis = factor_ref[1:2]
    near = 2 * PAD
    spots = STEPS * near
    for moment in range(STEPS):
        h, u, v = model_step(state_ref[0], state_ref[1], state_ref[2], 1.0, metric, coriolis)
        state_ref[0] = h
        state_ref[1] = u
        state_ref[2] = v
        high, low = split_two(h[PAD : 3 * PAD])
        parts_ref[moment * near : (moment + 1) * near] = high
        parts_ref[spots + moment * near : spots + (moment + 1) * near] = low
    chunk = 512
    for start in range(0, nobs, chunk):
        here = slice(start, start + chunk)
        row, slot, col = rows_and_spots(cell_ref[:, here], slot_ref[:, here], cols)
        picked = dot(parts_ref[...], one_hot_rows(row, rows), NN)
        picked = picked[0:spots] + picked[spots : 2 * spots]
        east_spot = jnp.where(col >= cols - PAD, slot * near + (col - cols + near), -1)
        spot = jnp.where(col < PAD, slot * near + col, east_spot)
        spot_hot = lax.broadcasted_iota(jnp.int32, (spots, chunk), 0) == spot
        value = jnp.sum(jnp.where(spot_hot, picked, 0.0), axis=0, keepdims=True)
        value = value + own_ref[:, here]
        for i in range(0, chunk, 128):
            line = (start + i) // 128
            out_ref[:, line, :] = jnp.broadcast_to(value[:, i : i + 128], (out_ref.shape[0], 128))


def observed_parts(own, west, east, factors, cell, slot, cols, copies):
    rows = west.shape[1]
    return call(
        functools.partial(border_kernel, cols=cols),
        "border",
        floats(copies, cell.shape[1] // 128, 128),
        [
            pltpu.VMEM((3, 4 * PAD, rows), F32),
            pltpu.VMEM((4 * STEPS * PAD, rows), BF16),
        ],
        10**9,
    )(own, west, east, factors, cell, slot)


def adjoint_kernel(
    seen_ref, weight_ref, cell_ref, slot_ref, factor_ref, adj_ref, left_ref, right_ref,
    state_ref, force_ref,
):
    _, cols, rows = adj_ref.shape
    nobs = cell_ref.shape[1]
    spots = STEPS * cols
    chunk = 512
    seen = jnp.sum(seen_ref[...], axis=0)
    for start in range(0, nobs, chunk):
        here = slice(start, start + chunk)
        row, slot, col = rows_and_spots(cell_ref[:, here], slot_ref[:, here], cols)
        lines = range(start // 128, (start + chunk) // 128)
        total = jnp.concatenate([seen[i : i + 1] for i in lines], axis=1)
        weighted = weight_ref[:, here] * total
        spot_hot = lax.broadcasted_iota(jnp.int32, (spots, chunk), 0) == slot * cols + col
        high, low = split_two(jnp.where(spot_hot, weighted, 0.0))
        part = dot(jnp.concatenate([high, low], axis=0), one_hot_rows(row, rows), NT)
        part = part[0:spots] + part[spots : 2 * spots]
        if start == 0:
            force_ref[...] = part
        else:
            force_ref[...] += part
    metric = factor_ref[0:1]
    coriolis = factor_ref[1:2]
    state_ref[...] = jnp.zeros(state_ref.shape, F32)
    for moment in reversed(range(STEPS)):
        state_ref[0, PAD : PAD + cols] += force_ref[moment * cols : (moment + 1) * cols]
        h, u, v = model_step(state_ref[0], state_ref[1], state_ref[2], -1.0, metric, coriolis)
        state_ref[0] = h
        state_ref[1] = u
        state_ref[2] = v
    for field in range(3):
        adj_ref[field] = state_ref[field, PAD : PAD + cols]
        left_ref[edges_of(field)] = state_ref[field, PAD - HALO : PAD]
        right_ref[edges_of(field)] = state_ref[field, PAD + cols : PAD + cols + HALO]


def tile_adjoint(seen, weight, cell, slot, factors, cols):
    rows = factors.shape[1]
    return call(
        adjoint_kernel,
        "adjoint",
        [floats(3, cols, rows), floats(3 * HALO, rows), floats(3 * HALO, rows)],
        [
            pltpu.VMEM((3, cols + 2 * PAD, rows), F32),
            pltpu.VMEM((STEPS * cols, rows), F32),
        ],
        4 * 10**9,
    )(seen, weight, cell, slot, factors)


def three_products(parts_ref, high_ref, low_ref, lines):
    both = dot(parts_ref[...], high_ref[...], NN)
    rest = dot(parts_ref[0:lines], low_ref[...], NN)
    return both[0:lines] + both[lines : 2 * lines] + rest


def image_kernel(high_ref, low_ref, adj_ref, pert_ref, dir_ref, img_ref, parts_ref):
    members, cols, rows = dir_ref.shape
    lines = members * cols
    for m in range(members):
        projected = pert_ref[m, 0].astype(F32) * adj_ref[0]
        projected += pert_ref[m, 1].astype(F32) * adj_ref[1]
        projected += pert_ref[m, 2].astype(F32) * adj_ref[2]
        high, low = split_two(projected)
        parts_ref[m * cols : (m + 1) * cols] = high
        parts_ref[lines + m * cols : lines + (m + 1) * cols] = low
    pulled = three_products(parts_ref, high_ref, low_ref, lines)
    img_ref[...] = dir_ref[...] + pulled.reshape(members, cols, rows)


def own_image(high, low, adj, pert, direction):
    members, cols, rows = direction.shape
    return call(
        image_kernel,
        "image",
        floats(members, cols, rows),
        [pltpu.VMEM((2 * members * cols, rows), BF16)],
        10**9,
    )(high, low, adj, pert, direction)


def closing_kernel(
    high_ref, low_ref, own_ref, west_ref, east_ref, pert_ref, dir_ref, res_ref, img_ref, sums_ref,
    edge_ref, parts_ref,
):
    members, cols, rows = dir_ref.shape
    near = 2 * PAD
    lines = members * near
    edge_ref[...] = jnp.zeros(edge_ref.shape, F32)
    for field in range(3):
        edge_ref[field, 0:HALO] = west_ref[edges_of(field)]
        edge_ref[field, near - HALO : near] = east_ref[edges_of(field)]
    for m in range(members):
        west = jnp.zeros((PAD, rows), F32)
        east = jnp.zeros((PAD, rows), F32)
        for field in range(3):
            west += pert_ref[m, field, 0:PAD].astype(F32) * edge_ref[field, 0:PAD]
            east += pert_ref[m, field, cols - PAD : cols].astype(F32) * edge_ref[field, PAD:near]
        high, low = split_two(jnp.concatenate([west, east], axis=0))
        parts_ref[m * near : (m + 1) * near] = high
        parts_ref[lines + m * near : lines + (m + 1) * near] = low
    pulled = three_products(parts_ref, high_ref, low_ref, lines)
    totals = [jnp.zeros((8, rows), F32) for _ in range(4)]
    for m in range(members):
        for start in range(0, cols, PAD):
            here = slice(start, start + PAD)
            image = own_ref[m, here]
            if start == 0:
                image = image + pulled[m * near : m * near + PAD]
            if start == cols - PAD:
                image = image + pulled[m * near + PAD : (m + 1) * near]
            img_ref[m, here] = image
            way = dir_ref[m, here]
            left = res_ref[m, here]
            totals[0] += left * left
            totals[1] += way * image
            totals[2] += left * image
            totals[3] += image * image
    lane = lax.broadcasted_iota(jnp.int32, (1, 128), 1)
    packed = jnp.zeros((1, 128), F32)
    for i in range(4):
        total = jnp.sum(jnp.sum(totals[i], axis=0, keepdims=True), axis=1, keepdims=True)
        packed = jnp.where(lane == i, total, packed)
    sums_ref[...] = jnp.broadcast_to(packed, sums_ref.shape)


def image_and_sums(high, low, own, west, east, pert, direction, residual, copies):
    members, cols, rows = direction.shape
    return call(
        closing_kernel,
        "closing",
        [floats(members, cols, rows), floats(copies, 128)],
        [
            pltpu.VMEM((3, 2 * PAD, rows), F32),
            pltpu.VMEM((4 * members * PAD, rows), BF16),
        ],
        5 * 10**8,
    )(high, low, own, west, east, pert, direction, residual)


def update_kernel(
    sums_ref, control_ref, res_ref, dir_ref, img_ref, control_out, res_out, dir_out, new_ref, sems
):
    members, cols, rows = dir_ref.shape
    total = jnp.sum(sums_ref[...], axis=0, keepdims=True)
    lane = lax.broadcasted_iota(jnp.int32, (1, 128), 1)

    def lane_of(i):
        return jnp.sum(jnp.where(lane == i, total, 0.0), axis=1, keepdims=True)

    norm_old, curvature, cross_term, square = (lane_of(i) for i in range(4))
    step_size = norm_old / curvature
    norm_new = norm_old - 2.0 * step_size * cross_term + step_size * step_size * square
    ratio = norm_new / norm_old
    copies = []
    for m in range(members):
        way = dir_ref[m]
        left = res_ref[m] - step_size * img_ref[m]
        new_ref[0, m] = control_ref[m] + step_size * way
        new_ref[1, m] = left
        new_ref[2, m] = left + ratio * way
        for i, out in enumerate((control_out, res_out, dir_out)):
            copy = pltpu.make_async_copy(new_ref.at[i, m], out.at[m], sems.at[3 * m + i])
            copy.start()
            copies.append(copy)
    for copy in copies:
        copy.wait()


def updated(sums, control, residual, direction, image):
    members = control.shape[0]
    return call(
        update_kernel,
        "update",
        [floats(*control.shape)] * 3,
        [pltpu.VMEM((3, *control.shape), F32), pltpu.SemaphoreType.DMA((3 * members,))],
        10**7,
        out_specs=[HBM, HBM, HBM],
    )(sums, control, residual, direction, image)


def neighbours(to_west, to_east):
    count = lax.axis_size(LON)
    east = [(i, (i + 1) % count) for i in range(count)]
    west = [(target, source) for source, target in east]
    from_west = lax.ppermute(to_east, LON, east)
    from_east = lax.ppermute(to_west, LON, west)
    return from_west, from_east


def body(control, residual, direction, ens_perturb, localize, obs_cell, obs_slot, obs_weight):
    cols = control.shape[2]
    factors = jnp.asarray(grid_factors(localize.shape[0]))
    turned = lambda x: jnp.swapaxes(x, 1, 2)
    control_t, residual_t, direction_t = turned(control), turned(residual), turned(direction)
    pert = jnp.swapaxes(ens_perturb, 2, 3)
    cell, slot, weight = obs_cell[None], obs_slot[None], obs_weight[None]
    inc, left, right, high, low = partial_increment(localize, direction_t, pert)
    west, east = neighbours(left, right)
    own = own_observed(inc, factors, cell, slot)
    seen = observed_parts(own, west, east, factors, cell, slot, cols, lax.axis_size(ENS))
    seen = lax.all_to_all(seen, ENS, 0, 0, tiled=True)
    adj, left, right = tile_adjoint(seen, weight, cell, slot, factors, cols)
    west, east = neighbours(left, right)
    image = own_image(high, low, adj, pert, direction_t)
    image, sums = image_and_sums(
        high, low, image, west, east, pert, direction_t, residual_t, lax.axis_size(ENS_LON)
    )
    sums = lax.all_to_all(sums, ENS_LON, 0, 0, tiled=True)
    results = updated(sums, control_t, residual_t, direction_t, image)
    return tuple(turned(x) for x in results)


def solution(mesh):
    split = Mesh(mesh.devices.reshape(2, 4, 8, 2, 2), ("ens_0", "ens_1", "lon_0", "lon_1", "lon_2"))
    placed = (
        P(ENS, None, LON),
        P(ENS, None, LON),
        P(ENS, None, LON),
        P(ENS, None, None, LON),
        P(),
        P(LON),
        P(LON),
        P(LON),
    )
    return jax.shard_map(
        body,
        mesh=split,
        in_specs=placed,
        out_specs=(P(ENS, None, LON), P(ENS, None, LON), P(ENS, None, LON)),
        check_vma=False,
    )
```

time: 88 us -> 69.2 us (0.79)
  Pallas kernels: 24 us -> 19.5 us
  other arithmetic: 3.9 us -> 0 us
  waiting for transfers between devices: 3.76 us -> 0.01 us
  local copies, waits for them, and re-layouts: 3.76 us -> 0.05 us
  between operations: 4.34 us -> 0.91 us
  starting transfers between devices: 8.27 us -> 10.2 us
  blocking collectives: 39.4 us -> 38.4 us
    pallas_call x4 -> x7, Pallas kernels: 24 us -> 19.5 us  [the longest x1 4.6 us: tile_adjoint(): call(adjoint_kernel, 'adjoint', [floats(3, cols, rows), floats(3 * HALO,...]
    ppermute x2, waiting for transfers between devices: 2.41 us -> 0.01 us  [neighbours(): from_east = lax.ppermute(to_west, LON, west)]
    transpose x1 -> x0, other arithmetic: 2.13 us -> none  [body(): turned = lambda x: jnp.swapaxes(x, 1, 2)]
    unnamed x19 -> x16, local copies, waits for them, and re-layouts: 2.02 us -> 0.05 us
    ppermute x2, starting transfers between devices: 3.59 us -> 5.4 us  [neighbours(): from_west = lax.ppermute(to_east, LON, east)]
    add x2 -> x0, other arithmetic: 1.49 us -> none  [the longest x1 0.86 us: body(): control_new = control_t + step_size * direction_t]
    ppermute x2, waiting for transfers between devices: 1.35 us -> 0.01 us  [neighbours(): from_west = lax.ppermute(to_east, LON, east)]
    all_to_all x1 -> x0, local copies, waits for them, and re-layouts: 1.13 us -> none  [body(): seen = lax.all_to_all(seen, ENS, 0, 0, tiled=True)]
  transfers between devices with their start and end apart: 4 -> 4, of which waited for: 4 -> 0; matrix products, arithmetic and copies ran while one was open for 1% -> 0% of each run, Pallas kernels for 0% -> 8%
where the time goes in v2:
time: 69.2 us; the launch traced here: 69.1 us
  blocking collectives  38.4 us (55%)
  Pallas kernels  19.5 us (28%)
  starting transfers between devices  10.2 us (15%)
  between operations  0.91 us (1%)
    all_to_all x1, blocking collectives, body(): sums = lax.all_to_all(sums, ENS_LON, 0, 0, tiled=True)  25.9 us
    all_to_all x1, blocking collectives, body(): seen = lax.all_to_all(seen, ENS, 0, 0, tiled=True)  12.5 us
    ppermute x2, starting transfers between devices, neighbours(): from_west = lax.ppermute(to_east, LON, east)  5.4 us
    ppermute x2, starting transfers between devices, neighbours(): from_east = lax.ppermute(to_west, LON, west)  4.79 us
    pallas_call x1, Pallas kernels, tile_adjoint(): call(adjoint_kernel, 'adjoint', [floats(3, cols, rows), floats(3 * HALO,...  4.6 us
    pallas_call x1, Pallas kernels, own_observed(): call(forward_kernel, 'forward', floats(1, cell.shape[1]), [pltpu.VMEM((3,...  4.5 us
    pallas_call x1, Pallas kernels, partial_increment(): call(increment_kernel, 'increment', [floats(3, cols, rows), floats(3 * HA...  4.35 us
    pallas_call x1, Pallas kernels, observed_parts(): call(functools.partial(border_kernel, cols=cols), 'border', floats(copies...  2.6 us
  transfers between devices with their start and end apart: 4, of which 0 were waited for; matrix products, arithmetic and copies ran while one was open for 0% of the time, Pallas kernels for 8%

profile of v2, /device:TPU:1, one launch (start us, length us, event | category | flops | bytes accessed | tf_op | source)
XLA Modules:
  0.0 69.1 jit_solution(4001831630007434098)
XLA Ops:
  0.6 0.0 copy-start.4
  0.6 0.0 copy-start.5
  0.7 0.0 copy-start.7
  0.7 4.4 %increment.1 = (f32[3,64,1024]{2,1,0:T(8,128)S(1)}, f32[9,1024]{1,0:T(8,128)S(1)}, f32[9,1024]{1,0:T(8,128)S(1)}, bf16[1024,1024]{1,0:T(8,128)(2,1)S(1)}, bf16[1024,1024]{1,0:T(8,128)(2,1)S(1)}) custom-call(f32[1024,1024]{1,0:T(8,128)} %loc_hbm.1, f32[2,64,1024]{2,1,0:T(8,128)} %bitcast.14, bf16[2,3,64,1024]{3,2,1,0:T(8,128)(2,1)} %bitcast.18), custom_call_target="tpu_custom_call" | custom-call | flops 1000000000 | bytes 1048576 | tf_op jit(solution)/shard_map/increment/pallas_call | solution.py:147
  5.0 2.8 %collective-permute-start = (f32[9,1024]{1,0:T(8,128)S(1)}, f32[9,1024]{1,0:T(8,128)S(1)}, u32[]{:S(2)}, u32[]{:S(2)}) collective-permute-start(f32[9,1024]{1,0:T(8,128)S(1)} %get-tuple-element.19), channel_id=1, source_target_pairs={{0,1},{1,2},{2,3},{3,4},{4,5},{5,6},{6,7},{7,8},{8,9},{9,10},{10,1... | collective-permute-start | bytes 110600 | tf_op jit(solution)/shard_map/ppermute | solution.py:443
  7.8 0.6 collective-permute-start.1
  8.4 0.0 copy-done.4
  8.4 0.0 copy-done.5
  8.4 0.0 copy-done.7
  8.4 4.5 %forward.1.own_ref = f32[1,4096]{1,0:T(1,128)S(1)} custom-call(f32[3,64,1024]{2,1,0:T(8,128)S(1)} %get-tuple-element.18.inc_ref, f32[2,1024]{1,0:T(2,128)S(1)} %copy-done.7, s32[1,4096]{1,0:T(1,128)S(1)} %bitcast.26, s32[1,4096]{1,0:T(1,128)S(1)} %bitcast.29), custom_call_target="tpu_custom_call" | custom-call | flops 4000000000 | bytes 1048576 | tf_op jit(solution)/shard_map/forward/pallas_call | solution.py:192
  12.9 0.0 copy-start.6
  12.9 0.0 collective-permute-done.west_ref
  12.9 0.0 collective-permute-done.1.east_ref
  12.9 2.6 %border.1 = f32[8,32,128]{2,1,0:T(8,128)S(1)} custom-call(f32[1,4096]{1,0:T(1,128)S(1)} %forward.1.own_ref, f32[9,1024]{1,0:T(8,128)S(1)} %collective-permute-done.west_ref, f32[9,1024]{1,0:T(8,128)S(1)} %collective-permute-done.1.east_ref, f32[2,1024]{1,0:T(2,128)S(1)} %copy-done.7, s32[1,4096]{1,0:T(1,128)S(1)} %bitcast.27, s32[1,4096]{1,0:T(1,128)S(1)} %bitcast.30), custom_call_target="tpu_custom_call" | custom-call | flops 1000000000 | bytes 1048576 | tf_op jit(solution)/shard_map/border/pallas_call | solution.py:244
  15.6 12.5 %all_to_all.16.seen_ref = f32[8,32,128]{2,1,0:T(8,128)S(1)} all-to-all(f32[8,32,128]{2,1,0:T(8,128)S(1)} %border.1), channel_id=1, replica_groups=mesh['ens_0'=2,'ens_1'=4,'lon_0'=8,'lon_1'=2,'lon_2'=2] {'ens_0','ens_1'}, dimensions={0} | all-to-all | bytes 262144 | tf_op jit(solution)/shard_map/all_to_all | solution.py:459
  28.0 0.0 copy-done.6
  28.0 0.0 copy-start
  28.0 0.0 copy-start.1
  28.0 4.6 %adjoint.1 = (f32[3,64,1024]{2,1,0:T(8,128)S(1)}, f32[9,1024]{1,0:T(8,128)S(1)}, f32[9,1024]{1,0:T(8,128)S(1)}) custom-call(f32[8,32,128]{2,1,0:T(8,128)S(1)} %all_to_all.16.seen_ref, f32[1,4096]{1,0:T(1,128)S(1)} %bitcast.32, s32[1,4096]{1,0:T(1,128)S(1)} %bitcast.28, s32[1,4096]{1,0:T(1,128)S(1)} %bitcast.31, f32[2,1024]{1,0:T(2,128)S(1)} %copy-done.7), custom_call_target="tpu_custom_call" | custom-call | flops 4000000000 | bytes 1048576 | tf_op jit(solution)/shard_map/adjoint/pallas_call | solution.py:296
  32.7 2.6 %collective-permute-start.2 = (f32[9,1024]{1,0:T(8,128)S(1)}, f32[9,1024]{1,0:T(8,128)S(1)}, u32[]{:S(2)}, u32[]{:S(2)}) collective-permute-start(f32[9,1024]{1,0:T(8,128)S(1)} %get-tuple-element.22), channel_id=1, source_target_pairs={{0,1},{1,2},{2,3},{3,4},{4,5},{5,6},{6,7},{7,8},{8,9},{9,10},{10,1... | collective-permute-start | bytes 110600 | tf_op jit(solution)/shard_map/ppermute | solution.py:443
  35.3 4.2 %collective-permute-start.3 = (f32[9,1024]{1,0:T(8,128)S(1)}, f32[9,1024]{1,0:T(8,128)S(1)}, u32[]{:S(2)}, u32[]{:S(2)}) collective-permute-start(f32[9,1024]{1,0:T(8,128)S(1)} %get-tuple-element.23), channel_id=1, source_target_pairs={{1,0},{2,1},{3,2},{4,3},{5,4},{6,5},{7,6},{8,7},{9,8},{10,9},{11,1... | collective-permute-start | bytes 110600 | tf_op jit(solution)/shard_map/ppermute | solution.py:444
  39.5 0.0 copy-done
  39.5 0.0 copy-done.1
  39.5 0.0 copy-start.2
  39.5 1.0 %image.1.own_ref = f32[2,64,1024]{2,1,0:T(8,128)S(1)} custom-call(bf16[1024,1024]{1,0:T(8,128)(2,1)S(1)} %get-tuple-element.16.high_ref, bf16[1024,1024]{1,0:T(8,128)(2,1)S(1)} %get-tuple-element.17.low_ref, f32[3,64,1024]{2,1,0:T(8,128)S(1)} %get-tuple-element.21.adj_ref, bf16[2,3,64,1024]{3,2,1,0:T(8,128)(2,1)S(1)} %bitcast.19, f32[2,64,1024]{2,1,0:T(8,128)S(1)} %bitcast.15), custom_call_target="tpu_custom_call" | custom-call | flops 1000000000 | bytes 1048576 | tf_op jit(solution)/shard_map/image/pallas_call | solution.py:330
  40.5 0.0 collective-permute-done.2.west_ref
  40.5 0.0 collective-permute-done.3.east_ref
  40.5 0.0 copy-done.2
  40.5 0.0 copy-start.3
  40.5 1.0 %closing.1 = (f32[2,64,1024]{2,1,0:T(8,128)S(1)}, f32[256,128]{1,0:T(8,128)S(1)}) custom-call(bf16[1024,1024]{1,0:T(8,128)(2,1)S(1)} %get-tuple-element.16.high_ref, bf16[1024,1024]{1,0:T(8,128)(2,1)S(1)} %get-tuple-element.17.low_ref, f32[2,64,1024]{2,1,0:T(8,128)S(1)} %image.1.own_ref, f32[9,1024]{1,0:T(8,128)S(1)} %collective-permute-done.2.west_ref, ...), custom_call_target="tpu_custom_call" | custom-call | flops 500000000 | bytes 1048576 | tf_op jit(solution)/shard_map/closing/pallas_call | solution.py:386
  41.5 25.9 %all_to_all.17 = f32[256,1,128]{2,1,0:T(1,128)S(1)} all-to-all(f32[256,1,128]{2,1,0:T(1,128)S(1)} %bitcast.25), channel_id=1, replica_groups=mesh['ens_0'=2,'ens_1'=4,'lon_0'=8,'lon_1'=2,'lon_2'=2] {'ens_0','ens_1'..., dimensions={0} | all-to-all | bytes 262144 | tf_op jit(solution)/shard_map/all_to_all | solution.py:466
  67.5 0.0 copy-done.3
  67.5 1.4 %update.1 = (f32[2,64,1024]{2,1,0:T(8,128)}, f32[2,64,1024]{2,1,0:T(8,128)}, f32[2,64,1024]{2,1,0:T(8,128)}) custom-call(f32[256,128]{1,0:T(8,128)S(1)} %bitcast.24, f32[2,64,1024]{2,1,0:T(8,128)S(1)} %bitcast.23, f32[2,64,1024]{2,1,0:T(8,128)S(1)} %bitcast.22, f32[2,64,1024]{2,1,0:T(8,128)S(1)} %bitcast.17, f32[2,64,1024]{2,1,0:T(8,128)S(1)} %get-tuple-element.25.img_ref), custom_call_target="tpu_custom_call" | custom-call | flops 10000000 | bytes 1048576 | tf_op jit(solution)/shard_map/update/pallas_call | solution.py:429
Async XLA Ops:
  0.6 7.8 %copy-start.4 = (s32[4096]{0:T(1024)S(1)}, s32[4096]{0:T(1024)}, u32[]{:S(2)}) copy-start(s32[4096]{0:T(1024)} %param.14) | copy-start | bytes 49156
  0.6 7.8 %copy-start.5 = (s32[4096]{0:T(1024)S(1)}, s32[4096]{0:T(1024)}, u32[]{:S(2)}) copy-start(s32[4096]{0:T(1024)} %param.15) | copy-start | bytes 49156
  0.7 7.7 %copy-start.7 = (f32[2,1024]{1,0:T(2,128)S(1)}, f32[2,1024]{1,0:T(2,128)}, u32[]{:S(2)}) copy-start(f32[2,1024]{1,0:T(2,128)} %constant.2.clone.factor_ref) | copy-start | bytes 24580
  5.0 7.9 %collective-permute-start = (f32[9,1024]{1,0:T(8,128)S(1)}, f32[9,1024]{1,0:T(8,128)S(1)}, u32[]{:S(2)}, u32[]{:S(2)}) collective-permute-start(f32[9,1024]{1,0:T(8,128)S(1)} %get-tuple-element.19), channel_id=1, source_target_pairs={{0,1},{1,2},{2,3},{3,4},{4,5},{5,6},{6,7},{7,8},{8,9},{9,10},{10,1... | collective-permute-start | bytes 110600 | tf_op jit(solution)/shard_map/ppermute | solution.py:443
  7.8 5.2 %collective-permute-start.1 = (f32[9,1024]{1,0:T(8,128)S(1)}, f32[9,1024]{1,0:T(8,128)S(1)}, u32[]{:S(2)}, u32[]{:S(2)}) collective-permute-start(f32[9,1024]{1,0:T(8,128)S(1)} %get-tuple-element.20), channel_id=1, source_target_pairs={{1,0},{2,1},{3,2},{4,3},{5,4},{6,5},{7,6},{8,7},{9,8},{10,9},{11,1... | collective-permute-start | bytes 110600 | tf_op jit(solution)/shard_map/ppermute | solution.py:444
  12.9 15.1 %copy-start.6 = (f32[4096]{0:T(1024)S(1)}, f32[4096]{0:T(1024)}, u32[]{:S(2)}) copy-start(f32[4096]{0:T(1024)} %param.16) | copy-start | bytes 49156
  28.0 11.4 %copy-start = (f32[2,1024,64]{1,2,0:T(8,128)S(1)}, f32[2,1024,64]{1,2,0:T(8,128)}, u32[]{:S(2)}) copy-start(f32[2,1024,64]{1,2,0:T(8,128)} %param.11) | copy-start | bytes 1572868
  28.0 11.4 %copy-start.1 = (bf16[2,3,1024,64]{2,3,1,0:T(8,128)(2,1)S(1)}, bf16[2,3,1024,64]{2,3,1,0:T(8,128)(2,1)}, u32[]{:S(2)}) copy-start(bf16[2,3,1024,64]{2,3,1,0:T(8,128)(2,1)} %param.12) | copy-start | bytes 2359300
  32.7 7.8 %collective-permute-start.2 = (f32[9,1024]{1,0:T(8,128)S(1)}, f32[9,1024]{1,0:T(8,128)S(1)}, u32[]{:S(2)}, u32[]{:S(2)}) collective-permute-start(f32[9,1024]{1,0:T(8,128)S(1)} %get-tuple-element.22), channel_id=1, source_target_pairs={{0,1},{1,2},{2,3},{3,4},{4,5},{5,6},{6,7},{7,8},{8,9},{9,10},{10,1... | collective-permute-start | bytes 110600 | tf_op jit(solution)/shard_map/ppermute | solution.py:443
  35.3 5.2 %collective-permute-start.3 = (f32[9,1024]{1,0:T(8,128)S(1)}, f32[9,1024]{1,0:T(8,128)S(1)}, u32[]{:S(2)}, u32[]{:S(2)}) collective-permute-start(f32[9,1024]{1,0:T(8,128)S(1)} %get-tuple-element.23), channel_id=1, source_target_pairs={{1,0},{2,1},{3,2},{4,3},{5,4},{6,5},{7,6},{8,7},{9,8},{10,9},{11,1... | collective-permute-start | bytes 110600 | tf_op jit(solution)/shard_map/ppermute | solution.py:444
  39.5 1.0 %copy-start.2 = (f32[2,1024,64]{1,2,0:T(8,128)S(1)}, f32[2,1024,64]{1,2,0:T(8,128)}, u32[]{:S(2)}) copy-start(f32[2,1024,64]{1,2,0:T(8,128)} %param.10) | copy-start | bytes 1572868
  40.5 26.9 %copy-start.3 = (f32[2,1024,64]{1,2,0:T(8,128)S(1)}, f32[2,1024,64]{1,2,0:T(8,128)}, u32[]{:S(2)}) copy-start(f32[2,1024,64]{1,2,0:T(8,128)} %param.9) | copy-start | bytes 1572868

commit v3 on v2

--- a/solution.py
+++ b/solution.py
@@ -1,5 +1,3 @@
-import functools
-
 import jax
 import jax.numpy as jnp
 import numpy as np
@@ -87,8 +85,12 @@
 
 
 def one_hot_rows(row, rows):
-    ids = lax.broadcasted_iota(jnp.int32, (rows, row.shape[1]), 0)
-    return (ids == row).astype(F32).astype(BF16)
+    ids = lax.broadcasted_iota(jnp.int16, (rows, row.shape[1]), 0)
+    return jnp.where(ids == row.astype(jnp.int16), jnp.ones((), BF16), jnp.zeros((), BF16))
+
+
+def on_odd_tile():
+    return lax.axis_index("lon_2") == 1
 
 
 def edges_of(field):
@@ -96,7 +98,7 @@
 
 
 def increment_kernel(
-    loc_hbm, dir_hbm, pert_hbm, inc_ref, left_ref, right_ref, high_ref, low_ref,
+    loc_hbm, dir_hbm, pert_hbm, inc_ref, inner_ref, outer_ref, high_ref, low_ref,
     loc_ref, dir_ref, pert_ref, parts_ref, sems,
 ):
     members, cols, rows = dir_ref.shape
@@ -104,41 +106,46 @@
     block = 256
     blocks = rows // block
     first = pltpu.make_async_copy(dir_hbm, dir_ref, sems.at[0])
+    second = pltpu.make_async_copy(pert_hbm, pert_ref, sems.at[1])
+    places = [slice(i * block, (i + 1) * block) for i in range(blocks)]
+    copies = [
+        pltpu.make_async_copy(loc_hbm.at[here], loc_ref.at[here], sems.at[2 + i])
+        for i, here in enumerate(places)
+    ]
+    odd = on_odd_tile()
     first.start()
-    copies = []
-    for i in range(blocks):
-        here = slice(i * block, (i + 1) * block)
-        copies.append(
-            pltpu.make_async_copy(loc_hbm.at[here], loc_ref.at[here], sems.at[2 + i])
-        )
     copies[0].start()
-    second = pltpu.make_async_copy(pert_hbm, pert_ref, sems.at[1])
-    second.start()
-    for copy in copies[1:]:
-        copy.start()
+    copies[1].start()
     first.wait()
+    copies[2].start()
     high, low = split_two(dir_ref[...].reshape(lines, rows))
     parts_ref[0:lines] = high
     parts_ref[lines : 2 * lines] = low
-    for i in range(blocks):
-        here = slice(i * block, (i + 1) * block)
-        copies[i].wait()
-        loc_high, loc_low = split_two(loc_ref[here])
-        high_ref[here] = loc_high
-        low_ref[here] = loc_low
-        both = dot(parts_ref[...], loc_high, NT)
-        rest = dot(parts_ref[0:lines], loc_low, NT)
+    for i in range(blocks + 1):
+        if i < blocks:
+            copies[i].wait()
+            if i == 0:
+                second.start()
+                for copy in copies[3:]:
+                    copy.start()
+            high_ref[places[i]], low_ref[places[i]] = split_two(loc_ref[places[i]])
+        if i == 0:
+            continue
+        if i == 1:
+            second.wait()
+        here = places[i - 1]
+        both = dot(parts_ref[...], high_ref[here], NT)
+        rest = dot(parts_ref[0:lines], low_ref[here], NT)
         localized = both[0:lines] + both[lines : 2 * lines] + rest
-        if i == 0:
-            second.wait()
         for field in range(3):
             total = None
             for m in range(members):
                 term = pert_ref[m, field, :, here].astype(F32) * localized[m * cols : (m + 1) * cols]
                 total = term if total is None else total + term
             inc_ref[field, :, here] = total
-            left_ref[edges_of(field), here] = total[0:HALO]
-            right_ref[edges_of(field), here] = total[cols - HALO : cols]
+            west, east = total[0:HALO], total[cols - HALO : cols]
+            inner_ref[edges_of(field), here] = jnp.where(odd, west, east)
+            outer_ref[edges_of(field), here] = jnp.where(odd, east, west)
 
 
 def partial_increment(localize, direction, pert):
@@ -160,101 +167,104 @@
     )(*(pltpu.with_memory_space_constraint(x, pltpu.HBM) for x in (localize, direction, pert)))
 
 
+def forward_steps(state_ref, factor_ref, parts_ref, places):
+    metric = factor_ref[0:1]
+    coriolis = factor_ref[1:2]
+    count = sum(stop - start for start, stop in places)
+    for moment in range(STEPS):
+        h, u, v = model_step(state_ref[0], state_ref[1], state_ref[2], 1.0, metric, coriolis)
+        if moment + 1 < STEPS:
+            state_ref[0] = h
+            state_ref[1] = u
+            state_ref[2] = v
+        line = moment * count
+        for start, stop in places:
+            high, low = split_two(h[start:stop])
+            parts_ref[line : line + stop - start] = high
+            parts_ref[STEPS * count + line : STEPS * count + line + stop - start] = low
+            line += stop - start
+
+
+def sampled(parts_ref, row, spot, rows):
+    spots = parts_ref.shape[0] // 2
+    picked = dot(parts_ref[...], one_hot_rows(row, rows), NN)
+    picked = picked[0:spots] + picked[spots : 2 * spots]
+    spot_hot = lax.broadcasted_iota(jnp.int32, picked.shape, 0) == spot
+    return jnp.sum(jnp.where(spot_hot, picked, 0.0), axis=0, keepdims=True)
+
+
 def forward_kernel(inc_ref, factor_ref, cell_ref, slot_ref, out_ref, state_ref, parts_ref):
     _, cols, rows = inc_ref.shape
     nobs = cell_ref.shape[1]
-    state_ref[...] = jnp.zeros(state_ref.shape, F32)
-    for field in range(3):
-        state_ref[field, PAD : PAD + cols] = inc_ref[field]
-    metric = factor_ref[0:1]
-    coriolis = factor_ref[1:2]
-    spots = STEPS * cols
-    for moment in range(STEPS):
-        h, u, v = model_step(state_ref[0], state_ref[1], state_ref[2], 1.0, metric, coriolis)
-        state_ref[0] = h
-        state_ref[1] = u
-        state_ref[2] = v
-        high, low = split_two(h[PAD : PAD + cols])
-        parts_ref[moment * cols : (moment + 1) * cols] = high
-        parts_ref[spots + moment * cols : spots + (moment + 1) * cols] = low
+    state_ref[...] = inc_ref[...]
+    forward_steps(state_ref, factor_ref, parts_ref, ((PAD, cols - PAD),))
     chunk = 512
     for start in range(0, nobs, chunk):
         here = slice(start, start + chunk)
         row, slot, col = rows_and_spots(cell_ref[:, here], slot_ref[:, here], cols)
-        picked = dot(parts_ref[...], one_hot_rows(row, rows), NN)
-        picked = picked[0:spots] + picked[spots : 2 * spots]
-        spot_hot = lax.broadcasted_iota(jnp.int32, (spots, chunk), 0) == slot * cols + col
-        out_ref[:, here] = jnp.sum(jnp.where(spot_hot, picked, 0.0), axis=0, keepdims=True)
-
-
-def own_observed(inc, factors, cell, slot):
+        within = (col >= PAD) & (col < cols - PAD)
+        spot = jnp.where(within, slot * (cols - 2 * PAD) + (col - PAD), -1)
+        out_ref[:, here] = sampled(parts_ref, row, spot, rows)
+
+
+def inner_observed(inc, factors, cell, slot):
     _, cols, rows = inc.shape
     return call(
         forward_kernel,
         "forward",
         floats(1, cell.shape[1]),
         [
-            pltpu.VMEM((3, cols + 2 * PAD, rows), F32),
-            pltpu.VMEM((2 * STEPS * cols, rows), BF16),
+            pltpu.VMEM((3, cols, rows), F32),
+            pltpu.VMEM((2 * STEPS * (cols - 2 * PAD), rows), BF16),
         ],
         4 * 10**9,
     )(inc, factors, cell, slot)
 
 
 def border_kernel(
-    own_ref, west_ref, east_ref, factor_ref, cell_ref, slot_ref, out_ref, state_ref, parts_ref,
-    *, cols,
+    seen_ref, inc_ref, inner_ref, outer_ref, factor_ref, cell_ref, slot_ref, out_ref,
+    state_ref, parts_ref,
 ):
-    rows = west_ref.shape[1]
+    _, cols, rows = inc_ref.shape
     nobs = cell_ref.shape[1]
+    odd = on_odd_tile()
     state_ref[...] = jnp.zeros(state_ref.shape, F32)
     for field in range(3):
-        state_ref[field, PAD - HALO : PAD] = west_ref[edges_of(field)]
-        state_ref[field, 3 * PAD : 3 * PAD + HALO] = east_ref[edges_of(field)]
-    metric = factor_ref[0:1]
-    coriolis = factor_ref[1:2]
+        inner, outer = inner_ref[edges_of(field)], outer_ref[edges_of(field)]
+        state_ref[field, PAD - HALO : PAD] = jnp.where(odd, inner, outer)
+        state_ref[field, PAD : 3 * PAD] = inc_ref[field, 0 : 2 * PAD]
+        state_ref[field, 3 * PAD : 5 * PAD] = inc_ref[field, cols - 2 * PAD : cols]
+        state_ref[field, 5 * PAD : 5 * PAD + HALO] = jnp.where(odd, outer, inner)
+    forward_steps(state_ref, factor_ref, parts_ref, ((PAD, 2 * PAD), (4 * PAD, 5 * PAD)))
     near = 2 * PAD
-    spots = STEPS * near
-    for moment in range(STEPS):
-        h, u, v = model_step(state_ref[0], state_ref[1], state_ref[2], 1.0, metric, coriolis)
-        state_ref[0] = h
-        state_ref[1] = u
-        state_ref[2] = v
-        high, low = split_two(h[PAD : 3 * PAD])
-        parts_ref[moment * near : (moment + 1) * near] = high
-        parts_ref[spots + moment * near : spots + (moment + 1) * near] = low
     chunk = 512
     for start in range(0, nobs, chunk):
         here = slice(start, start + chunk)
         row, slot, col = rows_and_spots(cell_ref[:, here], slot_ref[:, here], cols)
-        picked = dot(parts_ref[...], one_hot_rows(row, rows), NN)
-        picked = picked[0:spots] + picked[spots : 2 * spots]
         east_spot = jnp.where(col >= cols - PAD, slot * near + (col - cols + near), -1)
         spot = jnp.where(col < PAD, slot * near + col, east_spot)
-        spot_hot = lax.broadcasted_iota(jnp.int32, (spots, chunk), 0) == spot
-        value = jnp.sum(jnp.where(spot_hot, picked, 0.0), axis=0, keepdims=True)
-        value = value + own_ref[:, here]
+        value = sampled(parts_ref, row, spot, rows) + seen_ref[:, here]
         for i in range(0, chunk, 128):
             line = (start + i) // 128
             out_ref[:, line, :] = jnp.broadcast_to(value[:, i : i + 128], (out_ref.shape[0], 128))
 
 
-def observed_parts(own, west, east, factors, cell, slot, cols, copies):
-    rows = west.shape[1]
-    return call(
-        functools.partial(border_kernel, cols=cols),
+def observed_parts(seen, inc, inner, outer, factors, cell, slot, copies):
+    rows = inc.shape[2]
+    return call(
+        border_kernel,
         "border",
         floats(copies, cell.shape[1] // 128, 128),
         [
-            pltpu.VMEM((3, 4 * PAD, rows), F32),
+            pltpu.VMEM((3, 6 * PAD, rows), F32),
             pltpu.VMEM((4 * STEPS * PAD, rows), BF16),
         ],
         10**9,
-    )(own, west, east, factors, cell, slot)
+    )(seen, inc, inner, outer, factors, cell, slot)
 
 
 def adjoint_kernel(
-    seen_ref, weight_ref, cell_ref, slot_ref, factor_ref, adj_ref, left_ref, right_ref,
+    seen_ref, weight_ref, cell_ref, slot_ref, factor_ref, adj_ref, inner_ref, outer_ref,
     state_ref, force_ref,
 ):
     _, cols, rows = adj_ref.shape
@@ -285,10 +295,13 @@
         state_ref[0] = h
         state_ref[1] = u
         state_ref[2] = v
+    odd = on_odd_tile()
     for field in range(3):
         adj_ref[field] = state_ref[field, PAD : PAD + cols]
-        left_ref[edges_of(field)] = state_ref[field, PAD - HALO : PAD]
-        right_ref[edges_of(field)] = state_ref[field, PAD + cols : PAD + cols + HALO]
+        west = state_ref[field, PAD - HALO : PAD]
+        east = state_ref[field, PAD + cols : PAD + cols + HALO]
+        inner_ref[edges_of(field)] = jnp.where(odd, west, east)
+        outer_ref[edges_of(field)] = jnp.where(odd, east, west)
 
 
 def tile_adjoint(seen, weight, cell, slot, factors, cols):
@@ -337,16 +350,18 @@
 
 
 def closing_kernel(
-    high_ref, low_ref, own_ref, west_ref, east_ref, pert_ref, dir_ref, res_ref, img_ref, sums_ref,
+    high_ref, low_ref, own_ref, inner_ref, outer_ref, pert_ref, dir_ref, res_ref, img_ref, sums_ref,
     edge_ref, parts_ref,
 ):
     members, cols, rows = dir_ref.shape
     near = 2 * PAD
     lines = members * near
+    odd = on_odd_tile()
     edge_ref[...] = jnp.zeros(edge_ref.shape, F32)
     for field in range(3):
-        edge_ref[field, 0:HALO] = west_ref[edges_of(field)]
-        edge_ref[field, near - HALO : near] = east_ref[edges_of(field)]
+        inner, outer = inner_ref[edges_of(field)], outer_ref[edges_of(field)]
+        edge_ref[field, 0:HALO] = jnp.where(odd, inner, outer)
+        edge_ref[field, near - HALO : near] = jnp.where(odd, outer, inner)
     for m in range(members):
         west = jnp.zeros((PAD, rows), F32)
         east = jnp.zeros((PAD, rows), F32)
@@ -381,7 +396,7 @@
     sums_ref[...] = jnp.broadcast_to(packed, sums_ref.shape)
 
 
-def image_and_sums(high, low, own, west, east, pert, direction, residual, copies):
+def image_and_sums(high, low, own, inner, outer, pert, direction, residual, copies):
     members, cols, rows = direction.shape
     return call(
         closing_kernel,
@@ -392,7 +407,7 @@
             pltpu.VMEM((4 * members * PAD, rows), BF16),
         ],
         5 * 10**8,
-    )(high, low, own, west, east, pert, direction, residual)
+    )(high, low, own, inner, outer, pert, direction, residual)
 
 
 def update_kernel(
@@ -436,13 +451,12 @@
     )(sums, control, residual, direction, image)
 
 
-def neighbours(to_west, to_east):
+def swapped(inner, outer):
     count = lax.axis_size(LON)
-    east = [(i, (i + 1) % count) for i in range(count)]
-    west = [(target, source) for source, target in east]
-    from_west = lax.ppermute(to_east, LON, east)
-    from_east = lax.ppermute(to_west, LON, west)
-    return from_west, from_east
+    inner_pairs = [(i, i ^ 1) for i in range(count)]
+    outer_pairs = [(i, ((i + 1) ^ 1) - 1) for i in range(count)]
+    outer_pairs = [(source, target % count) for source, target in outer_pairs]
+    return lax.ppermute(inner, LON, inner_pairs), lax.ppermute(outer, LON, outer_pairs)
 
 
 def body(control, residual, direction, ens_perturb, localize, obs_cell, obs_slot, obs_weight):
@@ -452,16 +466,16 @@
     control_t, residual_t, direction_t = turned(control), turned(residual), turned(direction)
     pert = jnp.swapaxes(ens_perturb, 2, 3)
     cell, slot, weight = obs_cell[None], obs_slot[None], obs_weight[None]
-    inc, left, right, high, low = partial_increment(localize, direction_t, pert)
-    west, east = neighbours(left, right)
-    own = own_observed(inc, factors, cell, slot)
-    seen = observed_parts(own, west, east, factors, cell, slot, cols, lax.axis_size(ENS))
+    inc, inner, outer, high, low = partial_increment(localize, direction_t, pert)
+    inner, outer = swapped(inner, outer)
+    seen = inner_observed(inc, factors, cell, slot)
+    seen = observed_parts(seen, inc, inner, outer, factors, cell, slot, lax.axis_size(ENS))
     seen = lax.all_to_all(seen, ENS, 0, 0, tiled=True)
-    adj, left, right = tile_adjoint(seen, weight, cell, slot, factors, cols)
-    west, east = neighbours(left, right)
+    adj, inner, outer = tile_adjoint(seen, weight, cell, slot, factors, cols)
+    inner, outer = swapped(inner, outer)
     image = own_image(high, low, adj, pert, direction_t)
     image, sums = image_and_sums(
-        high, low, image, west, east, pert, direction_t, residual_t, lax.axis_size(ENS_LON)
+        high, low, image, inner, outer, pert, direction_t, residual_t, lax.axis_size(ENS_LON)
     )
     sums = lax.all_to_all(sums, ENS_LON, 0, 0, tiled=True)
     results = updated(sums, control_t, residual_t, direction_t, image)

time: 69.2 us -> 66.1 us (0.955)
  blocking collectives: 38.4 us -> 33.1 us
  waiting for transfers between devices: 0.01 us -> 2.98 us
  Pallas kernels: 19.5 us -> 18.4 us
    all_to_all x1, blocking collectives: 25.9 us -> 20.8 us  [body(): sums = lax.all_to_all(sums, ENS_LON, 0, 0, tiled=True)]
    ppermute x4, waiting for transfers between devices: 0.01 us -> 2.98 us  [the longest x2 2.97 us: swapped(): lax.ppermute(outer, LON, outer_pairs)]
    pallas_call x2, Pallas kernels: 7.11 us -> 5.27 us  [the longest x1 3.32 us: inner_observed(): call(forward_kernel, 'forward', floats(1, cell.shape[1]), [pltpu.VMEM((3,...]
    pallas_call x1, Pallas kernels: 4.35 us -> 5.17 us  [partial_increment(): call(increment_kernel, 'increment', [floats(3, cols, rows), floats(3 * HA...]
  transfers between devices with their start and end apart: 4 -> 4, of which waited for: 0 -> 2; matrix products, arithmetic and copies ran while one was open for 0% -> 0% of each run, Pallas kernels for 8% -> 7%
where the time goes in v3:
time: 66.1 us; the launch traced here: 65.9 us
  blocking collectives  33.1 us (50%)
  Pallas kernels  18.4 us (28%)
  starting transfers between devices  10.5 us (16%)
  waiting for transfers between devices  2.98 us (5%)
  between operations  0.91 us (1%)
    all_to_all x1, blocking collectives, body(): sums = lax.all_to_all(sums, ENS_LON, 0, 0, tiled=True)  20.8 us
    all_to_all x1, blocking collectives, body(): seen = lax.all_to_all(seen, ENS, 0, 0, tiled=True)  12.3 us
    ppermute x2, starting transfers between devices, swapped(): lax.ppermute(inner, LON, inner_pairs)  10.5 us
    pallas_call x1, Pallas kernels, partial_increment(): call(increment_kernel, 'increment', [floats(3, cols, rows), floats(3 * HA...  5.17 us
    pallas_call x1, Pallas kernels, tile_adjoint(): call(adjoint_kernel, 'adjoint', [floats(3, cols, rows), floats(3 * HALO,...  4.51 us
    pallas_call x1, Pallas kernels, inner_observed(): call(forward_kernel, 'forward', floats(1, cell.shape[1]), [pltpu.VMEM((3,...  3.32 us
    ppermute x2, waiting for transfers between devices, swapped(): lax.ppermute(outer, LON, outer_pairs)  2.97 us
    pallas_call x1, Pallas kernels, observed_parts(): call(border_kernel, 'border', floats(copies, cell.shape[1] // 128, 128),...  1.95 us
  transfers between devices with their start and end apart: 4, of which 2 were waited for; matrix products, arithmetic and copies ran while one was open for 0% of the time, Pallas kernels for 7%

profile of v3, /device:TPU:1, one launch (start us, length us, event | category | flops | bytes accessed | tf_op | source)
XLA Modules:
  0.0 65.9 jit_solution(2750944424979429169)
XLA Ops:
  0.6 0.0 copy-start.4
  0.6 0.0 copy-start.5
  0.7 0.0 copy-start.7
  0.7 5.2 %increment.1 = (f32[3,64,1024]{2,1,0:T(8,128)S(1)}, f32[9,1024]{1,0:T(8,128)S(1)}, f32[9,1024]{1,0:T(8,128)S(1)}, bf16[1024,1024]{1,0:T(8,128)(2,1)S(1)}, bf16[1024,1024]{1,0:T(8,128)(2,1)S(1)}) custom-call(f32[1024,1024]{1,0:T(8,128)} %loc_hbm.1, f32[2,64,1024]{2,1,0:T(8,128)} %bitcast.14, bf16[2,3,64,1024]{3,2,1,0:T(8,128)(2,1)} %bitcast.18), custom_call_target="tpu_custom_call" | custom-call | flops 1000000000 | bytes 1048576 | tf_op jit(solution)/shard_map/increment/pallas_call | solution.py:154
  5.8 3.3 %collective-permute-start = (f32[9,1024]{1,0:T(8,128)S(1)}, f32[9,1024]{1,0:T(8,128)S(1)}, u32[]{:S(2)}, u32[]{:S(2)}) collective-permute-start(f32[9,1024]{1,0:T(8,128)S(1)} %get-tuple-element.19), channel_id=1, source_target_pairs={{0,1},{1,0},{2,3},{3,2},{4,5},{5,4},{6,7},{7,6},{8,9},{9,8},{10,11... | collective-permute-start | bytes 110600 | tf_op jit(solution)/shard_map/ppermute | solution.py:459
  9.1 0.0 collective-permute-start.1
  9.1 0.0 copy-done.4
  9.1 0.0 copy-done.5
  9.1 0.0 copy-done.7
  9.2 3.3 %forward.1.seen_ref = f32[1,4096]{1,0:T(1,128)S(1)} custom-call(f32[3,64,1024]{2,1,0:T(8,128)S(1)} %get-tuple-element.18.inc_ref, f32[2,1024]{1,0:T(2,128)S(1)} %copy-done.7, s32[1,4096]{1,0:T(1,128)S(1)} %bitcast.26, s32[1,4096]{1,0:T(1,128)S(1)} %bitcast.29), custom_call_target="tpu_custom_call" | custom-call | flops 4000000000 | bytes 1048576 | tf_op jit(solution)/shard_map/forward/pallas_call | solution.py:212
  12.5 0.0 copy-start.6
  12.5 0.0 collective-permute-done.inner_ref
  12.5 0.3 collective-permute-done.1.outer_ref
  12.8 1.9 %border.1 = f32[8,32,128]{2,1,0:T(8,128)S(1)} custom-call(f32[1,4096]{1,0:T(1,128)S(1)} %forward.1.seen_ref, f32[3,64,1024]{2,1,0:T(8,128)S(1)} %get-tuple-element.18.inc_ref, f32[9,1024]{1,0:T(8,128)S(1)} %collective-permute-done.inner_ref, f32[9,1024]{1,0:T(8,128)S(1)} %collective-permute-done.1.outer_ref, f32[2,1024]{1,0:T(2,128)S(1)} %copy-done.7, ...), custom_call_target="tpu_custom_call" | custom-call | flops 1000000000 | bytes 1048576 | tf_op jit(solution)/shard_map/border/pallas_call | solution.py:254
  14.8 12.3 %all_to_all.16.seen_ref = f32[8,32,128]{2,1,0:T(8,128)S(1)} all-to-all(f32[8,32,128]{2,1,0:T(8,128)S(1)} %border.1), channel_id=1, replica_groups=mesh['ens_0'=2,'ens_1'=4,'lon_0'=8,'lon_1'=2,'lon_2'=2] {'ens_0','ens_1'}, dimensions={0} | all-to-all | bytes 262144 | tf_op jit(solution)/shard_map/all_to_all | solution.py:473
  27.1 0.0 copy-done.6
  27.1 0.0 copy-start
  27.1 0.0 copy-start.1
  27.1 4.5 %adjoint.1 = (f32[3,64,1024]{2,1,0:T(8,128)S(1)}, f32[9,1024]{1,0:T(8,128)S(1)}, f32[9,1024]{1,0:T(8,128)S(1)}) custom-call(f32[8,32,128]{2,1,0:T(8,128)S(1)} %all_to_all.16.seen_ref, f32[1,4096]{1,0:T(1,128)S(1)} %bitcast.32, s32[1,4096]{1,0:T(1,128)S(1)} %bitcast.28, s32[1,4096]{1,0:T(1,128)S(1)} %bitcast.31, f32[2,1024]{1,0:T(2,128)S(1)} %copy-done.7), custom_call_target="tpu_custom_call" | custom-call | flops 4000000000 | bytes 1048576 | tf_op jit(solution)/shard_map/adjoint/pallas_call | solution.py:309
  31.6 7.2 %collective-permute-start.2 = (f32[9,1024]{1,0:T(8,128)S(1)}, f32[9,1024]{1,0:T(8,128)S(1)}, u32[]{:S(2)}, u32[]{:S(2)}) collective-permute-start(f32[9,1024]{1,0:T(8,128)S(1)} %get-tuple-element.22), channel_id=1, source_target_pairs={{0,1},{1,0},{2,3},{3,2},{4,5},{5,4},{6,7},{7,6},{8,9},{9,8},{10,11... | collective-permute-start | bytes 110600 | tf_op jit(solution)/shard_map/ppermute | solution.py:459
  38.9 0.0 collective-permute-start.3
  38.9 0.0 copy-done
  38.9 0.0 copy-done.1
  38.9 0.0 copy-start.2
  38.9 1.0 %image.1.own_ref = f32[2,64,1024]{2,1,0:T(8,128)S(1)} custom-call(bf16[1024,1024]{1,0:T(8,128)(2,1)S(1)} %get-tuple-element.16.high_ref, bf16[1024,1024]{1,0:T(8,128)(2,1)S(1)} %get-tuple-element.17.low_ref, f32[3,64,1024]{2,1,0:T(8,128)S(1)} %get-tuple-element.21.adj_ref, bf16[2,3,64,1024]{3,2,1,0:T(8,128)(2,1)S(1)} %bitcast.19, f32[2,64,1024]{2,1,0:T(8,128)S(1)} %bitcast.15), custom_call_target="tpu_custom_call" | custom-call | flops 1000000000 | bytes 1048576 | tf_op jit(solution)/shard_map/image/pallas_call | solution.py:343
  39.9 0.0 collective-permute-done.2.inner_ref
  39.9 2.7 %collective-permute-done.3.outer_ref = f32[9,1024]{1,0:T(8,128)S(1)} collective-permute-done((f32[9,1024]{1,0:T(8,128)S(1)}, f32[9,1024]{1,0:T(8,128)S(1)}, u32[]{:S(2)}, u32[]{:S(2)}) %collective-permute-start.3) | collective-permute-done | bytes 36896 | tf_op jit(solution)/shard_map/ppermute | solution.py:459
  42.6 0.0 copy-done.2
  42.6 0.0 copy-start.3
  42.6 1.0 %closing.1 = (f32[2,64,1024]{2,1,0:T(8,128)S(1)}, f32[256,128]{1,0:T(8,128)S(1)}) custom-call(bf16[1024,1024]{1,0:T(8,128)(2,1)S(1)} %get-tuple-element.16.high_ref, bf16[1024,1024]{1,0:T(8,128)(2,1)S(1)} %get-tuple-element.17.low_ref, f32[2,64,1024]{2,1,0:T(8,128)S(1)} %image.1.own_ref, f32[9,1024]{1,0:T(8,128)S(1)} %collective-permute-done.2.inner_ref, ...), custom_call_target="tpu_custom_call" | custom-call | flops 500000000 | bytes 1048576 | tf_op jit(solution)/shard_map/closing/pallas_call | solution.py:401
  43.6 20.8 %all_to_all.17 = f32[256,1,128]{2,1,0:T(1,128)S(1)} all-to-all(f32[256,1,128]{2,1,0:T(1,128)S(1)} %bitcast.25), channel_id=1, replica_groups=mesh['ens_0'=2,'ens_1'=4,'lon_0'=8,'lon_1'=2,'lon_2'=2] {'ens_0','ens_1'..., dimensions={0} | all-to-all | bytes 262144 | tf_op jit(solution)/shard_map/all_to_all | solution.py:480
  64.3 0.0 copy-done.3
  64.3 1.4 %update.1 = (f32[2,64,1024]{2,1,0:T(8,128)}, f32[2,64,1024]{2,1,0:T(8,128)}, f32[2,64,1024]{2,1,0:T(8,128)}) custom-call(f32[256,128]{1,0:T(8,128)S(1)} %bitcast.24, f32[2,64,1024]{2,1,0:T(8,128)S(1)} %bitcast.23, f32[2,64,1024]{2,1,0:T(8,128)S(1)} %bitcast.22, f32[2,64,1024]{2,1,0:T(8,128)S(1)} %bitcast.17, f32[2,64,1024]{2,1,0:T(8,128)S(1)} %get-tuple-element.25.img_ref), custom_call_target="tpu_custom_call" | custom-call | flops 10000000 | bytes 1048576 | tf_op jit(solution)/shard_map/update/pallas_call | solution.py:444
Async XLA Ops:
  0.6 8.5 %copy-start.4 = (s32[4096]{0:T(1024)S(1)}, s32[4096]{0:T(1024)}, u32[]{:S(2)}) copy-start(s32[4096]{0:T(1024)} %param.14) | copy-start | bytes 49156
  0.6 8.5 %copy-start.5 = (s32[4096]{0:T(1024)S(1)}, s32[4096]{0:T(1024)}, u32[]{:S(2)}) copy-start(s32[4096]{0:T(1024)} %param.15) | copy-start | bytes 49156
  0.7 8.5 %copy-start.7 = (f32[2,1024]{1,0:T(2,128)S(1)}, f32[2,1024]{1,0:T(2,128)}, u32[]{:S(2)}) copy-start(f32[2,1024]{1,0:T(2,128)} %constant.2.clone.factor_ref) | copy-start | bytes 24580
  5.8 6.7 %collective-permute-start = (f32[9,1024]{1,0:T(8,128)S(1)}, f32[9,1024]{1,0:T(8,128)S(1)}, u32[]{:S(2)}, u32[]{:S(2)}) collective-permute-start(f32[9,1024]{1,0:T(8,128)S(1)} %get-tuple-element.19), channel_id=1, source_target_pairs={{0,1},{1,0},{2,3},{3,2},{4,5},{5,4},{6,7},{7,6},{8,9},{9,8},{10,11... | collective-permute-start | bytes 110600 | tf_op jit(solution)/shard_map/ppermute | solution.py:459
  9.1 3.7 %collective-permute-start.1 = (f32[9,1024]{1,0:T(8,128)S(1)}, f32[9,1024]{1,0:T(8,128)S(1)}, u32[]{:S(2)}, u32[]{:S(2)}) collective-permute-start(f32[9,1024]{1,0:T(8,128)S(1)} %get-tuple-element.20), channel_id=1, source_target_pairs={{0,31},{1,2},{2,1},{3,4},{4,3},{5,6},{6,5},{7,8},{8,7},{9,10},{10,... | collective-permute-start | bytes 110600 | tf_op jit(solution)/shard_map/ppermute | solution.py:459
  12.5 14.6 %copy-start.6 = (f32[4096]{0:T(1024)S(1)}, f32[4096]{0:T(1024)}, u32[]{:S(2)}) copy-start(f32[4096]{0:T(1024)} %param.16) | copy-start | bytes 49156
  27.1 11.8 %copy-start = (f32[2,1024,64]{1,2,0:T(8,128)S(1)}, f32[2,1024,64]{1,2,0:T(8,128)}, u32[]{:S(2)}) copy-start(f32[2,1024,64]{1,2,0:T(8,128)} %param.11) | copy-start | bytes 1572868
  27.1 11.8 %copy-start.1 = (bf16[2,3,1024,64]{2,3,1,0:T(8,128)(2,1)S(1)}, bf16[2,3,1024,64]{2,3,1,0:T(8,128)(2,1)}, u32[]{:S(2)}) copy-start(bf16[2,3,1024,64]{2,3,1,0:T(8,128)(2,1)} %param.12) | copy-start | bytes 2359300
  31.6 8.3 %collective-permute-start.2 = (f32[9,1024]{1,0:T(8,128)S(1)}, f32[9,1024]{1,0:T(8,128)S(1)}, u32[]{:S(2)}, u32[]{:S(2)}) collective-permute-start(f32[9,1024]{1,0:T(8,128)S(1)} %get-tuple-element.22), channel_id=1, source_target_pairs={{0,1},{1,0},{2,3},{3,2},{4,5},{5,4},{6,7},{7,6},{8,9},{9,8},{10,11... | collective-permute-start | bytes 110600 | tf_op jit(solution)/shard_map/ppermute | solution.py:459
  38.9 3.7 %collective-permute-start.3 = (f32[9,1024]{1,0:T(8,128)S(1)}, f32[9,1024]{1,0:T(8,128)S(1)}, u32[]{:S(2)}, u32[]{:S(2)}) collective-permute-start(f32[9,1024]{1,0:T(8,128)S(1)} %get-tuple-element.23), channel_id=1, source_target_pairs={{0,31},{1,2},{2,1},{3,4},{4,3},{5,6},{6,5},{7,8},{8,7},{9,10},{10,... | collective-permute-start | bytes 110600 | tf_op jit(solution)/shard_map/ppermute | solution.py:459
  38.9 3.7 %copy-start.2 = (f32[2,1024,64]{1,2,0:T(8,128)S(1)}, f32[2,1024,64]{1,2,0:T(8,128)}, u32[]{:S(2)}) copy-start(f32[2,1024,64]{1,2,0:T(8,128)} %param.10) | copy-start | bytes 1572868
  42.6 21.8 %copy-start.3 = (f32[2,1024,64]{1,2,0:T(8,128)S(1)}, f32[2,1024,64]{1,2,0:T(8,128)}, u32[]{:S(2)}) copy-start(f32[2,1024,64]{1,2,0:T(8,128)} %param.9) | copy-start | bytes 1572868

commit v4 on v3

--- a/solution.py
+++ b/solution.py
@@ -93,8 +93,21 @@
     return lax.axis_index("lon_2") == 1
 
 
-def edges_of(field):
-    return slice(HALO * field, HALO * (field + 1))
+def put_edge(ref, field, lanes, value):
+    for i in range(lanes // 128, lanes // 128 + value.shape[1] // 128):
+        line = 3 * HALO * i + HALO * field
+        at = i * 128 - lanes
+        ref[line : line + HALO] = value[:, at : at + 128]
+
+
+def get_edge(ref, field):
+    tiles = range(ref.shape[0] // (3 * HALO))
+    lines = [3 * HALO * i + HALO * field for i in tiles]
+    return jnp.concatenate([ref[line : line + HALO] for line in lines], axis=1)
+
+
+def edge_floats(rows):
+    return floats(3 * HALO * rows // 128, 128)
 
 
 def increment_kernel(
@@ -115,19 +128,16 @@
     odd = on_odd_tile()
     first.start()
     copies[0].start()
-    copies[1].start()
+    second.start()
+    for copy in copies[1:]:
+        copy.start()
     first.wait()
-    copies[2].start()
     high, low = split_two(dir_ref[...].reshape(lines, rows))
     parts_ref[0:lines] = high
     parts_ref[lines : 2 * lines] = low
     for i in range(blocks + 1):
         if i < blocks:
             copies[i].wait()
-            if i == 0:
-                second.start()
-                for copy in copies[3:]:
-                    copy.start()
             high_ref[places[i]], low_ref[places[i]] = split_two(loc_ref[places[i]])
         if i == 0:
             continue
@@ -144,8 +154,8 @@
                 total = term if total is None else total + term
             inc_ref[field, :, here] = total
             west, east = total[0:HALO], total[cols - HALO : cols]
-            inner_ref[edges_of(field), here] = jnp.where(odd, west, east)
-            outer_ref[edges_of(field), here] = jnp.where(odd, east, west)
+            put_edge(inner_ref, field, here.start, jnp.where(odd, west, east))
+            put_edge(outer_ref, field, here.start, jnp.where(odd, east, west))
 
 
 def partial_increment(localize, direction, pert):
@@ -154,7 +164,7 @@
     return call(
         increment_kernel,
         "increment",
-        [floats(3, cols, rows), floats(3 * HALO, rows), floats(3 * HALO, rows), half, half],
+        [floats(3, cols, rows), edge_floats(rows), edge_floats(rows), half, half],
         [
             pltpu.VMEM((rows, rows), F32),
             pltpu.VMEM(direction.shape, F32),
@@ -230,7 +240,7 @@
     odd = on_odd_tile()
     state_ref[...] = jnp.zeros(state_ref.shape, F32)
     for field in range(3):
-        inner, outer = inner_ref[edges_of(field)], outer_ref[edges_of(field)]
+        inner, outer = get_edge(inner_ref, field), get_edge(outer_ref, field)
         state_ref[field, PAD - HALO : PAD] = jnp.where(odd, inner, outer)
         state_ref[field, PAD : 3 * PAD] = inc_ref[field, 0 : 2 * PAD]
         state_ref[field, 3 * PAD : 5 * PAD] = inc_ref[field, cols - 2 * PAD : cols]
@@ -263,59 +273,121 @@
     )(seen, inc, inner, outer, factors, cell, slot)
 
 
-def adjoint_kernel(
-    seen_ref, weight_ref, cell_ref, slot_ref, factor_ref, adj_ref, inner_ref, outer_ref,
-    state_ref, force_ref,
-):
-    _, cols, rows = adj_ref.shape
-    nobs = cell_ref.shape[1]
-    spots = STEPS * cols
-    chunk = 512
-    seen = jnp.sum(seen_ref[...], axis=0)
-    for start in range(0, nobs, chunk):
-        here = slice(start, start + chunk)
-        row, slot, col = rows_and_spots(cell_ref[:, here], slot_ref[:, here], cols)
-        lines = range(start // 128, (start + chunk) // 128)
-        total = jnp.concatenate([seen[i : i + 1] for i in lines], axis=1)
-        weighted = weight_ref[:, here] * total
-        spot_hot = lax.broadcasted_iota(jnp.int32, (spots, chunk), 0) == slot * cols + col
-        high, low = split_two(jnp.where(spot_hot, weighted, 0.0))
-        part = dot(jnp.concatenate([high, low], axis=0), one_hot_rows(row, rows), NT)
-        part = part[0:spots] + part[spots : 2 * spots]
-        if start == 0:
-            force_ref[...] = part
-        else:
-            force_ref[...] += part
+def backward_steps(state_ref, factor_ref, add_force):
     metric = factor_ref[0:1]
     coriolis = factor_ref[1:2]
     state_ref[...] = jnp.zeros(state_ref.shape, F32)
     for moment in reversed(range(STEPS)):
-        state_ref[0, PAD : PAD + cols] += force_ref[moment * cols : (moment + 1) * cols]
+        add_force(moment)
         h, u, v = model_step(state_ref[0], state_ref[1], state_ref[2], -1.0, metric, coriolis)
         state_ref[0] = h
         state_ref[1] = u
         state_ref[2] = v
+
+
+def placed(spots, spot, weighted):
+    spot_hot = lax.broadcasted_iota(jnp.int32, (spots, spot.shape[1]), 0) == spot
+    return jnp.concatenate(split_two(jnp.where(spot_hot, weighted, 0.0)), axis=0)
+
+
+def gather_force(force_ref, part, start):
+    spots = force_ref.shape[0]
+    part = part[0:spots] + part[spots : 2 * spots]
+    if start == 0:
+        force_ref[...] = part
+    else:
+        force_ref[...] += part
+
+
+def edge_adjoint_kernel(
+    seen_ref, weight_ref, cell_ref, slot_ref, lines_ref, factor_ref,
+    weighted_ref, force_ref, inner_ref, outer_ref, state_ref, *, cols,
+):
+    rows = factor_ref.shape[1]
+    nobs = cell_ref.shape[1]
+    near = 2 * PAD
+    chunk = 512
+    seen = jnp.sum(seen_ref[...], axis=0)
+    upright = jnp.transpose(lax.shift_right_logical(lines_ref[...], cols.bit_length() - 1))
+    ids = lax.broadcasted_iota(jnp.int16, (128, rows), 1)
+    for start in range(0, nobs, chunk):
+        here = slice(start, start + chunk)
+        _, slot, col = rows_and_spots(cell_ref[:, here], slot_ref[:, here], cols)
+        lines = range(start // 128, (start + chunk) // 128)
+        weighted = weight_ref[:, here] * jnp.concatenate([seen[i : i + 1] for i in lines], axis=1)
+        weighted_ref[:, here] = weighted
+        east_spot = jnp.where(col >= cols - PAD, slot * near + (col - cols + near), -1)
+        spot = jnp.where(col < PAD, slot * near + col, east_spot)
+        hots = []
+        for i in lines:
+            row = jnp.broadcast_to(upright[:, i : i + 1], (128, 128)).astype(jnp.int16)
+            row = jnp.concatenate([row] * (rows // 128), axis=1)
+            hots.append(jnp.where(ids == row, jnp.ones((), BF16), jnp.zeros((), BF16)))
+        part = dot(placed(STEPS * near, spot, weighted), jnp.concatenate(hots, axis=0), NN)
+        gather_force(force_ref, part, start)
+
+    def add_force(moment):
+        state_ref[0, PAD : 3 * PAD] += force_ref[moment * near : (moment + 1) * near]
+
+    backward_steps(state_ref, factor_ref, add_force)
     odd = on_odd_tile()
     for field in range(3):
+        west = state_ref[field, PAD - HALO : PAD]
+        east = state_ref[field, 3 * PAD : 3 * PAD + HALO]
+        put_edge(inner_ref, field, 0, jnp.where(odd, west, east))
+        put_edge(outer_ref, field, 0, jnp.where(odd, east, west))
+
+
+def edge_adjoint(seen, weight, cell, slot, factors, cols):
+    rows = factors.shape[1]
+    nobs = cell.shape[1]
+    return call(
+        lambda *refs: edge_adjoint_kernel(*refs, cols=cols),
+        "edge_adjoint",
+        [floats(1, nobs), floats(2 * STEPS * PAD, rows), edge_floats(rows), edge_floats(rows)],
+        [pltpu.VMEM((3, 4 * PAD, rows), F32)],
+        10**9,
+    )(seen, weight, cell, slot, cell.reshape(nobs // 128, 128), factors)
+
+
+def adjoint_kernel(
+    weighted_ref, edge_ref, cell_ref, slot_ref, factor_ref, adj_ref, state_ref, force_ref
+):
+    _, cols, rows = adj_ref.shape
+    nobs = cell_ref.shape[1]
+    count = cols - 2 * PAD
+    chunk = 512
+    for start in range(0, nobs, chunk):
+        here = slice(start, start + chunk)
+        row, slot, col = rows_and_spots(cell_ref[:, here], slot_ref[:, here], cols)
+        within = (col >= PAD) & (col < cols - PAD)
+        spot = jnp.where(within, slot * count + (col - PAD), -1)
+        hot = placed(STEPS * count, spot, weighted_ref[:, here])
+        gather_force(force_ref, dot(hot, one_hot_rows(row, rows), NT), start)
+
+    def add_force(moment):
+        near = 2 * PAD * moment
+        state_ref[0, PAD : 2 * PAD] += edge_ref[near : near + PAD]
+        state_ref[0, 2 * PAD : cols] += force_ref[moment * count : (moment + 1) * count]
+        state_ref[0, cols : PAD + cols] += edge_ref[near + PAD : near + 2 * PAD]
+
+    backward_steps(state_ref, factor_ref, add_force)
+    for field in range(3):
         adj_ref[field] = state_ref[field, PAD : PAD + cols]
-        west = state_ref[field, PAD - HALO : PAD]
-        east = state_ref[field, PAD + cols : PAD + cols + HALO]
-        inner_ref[edges_of(field)] = jnp.where(odd, west, east)
-        outer_ref[edges_of(field)] = jnp.where(odd, east, west)
-
-
-def tile_adjoint(seen, weight, cell, slot, factors, cols):
+
+
+def tile_adjoint(weighted, edge, cell, slot, factors, cols):
     rows = factors.shape[1]
     return call(
         adjoint_kernel,
         "adjoint",
-        [floats(3, cols, rows), floats(3 * HALO, rows), floats(3 * HALO, rows)],
+        floats(3, cols, rows),
         [
             pltpu.VMEM((3, cols + 2 * PAD, rows), F32),
-            pltpu.VMEM((STEPS * cols, rows), F32),
+            pltpu.VMEM((STEPS * (cols - 2 * PAD), rows), F32),
         ],
         4 * 10**9,
-    )(seen, weight, cell, slot, factors)
+    )(weighted, edge, cell, slot, factors)
 
 
 def three_products(parts_ref, high_ref, low_ref, lines):
@@ -359,7 +431,7 @@
     odd = on_odd_tile()
     edge_ref[...] = jnp.zeros(edge_ref.shape, F32)
     for field in range(3):
-        inner, outer = inner_ref[edges_of(field)], outer_ref[edges_of(field)]
+        inner, outer = get_edge(inner_ref, field), get_edge(outer_ref, field)
         edge_ref[field, 0:HALO] = jnp.where(odd, inner, outer)
         edge_ref[field, near - HALO : near] = jnp.where(odd, outer, inner)
     for m in range(members):
@@ -471,8 +543,9 @@
     seen = inner_observed(inc, factors, cell, slot)
     seen = observed_parts(seen, inc, inner, outer, factors, cell, slot, lax.axis_size(ENS))
     seen = lax.all_to_all(seen, ENS, 0, 0, tiled=True)
-    adj, inner, outer = tile_adjoint(seen, weight, cell, slot, factors, cols)
+    weighted, edge, inner, outer = edge_adjoint(seen, weight, cell, slot, factors, cols)
     inner, outer = swapped(inner, outer)
+    adj = tile_adjoint(weighted, edge, cell, slot, factors, cols)
     image = own_image(high, low, adj, pert, direction_t)
     image, sums = image_and_sums(
         high, low, image, inner, outer, pert, direction_t, residual_t, lax.axis_size(ENS_LON)

time: 66.1 us -> 62.6 us (0.947)
  waiting for transfers between devices: 2.98 us -> 0.02 us
  blocking collectives: 33.1 us -> 32.1 us
    ppermute x2, waiting for transfers between devices: 2.97 us -> 0.01 us  [swapped(): lax.ppermute(outer, LON, outer_pairs)]
    all_to_all x1, blocking collectives: 20.8 us -> 19.5 us  [body(): sums = lax.all_to_all(sums, ENS_LON, 0, 0, tiled=True)]
    pallas_call x2 -> x3, Pallas kernels: 9.68 us -> 10.1 us  [the longest x1 4.61 us: partial_increment(): call(increment_kernel, 'increment', [floats(3, cols, rows), edge_floats(r...]
  transfers between devices with their start and end apart: 4 -> 4, of which waited for: 2 -> 0; matrix products, arithmetic and copies ran while one was open for 0% -> 0% of each run, Pallas kernels for 7% -> 13%
where the time goes in v4:
time: 62.6 us; the launch traced here: 62.4 us
  blocking collectives  32.1 us (51%)
  Pallas kernels  18.8 us (30%)
  starting transfers between devices  10.5 us (17%)
  between operations  0.96 us (2%)
    all_to_all x1, blocking collectives, body(): sums = lax.all_to_all(sums, ENS_LON, 0, 0, tiled=True)  19.5 us
    all_to_all x1, blocking collectives, body(): seen = lax.all_to_all(seen, ENS, 0, 0, tiled=True)  12.7 us
    ppermute x2, starting transfers between devices, swapped(): lax.ppermute(inner, LON, inner_pairs)  10.5 us
    pallas_call x1, Pallas kernels, partial_increment(): call(increment_kernel, 'increment', [floats(3, cols, rows), edge_floats(r...  4.61 us
    pallas_call x1, Pallas kernels, tile_adjoint(): call(adjoint_kernel, 'adjoint', floats(3, cols, rows), [pltpu.VMEM((3, co...  3.5 us
    pallas_call x1, Pallas kernels, inner_observed(): call(forward_kernel, 'forward', floats(1, cell.shape[1]), [pltpu.VMEM((3,...  3.33 us
    pallas_call x1, Pallas kernels, edge_adjoint(): call(lambda *refs: edge_adjoint_kernel(*refs, cols=cols), 'edge_adjoint',...  1.96 us
    pallas_call x1, Pallas kernels, observed_parts(): call(border_kernel, 'border', floats(copies, cell.shape[1] // 128, 128),...  1.94 us
  transfers between devices with their start and end apart: 4, of which 0 were waited for; matrix products, arithmetic and copies ran while one was open for 0% of the time, Pallas kernels for 13%

profile of v4, /device:TPU:1, one launch (start us, length us, event | category | flops | bytes accessed | tf_op | source)
XLA Modules:
  0.0 62.4 jit_solution(17355074162518850616)
XLA Ops:
  0.6 0.0 copy-start.5
  0.6 0.0 copy-start.6
  0.7 0.0 copy-start.7
  0.7 4.6 %increment.1 = (f32[3,64,1024]{2,1,0:T(8,128)S(1)}, f32[72,128]{1,0:T(8,128)S(1)}, f32[72,128]{1,0:T(8,128)S(1)}, bf16[1024,1024]{1,0:T(8,128)(2,1)S(1)}, bf16[1024,1024]{1,0:T(8,128)(2,1)S(1)}) custom-call(f32[1024,1024]{1,0:T(8,128)} %loc_hbm.1, f32[2,64,1024]{2,1,0:T(8,128)} %bitcast.15, bf16[2,3,64,1024]{3,2,1,0:T(8,128)(2,1)} %bitcast.19), custom_call_target="tpu_custom_call" | custom-call | flops 1000000000 | bytes 1048576 | tf_op jit(solution)/shard_map/increment/pallas_call | solution.py:164
  5.3 3.3 %collective-permute-start = (f32[72,128]{1,0:T(8,128)S(1)}, f32[72,128]{1,0:T(8,128)S(1)}, u32[]{:S(2)}, u32[]{:S(2)}) collective-permute-start(f32[72,128]{1,0:T(8,128)S(1)} %get-tuple-element.20), channel_id=1, source_target_pairs={{0,1},{1,0},{2,3},{3,2},{4,5},{5,4},{6,7},{7,6},{8,9},{9,8},{10,11... | collective-permute-start | bytes 110600 | tf_op jit(solution)/shard_map/ppermute | solution.py:531
  8.6 0.0 collective-permute-start.1
  8.6 0.0 copy-done.5
  8.6 0.0 copy-done.6
  8.6 0.0 copy-done.7
  8.6 3.3 %forward.1.seen_ref = f32[1,4096]{1,0:T(1,128)S(1)} custom-call(f32[3,64,1024]{2,1,0:T(8,128)S(1)} %get-tuple-element.19.inc_ref, f32[2,1024]{1,0:T(2,128)S(1)} %copy-done.7, s32[1,4096]{1,0:T(1,128)S(1)} %bitcast.28, s32[1,4096]{1,0:T(1,128)S(1)} %bitcast.33), custom_call_target="tpu_custom_call" | custom-call | flops 4000000000 | bytes 1048576 | tf_op jit(solution)/shard_map/forward/pallas_call | solution.py:222
  11.9 0.0 copy-start.4
  11.9 0.0 collective-permute-done.inner_ref
  11.9 0.0 collective-permute-done.1.outer_ref
  12.0 1.9 %border.1 = f32[8,32,128]{2,1,0:T(8,128)S(1)} custom-call(f32[1,4096]{1,0:T(1,128)S(1)} %forward.1.seen_ref, f32[3,64,1024]{2,1,0:T(8,128)S(1)} %get-tuple-element.19.inc_ref, f32[72,128]{1,0:T(8,128)S(1)} %collective-permute-done.inner_ref, f32[72,128]{1,0:T(8,128)S(1)} %collective-permute-done.1.outer_ref, f32[2,1024]{1,0:T(2,128)S(1)} %copy-done.7, ...), custom_call_target="tpu_custom_call" | custom-call | flops 1000000000 | bytes 1048576 | tf_op jit(solution)/shard_map/border/pallas_call | solution.py:264
  13.9 12.7 %all_to_all.16.refs_0_ = f32[8,32,128]{2,1,0:T(8,128)S(1)} all-to-all(f32[8,32,128]{2,1,0:T(8,128)S(1)} %border.1), channel_id=1, replica_groups=mesh['ens_0'=2,'ens_1'=4,'lon_0'=8,'lon_1'=2,'lon_2'=2] {'ens_0','ens_1'}, dimensions={0} | all-to-all | bytes 262144 | tf_op jit(solution)/shard_map/all_to_all | solution.py:545
  26.6 0.0 copy-done.4
  26.6 2.0 %edge_adjoint.1 = (f32[1,4096]{1,0:T(1,128)S(1)}, f32[48,1024]{1,0:T(8,128)S(1)}, f32[72,128]{1,0:T(8,128)S(1)}, f32[72,128]{1,0:T(8,128)S(1)}) custom-call(f32[8,32,128]{2,1,0:T(8,128)S(1)} %all_to_all.16.refs_0_, f32[1,4096]{1,0:T(1,128)S(1)} %bitcast.27, s32[1,4096]{1,0:T(1,128)S(1)} %bitcast.30, s32[1,4096]{1,0:T(1,128)S(1)} %bitcast.35, ...), custom_call_target="tpu_custom_call" | custom-call | flops 1000000000 | bytes 1048576 | tf_op jit(solution)/shard_map/edge_adjoint/pallas_call | solution.py:344
  28.5 7.2 %collective-permute-start.2 = (f32[72,128]{1,0:T(8,128)S(1)}, f32[72,128]{1,0:T(8,128)S(1)}, u32[]{:S(2)}, u32[]{:S(2)}) collective-permute-start(f32[72,128]{1,0:T(8,128)S(1)} %get-tuple-element.24), channel_id=1, source_target_pairs={{0,1},{1,0},{2,3},{3,2},{4,5},{5,4},{6,7},{7,6},{8,9},{9,8},{10,11... | collective-permute-start | bytes 110600 | tf_op jit(solution)/shard_map/ppermute | solution.py:531
  35.7 0.0 collective-permute-start.3
  35.7 0.0 copy-start
  35.7 0.0 copy-start.1
  35.7 3.5 %adjoint.1.adj_ref = f32[3,64,1024]{2,1,0:T(8,128)S(1)} custom-call(f32[1,4096]{1,0:T(1,128)S(1)} %get-tuple-element.22.weighted_ref, f32[48,1024]{1,0:T(8,128)S(1)} %get-tuple-element.23.edge_ref, s32[1,4096]{1,0:T(1,128)S(1)} %bitcast.32, s32[1,4096]{1,0:T(1,128)S(1)} %bitcast.36, f32[2,1024]{1,0:T(2,128)S(1)} %copy-done.7), custom_call_target="tpu_custom_call" | custom-call | flops 4000000000 | bytes 1048576 | tf_op jit(solution)/shard_map/adjoint/pallas_call | solution.py:381
  39.2 0.0 copy-done
  39.3 0.0 copy-done.1
  39.3 0.0 copy-start.2
  39.3 1.0 %image.1.own_ref = f32[2,64,1024]{2,1,0:T(8,128)S(1)} custom-call(bf16[1024,1024]{1,0:T(8,128)(2,1)S(1)} %get-tuple-element.17.high_ref, bf16[1024,1024]{1,0:T(8,128)(2,1)S(1)} %get-tuple-element.18.low_ref, f32[3,64,1024]{2,1,0:T(8,128)S(1)} %adjoint.1.adj_ref, bf16[2,3,64,1024]{3,2,1,0:T(8,128)(2,1)S(1)} %bitcast.20, f32[2,64,1024]{2,1,0:T(8,128)S(1)} %bitcast.16), custom_call_target="tpu_custom_call" | custom-call | flops 1000000000 | bytes 1048576 | tf_op jit(solution)/shard_map/image/pallas_call | solution.py:415
  40.3 0.0 collective-permute-done.2.inner_ref
  40.3 0.0 collective-permute-done.3.outer_ref
  40.3 0.0 copy-done.2
  40.4 0.0 copy-start.3
  40.4 1.0 %closing.1 = (f32[2,64,1024]{2,1,0:T(8,128)S(1)}, f32[256,128]{1,0:T(8,128)S(1)}) custom-call(bf16[1024,1024]{1,0:T(8,128)(2,1)S(1)} %get-tuple-element.17.high_ref, bf16[1024,1024]{1,0:T(8,128)(2,1)S(1)} %get-tuple-element.18.low_ref, f32[2,64,1024]{2,1,0:T(8,128)S(1)} %image.1.own_ref, f32[72,128]{1,0:T(8,128)S(1)} %collective-permute-done.2.inner_ref, ...), custom_call_target="tpu_custom_call" | custom-call | flops 500000000 | bytes 1048576 | tf_op jit(solution)/shard_map/closing/pallas_call | solution.py:473
  41.4 19.5 %all_to_all.17 = f32[256,1,128]{2,1,0:T(1,128)S(1)} all-to-all(f32[256,1,128]{2,1,0:T(1,128)S(1)} %bitcast.26), channel_id=1, replica_groups=mesh['ens_0'=2,'ens_1'=4,'lon_0'=8,'lon_1'=2,'lon_2'=2] {'ens_0','ens_1'..., dimensions={0} | all-to-all | bytes 262144 | tf_op jit(solution)/shard_map/all_to_all | solution.py:553
  60.8 0.0 copy-done.3
  60.8 1.4 %update.1 = (f32[2,64,1024]{2,1,0:T(8,128)}, f32[2,64,1024]{2,1,0:T(8,128)}, f32[2,64,1024]{2,1,0:T(8,128)}) custom-call(f32[256,128]{1,0:T(8,128)S(1)} %bitcast.25, f32[2,64,1024]{2,1,0:T(8,128)S(1)} %bitcast.24, f32[2,64,1024]{2,1,0:T(8,128)S(1)} %bitcast.23, f32[2,64,1024]{2,1,0:T(8,128)S(1)} %bitcast.18, f32[2,64,1024]{2,1,0:T(8,128)S(1)} %get-tuple-element.27.img_ref), custom_call_target="tpu_custom_call" | custom-call | flops 10000000 | bytes 1048576 | tf_op jit(solution)/shard_map/update/pallas_call | solution.py:516
Async XLA Ops:
  0.6 7.9 %copy-start.5 = (s32[4096]{0:T(1024)S(1)}, s32[4096]{0:T(1024)}, u32[]{:S(2)}) copy-start(s32[4096]{0:T(1024)} %param.14) | copy-start | bytes 49156
  0.6 7.9 %copy-start.6 = (s32[4096]{0:T(1024)S(1)}, s32[4096]{0:T(1024)}, u32[]{:S(2)}) copy-start(s32[4096]{0:T(1024)} %param.15) | copy-start | bytes 49156
  0.7 7.9 %copy-start.7 = (f32[2,1024]{1,0:T(2,128)S(1)}, f32[2,1024]{1,0:T(2,128)}, u32[]{:S(2)}) copy-start(f32[2,1024]{1,0:T(2,128)} %constant.2.clone.factor_ref.refs_5_) | copy-start | bytes 24580
  5.3 6.7 %collective-permute-start = (f32[72,128]{1,0:T(8,128)S(1)}, f32[72,128]{1,0:T(8,128)S(1)}, u32[]{:S(2)}, u32[]{:S(2)}) collective-permute-start(f32[72,128]{1,0:T(8,128)S(1)} %get-tuple-element.20), channel_id=1, source_target_pairs={{0,1},{1,0},{2,3},{3,2},{4,5},{5,4},{6,7},{7,6},{8,9},{9,8},{10,11... | collective-permute-start | bytes 110600 | tf_op jit(solution)/shard_map/ppermute | solution.py:531
  8.6 3.4 %collective-permute-start.1 = (f32[72,128]{1,0:T(8,128)S(1)}, f32[72,128]{1,0:T(8,128)S(1)}, u32[]{:S(2)}, u32[]{:S(2)}) collective-permute-start(f32[72,128]{1,0:T(8,128)S(1)} %get-tuple-element.21), channel_id=1, source_target_pairs={{0,31},{1,2},{2,1},{3,4},{4,3},{5,6},{6,5},{7,8},{8,7},{9,10},{10,... | collective-permute-start | bytes 110600 | tf_op jit(solution)/shard_map/ppermute | solution.py:531
  11.9 14.6 %copy-start.4 = (f32[4096]{0:T(1024)S(1)}, f32[4096]{0:T(1024)}, u32[]{:S(2)}) copy-start(f32[4096]{0:T(1024)} %param.16) | copy-start | bytes 49156
  28.5 11.8 %collective-permute-start.2 = (f32[72,128]{1,0:T(8,128)S(1)}, f32[72,128]{1,0:T(8,128)S(1)}, u32[]{:S(2)}, u32[]{:S(2)}) collective-permute-start(f32[72,128]{1,0:T(8,128)S(1)} %get-tuple-element.24), channel_id=1, source_target_pairs={{0,1},{1,0},{2,3},{3,2},{4,5},{5,4},{6,7},{7,6},{8,9},{9,8},{10,11... | collective-permute-start | bytes 110600 | tf_op jit(solution)/shard_map/ppermute | solution.py:531
  35.7 4.6 %collective-permute-start.3 = (f32[72,128]{1,0:T(8,128)S(1)}, f32[72,128]{1,0:T(8,128)S(1)}, u32[]{:S(2)}, u32[]{:S(2)}) collective-permute-start(f32[72,128]{1,0:T(8,128)S(1)} %get-tuple-element.25), channel_id=1, source_target_pairs={{0,31},{1,2},{2,1},{3,4},{4,3},{5,6},{6,5},{7,8},{8,7},{9,10},{10,... | collective-permute-start | bytes 110600 | tf_op jit(solution)/shard_map/ppermute | solution.py:531
  35.7 3.5 %copy-start = (f32[2,1024,64]{1,2,0:T(8,128)S(1)}, f32[2,1024,64]{1,2,0:T(8,128)}, u32[]{:S(2)}) copy-start(f32[2,1024,64]{1,2,0:T(8,128)} %param.11) | copy-start | bytes 1572868
  35.7 3.5 %copy-start.1 = (bf16[2,3,1024,64]{2,3,1,0:T(8,128)(2,1)S(1)}, bf16[2,3,1024,64]{2,3,1,0:T(8,128)(2,1)}, u32[]{:S(2)}) copy-start(bf16[2,3,1024,64]{2,3,1,0:T(8,128)(2,1)} %param.12) | copy-start | bytes 2359300
  39.3 1.1 %copy-start.2 = (f32[2,1024,64]{1,2,0:T(8,128)S(1)}, f32[2,1024,64]{1,2,0:T(8,128)}, u32[]{:S(2)}) copy-start(f32[2,1024,64]{1,2,0:T(8,128)} %param.10) | copy-start | bytes 1572868
  40.4 20.5 %copy-start.3 = (f32[2,1024,64]{1,2,0:T(8,128)S(1)}, f32[2,1024,64]{1,2,0:T(8,128)}, u32[]{:S(2)}) copy-start(f32[2,1024,64]{1,2,0:T(8,128)} %param.9) | copy-start | bytes 1572868

commit v5 on v4

--- a/solution.py
+++ b/solution.py
@@ -30,6 +30,10 @@
     return high, low
 
 
+def remainder(x):
+    return x - x.astype(BF16).astype(F32)
+
+
 def dot(a, b, dims):
     return lax.dot_general(a, b, dims, preferred_element_type=F32)
 
@@ -40,12 +44,11 @@
     return np.stack([1.0 / np.cos(latitude), np.sin(latitude)]).astype(np.float32)
 
 
-def model_step(h, u, v, orient, metric, coriolis):
-    wide, rows = h.shape
+def differences(shape, orient, metric):
+    wide, rows = shape
     lane = lax.broadcasted_iota(jnp.int32, (1, rows), 1)
     lon_scale = (orient * wave_speed * 0.5) * metric
     lat_scale = orient * wave_speed * 0.5
-    turn = (orient * rotation) * coriolis
     keep_next = jnp.where(lane == rows - 1, 0.0, lat_scale)
     keep_last = jnp.where(lane == 0, 0.0, lat_scale)
 
@@ -55,11 +58,22 @@
     def lat_diff(x):
         return keep_next * pltpu.roll(x, rows - 1, 1) - keep_last * pltpu.roll(x, 1, 1)
 
+    return lon_diff, lat_diff
+
+
+def model_step(h, u, v, orient, metric, coriolis):
+    turn = (orient * rotation) * coriolis
+    lon_diff, lat_diff = differences(h.shape, orient, metric)
     return (
         h - (lon_diff(u) + lat_diff(v)),
         u - lon_diff(h) + turn * v,
         v - lat_diff(h) - turn * u,
     )
+
+
+def first_step(h, orient, metric):
+    lon_diff, lat_diff = differences(h.shape, orient, metric)
+    return h, -lon_diff(h), -lat_diff(h)
 
 
 def call(kernel, name, out_shape, scratch, flops, limit_mib=24, **options):
@@ -111,8 +125,8 @@
 
 
 def increment_kernel(
-    loc_hbm, dir_hbm, pert_hbm, inc_ref, inner_ref, outer_ref, high_ref, low_ref,
-    loc_ref, dir_ref, pert_ref, parts_ref, sems,
+    loc_hbm, dir_hbm, pert_hbm, inc_ref, inner_ref, outer_ref, loc_ref, low_ref,
+    dir_ref, pert_ref, parts_ref, sems,
 ):
     members, cols, rows = dir_ref.shape
     lines = members * cols
@@ -132,20 +146,20 @@
     for copy in copies[1:]:
         copy.start()
     first.wait()
-    high, low = split_two(dir_ref[...].reshape(lines, rows))
-    parts_ref[0:lines] = high
-    parts_ref[lines : 2 * lines] = low
+    flat = dir_ref[...].reshape(lines, rows)
+    parts_ref[0:lines] = flat
+    parts_ref[lines : 2 * lines] = remainder(flat)
     for i in range(blocks + 1):
         if i < blocks:
             copies[i].wait()
-            high_ref[places[i]], low_ref[places[i]] = split_two(loc_ref[places[i]])
+            low_ref[places[i]] = remainder(loc_ref[places[i]]).astype(BF16)
         if i == 0:
             continue
         if i == 1:
             second.wait()
         here = places[i - 1]
-        both = dot(parts_ref[...], high_ref[here], NT)
-        rest = dot(parts_ref[0:lines], low_ref[here], NT)
+        both = dot(parts_ref[...], loc_ref[here], NT)
+        rest = dot(parts_ref[0:lines].astype(BF16), low_ref[here], NT)
         localized = both[0:lines] + both[lines : 2 * lines] + rest
         for field in range(3):
             total = None
@@ -160,16 +174,15 @@
 
 def partial_increment(localize, direction, pert):
     members, cols, rows = direction.shape
-    half = jax.ShapeDtypeStruct((rows, rows), BF16)
+    low = jax.ShapeDtypeStruct((rows, rows), BF16)
     return call(
         increment_kernel,
         "increment",
-        [floats(3, cols, rows), edge_floats(rows), edge_floats(rows), half, half],
+        [floats(3, cols, rows), edge_floats(rows), edge_floats(rows), floats(rows, rows), low],
         [
-            pltpu.VMEM((rows, rows), F32),
             pltpu.VMEM(direction.shape, F32),
             pltpu.VMEM(pert.shape, BF16),
-            pltpu.VMEM((2 * members * cols, rows), BF16),
+            pltpu.VMEM((2 * members * cols, rows), F32),
             pltpu.SemaphoreType.DMA((2 + rows // 256,)),
         ],
         10**9,
@@ -276,10 +289,13 @@
 def backward_steps(state_ref, factor_ref, add_force):
     metric = factor_ref[0:1]
     coriolis = factor_ref[1:2]
-    state_ref[...] = jnp.zeros(state_ref.shape, F32)
+    state_ref[0] = jnp.zeros(state_ref.shape[1:], F32)
     for moment in reversed(range(STEPS)):
         add_force(moment)
-        h, u, v = model_step(state_ref[0], state_ref[1], state_ref[2], -1.0, metric, coriolis)
+        if moment == STEPS - 1:
+            h, u, v = first_step(state_ref[0], -1.0, metric)
+        else:
+            h, u, v = model_step(state_ref[0], state_ref[1], state_ref[2], -1.0, metric, coriolis)
         state_ref[0] = h
         state_ref[1] = u
         state_ref[2] = v
@@ -350,10 +366,17 @@
     )(seen, weight, cell, slot, cell.reshape(nobs // 128, 128), factors)
 
 
+def three_products(parts_ref, loc_ref, low_ref, lines):
+    both = dot(parts_ref[...], loc_ref[...], NN)
+    rest = dot(parts_ref[0:lines].astype(BF16), low_ref[...], NN)
+    return both[0:lines] + both[lines : 2 * lines] + rest
+
+
 def adjoint_kernel(
-    weighted_ref, edge_ref, cell_ref, slot_ref, factor_ref, adj_ref, state_ref, force_ref
+    weighted_ref, edge_ref, cell_ref, slot_ref, factor_ref, loc_ref, low_ref, pert_ref, dir_ref,
+    img_ref, state_ref, force_ref, parts_ref,
 ):
-    _, cols, rows = adj_ref.shape
+    members, cols, rows = dir_ref.shape
     nobs = cell_ref.shape[1]
     count = cols - 2 * PAD
     chunk = 512
@@ -372,57 +395,34 @@
         state_ref[0, cols : PAD + cols] += edge_ref[near + PAD : near + 2 * PAD]
 
     backward_steps(state_ref, factor_ref, add_force)
-    for field in range(3):
-        adj_ref[field] = state_ref[field, PAD : PAD + cols]
-
-
-def tile_adjoint(weighted, edge, cell, slot, factors, cols):
-    rows = factors.shape[1]
+    lines = members * cols
+    for m in range(members):
+        projected = pert_ref[m, 0].astype(F32) * state_ref[0, PAD : PAD + cols]
+        projected += pert_ref[m, 1].astype(F32) * state_ref[1, PAD : PAD + cols]
+        projected += pert_ref[m, 2].astype(F32) * state_ref[2, PAD : PAD + cols]
+        parts_ref[m * cols : (m + 1) * cols] = projected
+        parts_ref[lines + m * cols : lines + (m + 1) * cols] = remainder(projected)
+    pulled = three_products(parts_ref, loc_ref, low_ref, lines)
+    img_ref[...] = dir_ref[...] + pulled.reshape(members, cols, rows)
+
+
+def own_image(weighted, edge, cell, slot, factors, loc, low, pert, direction):
+    members, cols, rows = direction.shape
     return call(
         adjoint_kernel,
         "adjoint",
-        floats(3, cols, rows),
+        floats(members, cols, rows),
         [
             pltpu.VMEM((3, cols + 2 * PAD, rows), F32),
             pltpu.VMEM((STEPS * (cols - 2 * PAD), rows), F32),
+            pltpu.VMEM((2 * members * cols, rows), F32),
         ],
         4 * 10**9,
-    )(weighted, edge, cell, slot, factors)
-
-
-def three_products(parts_ref, high_ref, low_ref, lines):
-    both = dot(parts_ref[...], high_ref[...], NN)
-    rest = dot(parts_ref[0:lines], low_ref[...], NN)
-    return both[0:lines] + both[lines : 2 * lines] + rest
-
-
-def image_kernel(high_ref, low_ref, adj_ref, pert_ref, dir_ref, img_ref, parts_ref):
-    members, cols, rows = dir_ref.shape
-    lines = members * cols
-    for m in range(members):
-        projected = pert_ref[m, 0].astype(F32) * adj_ref[0]
-        projected += pert_ref[m, 1].astype(F32) * adj_ref[1]
-        projected += pert_ref[m, 2].astype(F32) * adj_ref[2]
-        high, low = split_two(projected)
-        parts_ref[m * cols : (m + 1) * cols] = high
-        parts_ref[lines + m * cols : lines + (m + 1) * cols] = low
-    pulled = three_products(parts_ref, high_ref, low_ref, lines)
-    img_ref[...] = dir_ref[...] + pulled.reshape(members, cols, rows)
-
-
-def own_image(high, low, adj, pert, direction):
-    members, cols, rows = direction.shape
-    return call(
-        image_kernel,
-        "image",
-        floats(members, cols, rows),
-        [pltpu.VMEM((2 * members * cols, rows), BF16)],
-        10**9,
-    )(high, low, adj, pert, direction)
+    )(weighted, edge, cell, slot, factors, loc, low, pert, direction)
 
 
 def closing_kernel(
-    high_ref, low_ref, own_ref, inner_ref, outer_ref, pert_ref, dir_ref, res_ref, img_ref, sums_ref,
+    loc_ref, low_ref, own_ref, inner_ref, outer_ref, pert_ref, dir_ref, res_ref, img_ref, sums_ref,
     edge_ref, parts_ref,
 ):
     members, cols, rows = dir_ref.shape
@@ -440,10 +440,10 @@
         for field in range(3):
             west += pert_ref[m, field, 0:PAD].astype(F32) * edge_ref[field, 0:PAD]
             east += pert_ref[m, field, cols - PAD : cols].astype(F32) * edge_ref[field, PAD:near]
-        high, low = split_two(jnp.concatenate([west, east], axis=0))
-        parts_ref[m * near : (m + 1) * near] = high
-        parts_ref[lines + m * near : lines + (m + 1) * near] = low
-    pulled = three_products(parts_ref, high_ref, low_ref, lines)
+        projected = jnp.concatenate([west, east], axis=0)
+        parts_ref[m * near : (m + 1) * near] = projected
+        parts_ref[lines + m * near : lines + (m + 1) * near] = remainder(projected)
+    pulled = three_products(parts_ref, loc_ref, low_ref, lines)
     totals = [jnp.zeros((8, rows), F32) for _ in range(4)]
     for m in range(members):
         for start in range(0, cols, PAD):
@@ -468,7 +468,7 @@
     sums_ref[...] = jnp.broadcast_to(packed, sums_ref.shape)
 
 
-def image_and_sums(high, low, own, inner, outer, pert, direction, residual, copies):
+def image_and_sums(loc, low, own, inner, outer, pert, direction, residual, copies):
     members, cols, rows = direction.shape
     return call(
         closing_kernel,
@@ -476,10 +476,10 @@
         [floats(members, cols, rows), floats(copies, 128)],
         [
             pltpu.VMEM((3, 2 * PAD, rows), F32),
-            pltpu.VMEM((4 * members * PAD, rows), BF16),
+            pltpu.VMEM((4 * members * PAD, rows), F32),
         ],
         5 * 10**8,
-    )(high, low, own, inner, outer, pert, direction, residual)
+    )(loc, low, own, inner, outer, pert, direction, residual)
 
 
 def update_kernel(
@@ -538,17 +538,18 @@
     control_t, residual_t, direction_t = turned(control), turned(residual), turned(direction)
     pert = jnp.swapaxes(ens_perturb, 2, 3)
     cell, slot, weight = obs_cell[None], obs_slot[None], obs_weight[None]
-    inc, inner, outer, high, low = partial_increment(localize, direction_t, pert)
+    inc, inner, outer, loc, low = partial_increment(localize, direction_t, pert)
     inner, outer = swapped(inner, outer)
     seen = inner_observed(inc, factors, cell, slot)
     seen = observed_parts(seen, inc, inner, outer, factors, cell, slot, lax.axis_size(ENS))
     seen = lax.all_to_all(seen, ENS, 0, 0, tiled=True)
     weighted, edge, inner, outer = edge_adjoint(seen, weight, cell, slot, factors, cols)
     inner, outer = swapped(inner, outer)
-    adj = tile_adjoint(weighted, edge, cell, slot, factors, cols)
-    image = own_image(high, low, adj, pert, direction_t)
+    image = own_image(
+        weighted, edge, cell, slot, factors, loc, low, pert, direction_t
+    )
     image, sums = image_and_sums(
-        high, low, image, inner, outer, pert, direction_t, residual_t, lax.axis_size(ENS_LON)
+        loc, low, image, inner, outer, pert, direction_t, residual_t, lax.axis_size(ENS_LON)
     )
     sums = lax.all_to_all(sums, ENS_LON, 0, 0, tiled=True)
     results = updated(sums, control_t, residual_t, direction_t, image)

time: 62.6 us -> 62.1 us (level)
    pallas_call x2 -> x1, Pallas kernels: 4.53 us -> 4.51 us  [own_image(): call(adjoint_kernel, 'adjoint', floats(members, cols, rows), [pltpu.VMEM(...]
where the time goes in v5:
time: 62.1 us; the launch traced here: 61.9 us
  blocking collectives  32.1 us (52%)
  Pallas kernels  18.3 us (29%)
  starting transfers between devices  10.5 us (17%)
  between operations  0.95 us (2%)
    all_to_all x1, blocking collectives, body(): sums = lax.all_to_all(sums, ENS_LON, 0, 0, tiled=True)  19.4 us
    all_to_all x1, blocking collectives, body(): seen = lax.all_to_all(seen, ENS, 0, 0, tiled=True)  12.7 us
    ppermute x2, starting transfers between devices, swapped(): lax.ppermute(inner, LON, inner_pairs)  10.5 us
    pallas_call x1, Pallas kernels, own_image(): call(adjoint_kernel, 'adjoint', floats(members, cols, rows), [pltpu.VMEM(...  4.51 us
    pallas_call x1, Pallas kernels, partial_increment(): call(increment_kernel, 'increment', [floats(3, cols, rows), edge_floats(r...  4.18 us
    pallas_call x1, Pallas kernels, inner_observed(): call(forward_kernel, 'forward', floats(1, cell.shape[1]), [pltpu.VMEM((3,...  3.32 us
    pallas_call x1, Pallas kernels, edge_adjoint(): call(lambda *refs: edge_adjoint_kernel(*refs, cols=cols), 'edge_adjoint',...  1.94 us
    pallas_call x1, Pallas kernels, observed_parts(): call(border_kernel, 'border', floats(copies, cell.shape[1] // 128, 128),...  1.94 us
  transfers between devices with their start and end apart: 4, of which 0 were waited for; matrix products, arithmetic and copies ran while one was open for 0% of the time, Pallas kernels for 13%

profile of v5, /device:TPU:1, one launch (start us, length us, event | category | flops | bytes accessed | tf_op | source)
XLA Modules:
  0.0 61.9 jit_solution(13684412514404956517)
XLA Ops:
  0.6 0.0 copy-start.7
  0.6 0.0 copy-start.5
  0.7 0.0 copy-start.6
  0.7 4.2 %increment.1 = (f32[3,64,1024]{2,1,0:T(8,128)S(1)}, f32[72,128]{1,0:T(8,128)S(1)}, f32[72,128]{1,0:T(8,128)S(1)}, f32[1024,1024]{1,0:T(8,128)S(1)}, bf16[1024,1024]{1,0:T(8,128)(2,1)S(1)}) custom-call(f32[1024,1024]{1,0:T(8,128)} %loc_hbm.1, f32[2,64,1024]{2,1,0:T(8,128)} %bitcast.15, bf16[2,3,64,1024]{3,2,1,0:T(8,128)(2,1)} %bitcast.19), custom_call_target="tpu_custom_call" | custom-call | flops 1000000000 | bytes 1048576 | tf_op jit(solution)/shard_map/increment/pallas_call | solution.py:178
  4.8 3.3 %collective-permute-start = (f32[72,128]{1,0:T(8,128)S(1)}, f32[72,128]{1,0:T(8,128)S(1)}, u32[]{:S(2)}, u32[]{:S(2)}) collective-permute-start(f32[72,128]{1,0:T(8,128)S(1)} %get-tuple-element.20), channel_id=1, source_target_pairs={{0,1},{1,0},{2,3},{3,2},{4,5},{5,4},{6,7},{7,6},{8,9},{9,8},{10,11... | collective-permute-start | bytes 110600 | tf_op jit(solution)/shard_map/ppermute | solution.py:531
  8.1 0.0 collective-permute-start.1
  8.1 0.0 copy-done.7
  8.1 0.0 copy-done.5
  8.1 0.0 copy-done.6
  8.2 0.0 copy-start.4
  8.2 3.3 %forward.1.seen_ref = f32[1,4096]{1,0:T(1,128)S(1)} custom-call(f32[3,64,1024]{2,1,0:T(8,128)S(1)} %get-tuple-element.19.inc_ref, f32[2,1024]{1,0:T(2,128)S(1)} %copy-done.7, s32[1,4096]{1,0:T(1,128)S(1)} %bitcast.28, s32[1,4096]{1,0:T(1,128)S(1)} %bitcast.33), custom_call_target="tpu_custom_call" | custom-call | flops 4000000000 | bytes 1048576 | tf_op jit(solution)/shard_map/forward/pallas_call | solution.py:235
  11.5 0.0 copy-start
  11.5 0.0 copy-start.1
  11.5 0.0 collective-permute-done.inner_ref
  11.5 0.0 collective-permute-done.1.outer_ref
  11.5 1.9 %border.1 = f32[8,32,128]{2,1,0:T(8,128)S(1)} custom-call(f32[1,4096]{1,0:T(1,128)S(1)} %forward.1.seen_ref, f32[3,64,1024]{2,1,0:T(8,128)S(1)} %get-tuple-element.19.inc_ref, f32[72,128]{1,0:T(8,128)S(1)} %collective-permute-done.inner_ref, f32[72,128]{1,0:T(8,128)S(1)} %collective-permute-done.1.outer_ref, f32[2,1024]{1,0:T(2,128)S(1)} %copy-done.7, ...), custom_call_target="tpu_custom_call" | custom-call | flops 1000000000 | bytes 1048576 | tf_op jit(solution)/shard_map/border/pallas_call | solution.py:277
  13.5 12.7 %all_to_all.16.refs_0_ = f32[8,32,128]{2,1,0:T(8,128)S(1)} all-to-all(f32[8,32,128]{2,1,0:T(8,128)S(1)} %border.1), channel_id=1, replica_groups=mesh['ens_0'=2,'ens_1'=4,'lon_0'=8,'lon_1'=2,'lon_2'=2] {'ens_0','ens_1'}, dimensions={0} | all-to-all | bytes 262144 | tf_op jit(solution)/shard_map/all_to_all | solution.py:545
  26.1 0.0 copy-done.4
  26.1 1.9 %edge_adjoint.1 = (f32[1,4096]{1,0:T(1,128)S(1)}, f32[48,1024]{1,0:T(8,128)S(1)}, f32[72,128]{1,0:T(8,128)S(1)}, f32[72,128]{1,0:T(8,128)S(1)}) custom-call(f32[8,32,128]{2,1,0:T(8,128)S(1)} %all_to_all.16.refs_0_, f32[1,4096]{1,0:T(1,128)S(1)} %bitcast.27, s32[1,4096]{1,0:T(1,128)S(1)} %bitcast.30, s32[1,4096]{1,0:T(1,128)S(1)} %bitcast.35, ...), custom_call_target="tpu_custom_call" | custom-call | flops 1000000000 | bytes 1048576 | tf_op jit(solution)/shard_map/edge_adjoint/pallas_call | solution.py:360
  28.1 7.2 %collective-permute-start.2 = (f32[72,128]{1,0:T(8,128)S(1)}, f32[72,128]{1,0:T(8,128)S(1)}, u32[]{:S(2)}, u32[]{:S(2)}) collective-permute-start(f32[72,128]{1,0:T(8,128)S(1)} %get-tuple-element.24), channel_id=1, source_target_pairs={{0,1},{1,0},{2,3},{3,2},{4,5},{5,4},{6,7},{7,6},{8,9},{9,8},{10,11... | collective-permute-start | bytes 110600 | tf_op jit(solution)/shard_map/ppermute | solution.py:531
  35.3 0.0 collective-permute-start.3
  35.3 0.0 copy-done
  35.3 0.0 copy-done.1
  35.3 0.0 copy-start.2
  35.3 4.5 %adjoint.1.own_ref = f32[2,64,1024]{2,1,0:T(8,128)S(1)} custom-call(f32[1,4096]{1,0:T(1,128)S(1)} %get-tuple-element.22.weighted_ref, f32[48,1024]{1,0:T(8,128)S(1)} %get-tuple-element.23.edge_ref, s32[1,4096]{1,0:T(1,128)S(1)} %bitcast.32, s32[1,4096]{1,0:T(1,128)S(1)} %bitcast.36, f32[2,1024]{1,0:T(2,128)S(1)} %copy-done.7, ...), custom_call_target="tpu_custom_call" | custom-call | flops 4000000000 | bytes 1048576 | tf_op jit(solution)/shard_map/adjoint/pallas_call | solution.py:411
  39.8 0.0 collective-permute-done.2.inner_ref
  39.9 0.0 collective-permute-done.3.outer_ref
  39.9 0.0 copy-done.2
  39.9 0.0 copy-start.3
  39.9 1.0 %closing.1 = (f32[2,64,1024]{2,1,0:T(8,128)S(1)}, f32[256,128]{1,0:T(8,128)S(1)}) custom-call(f32[1024,1024]{1,0:T(8,128)S(1)} %get-tuple-element.17.loc_ref, bf16[1024,1024]{1,0:T(8,128)(2,1)S(1)} %get-tuple-element.18.low_ref, f32[2,64,1024]{2,1,0:T(8,128)S(1)} %adjoint.1.own_ref, f32[72,128]{1,0:T(8,128)S(1)} %collective-permute-done.2.inner_ref, ...), custom_call_target="tpu_custom_call" | custom-call | flops 500000000 | bytes 1048576 | tf_op jit(solution)/shard_map/closing/pallas_call | solution.py:473
  40.9 19.4 %all_to_all.17 = f32[256,1,128]{2,1,0:T(1,128)S(1)} all-to-all(f32[256,1,128]{2,1,0:T(1,128)S(1)} %bitcast.26), channel_id=1, replica_groups=mesh['ens_0'=2,'ens_1'=4,'lon_0'=8,'lon_1'=2,'lon_2'=2] {'ens_0','ens_1'..., dimensions={0} | all-to-all | bytes 262144 | tf_op jit(solution)/shard_map/all_to_all | solution.py:554
  60.3 0.0 copy-done.3
  60.3 1.4 %update.1 = (f32[2,64,1024]{2,1,0:T(8,128)}, f32[2,64,1024]{2,1,0:T(8,128)}, f32[2,64,1024]{2,1,0:T(8,128)}) custom-call(f32[256,128]{1,0:T(8,128)S(1)} %bitcast.25, f32[2,64,1024]{2,1,0:T(8,128)S(1)} %bitcast.24, f32[2,64,1024]{2,1,0:T(8,128)S(1)} %bitcast.23, f32[2,64,1024]{2,1,0:T(8,128)S(1)} %bitcast.18, f32[2,64,1024]{2,1,0:T(8,128)S(1)} %get-tuple-element.27.img_ref), custom_call_target="tpu_custom_call" | custom-call | flops 10000000 | bytes 1048576 | tf_op jit(solution)/shard_map/update/pallas_call | solution.py:516
Async XLA Ops:
  0.6 7.5 %copy-start.7 = (f32[2,1024]{1,0:T(2,128)S(1)}, f32[2,1024]{1,0:T(2,128)}, u32[]{:S(2)}) copy-start(f32[2,1024]{1,0:T(2,128)} %constant.2.clone.factor_ref.refs_5_) | copy-start | bytes 24580
  0.6 7.5 %copy-start.5 = (s32[4096]{0:T(1024)S(1)}, s32[4096]{0:T(1024)}, u32[]{:S(2)}) copy-start(s32[4096]{0:T(1024)} %param.14) | copy-start | bytes 49156
  0.7 7.5 %copy-start.6 = (s32[4096]{0:T(1024)S(1)}, s32[4096]{0:T(1024)}, u32[]{:S(2)}) copy-start(s32[4096]{0:T(1024)} %param.15) | copy-start | bytes 49156
  4.8 6.7 %collective-permute-start = (f32[72,128]{1,0:T(8,128)S(1)}, f32[72,128]{1,0:T(8,128)S(1)}, u32[]{:S(2)}, u32[]{:S(2)}) collective-permute-start(f32[72,128]{1,0:T(8,128)S(1)} %get-tuple-element.20), channel_id=1, source_target_pairs={{0,1},{1,0},{2,3},{3,2},{4,5},{5,4},{6,7},{7,6},{8,9},{9,8},{10,11... | collective-permute-start | bytes 110600 | tf_op jit(solution)/shard_map/ppermute | solution.py:531
  8.1 3.4 %collective-permute-start.1 = (f32[72,128]{1,0:T(8,128)S(1)}, f32[72,128]{1,0:T(8,128)S(1)}, u32[]{:S(2)}, u32[]{:S(2)}) collective-permute-start(f32[72,128]{1,0:T(8,128)S(1)} %get-tuple-element.21), channel_id=1, source_target_pairs={{0,31},{1,2},{2,1},{3,4},{4,3},{5,6},{6,5},{7,8},{8,7},{9,10},{10,... | collective-permute-start | bytes 110600 | tf_op jit(solution)/shard_map/ppermute | solution.py:531
  8.2 18.0 %copy-start.4 = (f32[4096]{0:T(1024)S(1)}, f32[4096]{0:T(1024)}, u32[]{:S(2)}) copy-start(f32[4096]{0:T(1024)} %param.16) | copy-start | bytes 49156
  11.5 23.8 %copy-start = (f32[2,1024,64]{1,2,0:T(8,128)S(1)}, f32[2,1024,64]{1,2,0:T(8,128)}, u32[]{:S(2)}) copy-start(f32[2,1024,64]{1,2,0:T(8,128)} %param.11) | copy-start | bytes 1572868
  11.5 23.8 %copy-start.1 = (bf16[2,3,1024,64]{2,3,1,0:T(8,128)(2,1)S(1)}, bf16[2,3,1024,64]{2,3,1,0:T(8,128)(2,1)}, u32[]{:S(2)}) copy-start(bf16[2,3,1024,64]{2,3,1,0:T(8,128)(2,1)} %param.12) | copy-start | bytes 2359300
  28.1 11.8 %collective-permute-start.2 = (f32[72,128]{1,0:T(8,128)S(1)}, f32[72,128]{1,0:T(8,128)S(1)}, u32[]{:S(2)}, u32[]{:S(2)}) collective-permute-start(f32[72,128]{1,0:T(8,128)S(1)} %get-tuple-element.24), channel_id=1, source_target_pairs={{0,1},{1,0},{2,3},{3,2},{4,5},{5,4},{6,7},{7,6},{8,9},{9,8},{10,11... | collective-permute-start | bytes 110600 | tf_op jit(solution)/shard_map/ppermute | solution.py:531
  35.3 4.6 %collective-permute-start.3 = (f32[72,128]{1,0:T(8,128)S(1)}, f32[72,128]{1,0:T(8,128)S(1)}, u32[]{:S(2)}, u32[]{:S(2)}) collective-permute-start(f32[72,128]{1,0:T(8,128)S(1)} %get-tuple-element.25), channel_id=1, source_target_pairs={{0,31},{1,2},{2,1},{3,4},{4,3},{5,6},{6,5},{7,8},{8,7},{9,10},{10,... | collective-permute-start | bytes 110600 | tf_op jit(solution)/shard_map/ppermute | solution.py:531
  35.3 4.6 %copy-start.2 = (f32[2,1024,64]{1,2,0:T(8,128)S(1)}, f32[2,1024,64]{1,2,0:T(8,128)}, u32[]{:S(2)}) copy-start(f32[2,1024,64]{1,2,0:T(8,128)} %param.10) | copy-start | bytes 1572868
  39.9 20.5 %copy-start.3 = (f32[2,1024,64]{1,2,0:T(8,128)S(1)}, f32[2,1024,64]{1,2,0:T(8,128)}, u32[]{:S(2)}) copy-start(f32[2,1024,64]{1,2,0:T(8,128)} %param.9) | copy-start | bytes 1572868

commit v6 on v5

--- a/solution.py
+++ b/solution.py
@@ -9,6 +9,8 @@
 
 STEPS = 3
 HALO = 3
+REACH = 2 * HALO
+CORNER = HALO * (HALO + 1) // 2
 PAD = 8
 LON = ("lon_0", "lon_1", "lon_2")
 ENS = ("ens_0", "ens_1")
@@ -107,26 +109,62 @@
     return lax.axis_index("lon_2") == 1
 
 
-def put_edge(ref, field, lanes, value):
-    for i in range(lanes // 128, lanes // 128 + value.shape[1] // 128):
-        line = 3 * HALO * i + HALO * field
-        at = i * 128 - lanes
-        ref[line : line + HALO] = value[:, at : at + 128]
-
-
-def get_edge(ref, field):
-    tiles = range(ref.shape[0] // (3 * HALO))
-    lines = [3 * HALO * i + HALO * field for i in tiles]
-    return jnp.concatenate([ref[line : line + HALO] for line in lines], axis=1)
+def corner(moment):
+    first = moment * (moment + 1) // 2
+    return slice(first, first + moment + 1)
 
 
 def edge_floats(rows):
-    return floats(3 * HALO * rows // 128, 128)
+    return floats(3 * REACH + CORNER, rows)
+
+
+def from_sides(inner, outer):
+    odd = on_odd_tile()
+    return jnp.where(odd, inner, outer), jnp.where(odd, outer, inner)
+
+
+def placed(spots, spot, weighted):
+    spot_hot = lax.broadcasted_iota(jnp.int32, (spots, spot.shape[1]), 0) == spot
+    return jnp.concatenate(split_two(jnp.where(spot_hot, weighted, 0.0)), axis=0)
+
+
+def gather_force(force_ref, part, start):
+    spots = force_ref.shape[0]
+    part = part[0:spots] + part[spots : 2 * spots]
+    if start == 0:
+        force_ref[...] = part
+    else:
+        force_ref[...] += part
+
+
+def edge_weights(sum_ref, cell, slot, weight, cols):
+    rows = sum_ref.shape[1]
+    upright = jnp.transpose(lax.shift_right_logical(cell, cols.bit_length() - 1))
+    ids = lax.broadcasted_iota(jnp.int16, (128, rows), 1)
+    for start in range(0, cell.shape[0], 4):
+        lines = range(start, start + 4)
+        cell_at, slot_at, weight_at = (
+            jnp.concatenate([x[i : i + 1] for i in lines], axis=1) for x in (cell, slot, weight)
+        )
+        _, _, col = rows_and_spots(cell_at, slot_at, cols)
+        first = lax.shift_right_logical(slot_at * (slot_at + 1), 1)
+        from_east = col - (cols - 1 - slot_at)
+        spot = jnp.where(from_east >= 0, CORNER + first + from_east, -1)
+        spot = jnp.where(col <= slot_at, first + col, spot)
+        spot = jnp.where(slot_at < STEPS, spot, -1)
+        hots = []
+        for i in lines:
+            row = jnp.broadcast_to(upright[:, i : i + 1], (128, 128)).astype(jnp.int16)
+            row = jnp.concatenate([row] * (rows // 128), axis=1)
+            hots.append(jnp.where(ids == row, jnp.ones((), BF16), jnp.zeros((), BF16)))
+        part = dot(placed(sum_ref.shape[0], spot, weight_at), jnp.concatenate(hots, axis=0), NN)
+        gather_force(sum_ref, part, start)
 
 
 def increment_kernel(
-    loc_hbm, dir_hbm, pert_hbm, inc_ref, inner_ref, outer_ref, loc_ref, low_ref,
-    dir_ref, pert_ref, parts_ref, sems,
+    loc_hbm, dir_hbm, pert_hbm, cell_hbm, slot_hbm, weight_hbm,
+    inc_ref, inner_ref, outer_ref, loc_ref, low_ref,
+    dir_ref, pert_ref, parts_ref, cell_ref, slot_ref, weight_ref, sum_ref, sems,
 ):
     members, cols, rows = dir_ref.shape
     lines = members * cols
@@ -139,12 +177,26 @@
         pltpu.make_async_copy(loc_hbm.at[here], loc_ref.at[here], sems.at[2 + i])
         for i, here in enumerate(places)
     ]
+    lists = [
+        pltpu.make_async_copy(source, target, sems.at[2 + blocks + i])
+        for i, (source, target) in enumerate(
+            ((cell_hbm, cell_ref), (slot_hbm, slot_ref), (weight_hbm, weight_ref))
+        )
+    ]
     odd = on_odd_tile()
+    for copy in lists:
+        copy.start()
     first.start()
     copies[0].start()
     second.start()
     for copy in copies[1:]:
         copy.start()
+    for copy in lists:
+        copy.wait()
+    edge_weights(sum_ref, cell_ref[...], slot_ref[...], weight_ref[...], cols)
+    west, east = sum_ref[0:CORNER], sum_ref[CORNER : 2 * CORNER]
+    inner_ref[3 * REACH : 3 * REACH + CORNER] = jnp.where(odd, west, east)
+    outer_ref[3 * REACH : 3 * REACH + CORNER] = jnp.where(odd, east, west)
     first.wait()
     flat = dir_ref[...].reshape(lines, rows)
     parts_ref[0:lines] = flat
@@ -167,12 +219,12 @@
                 term = pert_ref[m, field, :, here].astype(F32) * localized[m * cols : (m + 1) * cols]
                 total = term if total is None else total + term
             inc_ref[field, :, here] = total
-            west, east = total[0:HALO], total[cols - HALO : cols]
-            put_edge(inner_ref, field, here.start, jnp.where(odd, west, east))
-            put_edge(outer_ref, field, here.start, jnp.where(odd, east, west))
-
-
-def partial_increment(localize, direction, pert):
+            west, east = total[0:REACH], total[cols - REACH : cols]
+            inner_ref[REACH * field : REACH * (field + 1), here] = jnp.where(odd, west, east)
+            outer_ref[REACH * field : REACH * (field + 1), here] = jnp.where(odd, east, west)
+
+
+def partial_increment(localize, direction, pert, lists):
     members, cols, rows = direction.shape
     low = jax.ShapeDtypeStruct((rows, rows), BF16)
     return call(
@@ -183,14 +235,21 @@
             pltpu.VMEM(direction.shape, F32),
             pltpu.VMEM(pert.shape, BF16),
             pltpu.VMEM((2 * members * cols, rows), F32),
-            pltpu.SemaphoreType.DMA((2 + rows // 256,)),
+            *(pltpu.VMEM(x.shape, x.dtype) for x in lists),
+            pltpu.VMEM((16, rows), F32),
+            pltpu.SemaphoreType.DMA((2 + rows // 256 + len(lists),)),
         ],
         10**9,
-        in_specs=[HBM, HBM, HBM],
-    )(*(pltpu.with_memory_space_constraint(x, pltpu.HBM) for x in (localize, direction, pert)))
-
-
-def forward_steps(state_ref, factor_ref, parts_ref, places):
+        in_specs=[HBM] * (3 + len(lists)),
+    )(
+        *(
+            pltpu.with_memory_space_constraint(x, pltpu.HBM)
+            for x in (localize, direction, pert, *lists)
+        )
+    )
+
+
+def forward_steps(state_ref, factor_ref, parts_ref, places, keep=None):
     metric = factor_ref[0:1]
     coriolis = factor_ref[1:2]
     count = sum(stop - start for start, stop in places)
@@ -200,6 +259,8 @@
             state_ref[0] = h
             state_ref[1] = u
             state_ref[2] = v
+        if keep is not None:
+            keep(moment, h)
         line = moment * count
         for start, stop in places:
             high, low = split_two(h[start:stop])
@@ -246,19 +307,35 @@
 
 def border_kernel(
     seen_ref, inc_ref, inner_ref, outer_ref, factor_ref, cell_ref, slot_ref, out_ref,
-    state_ref, parts_ref,
+    state_ref, parts_ref, halo_ref,
 ):
     _, cols, rows = inc_ref.shape
     nobs = cell_ref.shape[1]
-    odd = on_odd_tile()
     state_ref[...] = jnp.zeros(state_ref.shape, F32)
     for field in range(3):
-        inner, outer = get_edge(inner_ref, field), get_edge(outer_ref, field)
-        state_ref[field, PAD - HALO : PAD] = jnp.where(odd, inner, outer)
+        edge = slice(REACH * field, REACH * (field + 1))
+        west, east = from_sides(inner_ref[edge], outer_ref[edge])
+        state_ref[field, PAD - REACH : PAD] = west
         state_ref[field, PAD : 3 * PAD] = inc_ref[field, 0 : 2 * PAD]
         state_ref[field, 3 * PAD : 5 * PAD] = inc_ref[field, cols - 2 * PAD : cols]
-        state_ref[field, 5 * PAD : 5 * PAD + HALO] = jnp.where(odd, outer, inner)
-    forward_steps(state_ref, factor_ref, parts_ref, ((PAD, 2 * PAD), (4 * PAD, 5 * PAD)))
+        state_ref[field, 5 * PAD : 5 * PAD + REACH] = east
+
+    def keep(moment, h):
+        at = corner(moment)
+        halo_ref[at] = h[PAD - moment - 1 : PAD]
+        halo_ref[CORNER + at.start : CORNER + at.stop] = h[5 * PAD : 5 * PAD + moment + 1]
+
+    places = ((PAD, 2 * PAD), (4 * PAD, 5 * PAD))
+    forward_steps(state_ref, factor_ref, parts_ref, places, keep)
+    copies = out_ref.shape[0]
+    tiles = rows // 128
+    base = nobs // 128
+    for i in range(tiles):
+        lanes = slice(128 * i, 128 * (i + 1))
+        for first, height in ((0, 8), (8, 4)):
+            line = base + first * tiles + height * i
+            value = halo_ref[first : first + height, lanes]
+            out_ref[:, line : line + height, :] = jnp.broadcast_to(value[None], (copies, height, 128))
     near = 2 * PAD
     chunk = 512
     for start in range(0, nobs, chunk):
@@ -277,10 +354,11 @@
     return call(
         border_kernel,
         "border",
-        floats(copies, cell.shape[1] // 128, 128),
+        floats(copies, (cell.shape[1] + 2 * CORNER * rows) // 128, 128),
         [
             pltpu.VMEM((3, 6 * PAD, rows), F32),
             pltpu.VMEM((4 * STEPS * PAD, rows), BF16),
+            pltpu.VMEM((16, rows), F32),
         ],
         10**9,
     )(seen, inc, inner, outer, factors, cell, slot)
@@ -301,98 +379,47 @@
         state_ref[2] = v
 
 
-def placed(spots, spot, weighted):
-    spot_hot = lax.broadcasted_iota(jnp.int32, (spots, spot.shape[1]), 0) == spot
-    return jnp.concatenate(split_two(jnp.where(spot_hot, weighted, 0.0)), axis=0)
-
-
-def gather_force(force_ref, part, start):
-    spots = force_ref.shape[0]
-    part = part[0:spots] + part[spots : 2 * spots]
-    if start == 0:
-        force_ref[...] = part
-    else:
-        force_ref[...] += part
-
-
-def edge_adjoint_kernel(
-    seen_ref, weight_ref, cell_ref, slot_ref, lines_ref, factor_ref,
-    weighted_ref, force_ref, inner_ref, outer_ref, state_ref, *, cols,
-):
-    rows = factor_ref.shape[1]
-    nobs = cell_ref.shape[1]
-    near = 2 * PAD
-    chunk = 512
-    seen = jnp.sum(seen_ref[...], axis=0)
-    upright = jnp.transpose(lax.shift_right_logical(lines_ref[...], cols.bit_length() - 1))
-    ids = lax.broadcasted_iota(jnp.int16, (128, rows), 1)
-    for start in range(0, nobs, chunk):
-        here = slice(start, start + chunk)
-        _, slot, col = rows_and_spots(cell_ref[:, here], slot_ref[:, here], cols)
-        lines = range(start // 128, (start + chunk) // 128)
-        weighted = weight_ref[:, here] * jnp.concatenate([seen[i : i + 1] for i in lines], axis=1)
-        weighted_ref[:, here] = weighted
-        east_spot = jnp.where(col >= cols - PAD, slot * near + (col - cols + near), -1)
-        spot = jnp.where(col < PAD, slot * near + col, east_spot)
-        hots = []
-        for i in lines:
-            row = jnp.broadcast_to(upright[:, i : i + 1], (128, 128)).astype(jnp.int16)
-            row = jnp.concatenate([row] * (rows // 128), axis=1)
-            hots.append(jnp.where(ids == row, jnp.ones((), BF16), jnp.zeros((), BF16)))
-        part = dot(placed(STEPS * near, spot, weighted), jnp.concatenate(hots, axis=0), NN)
-        gather_force(force_ref, part, start)
-
-    def add_force(moment):
-        state_ref[0, PAD : 3 * PAD] += force_ref[moment * near : (moment + 1) * near]
-
-    backward_steps(state_ref, factor_ref, add_force)
-    odd = on_odd_tile()
-    for field in range(3):
-        west = state_ref[field, PAD - HALO : PAD]
-        east = state_ref[field, 3 * PAD : 3 * PAD + HALO]
-        put_edge(inner_ref, field, 0, jnp.where(odd, west, east))
-        put_edge(outer_ref, field, 0, jnp.where(odd, east, west))
-
-
-def edge_adjoint(seen, weight, cell, slot, factors, cols):
-    rows = factors.shape[1]
-    nobs = cell.shape[1]
-    return call(
-        lambda *refs: edge_adjoint_kernel(*refs, cols=cols),
-        "edge_adjoint",
-        [floats(1, nobs), floats(2 * STEPS * PAD, rows), edge_floats(rows), edge_floats(rows)],
-        [pltpu.VMEM((3, 4 * PAD, rows), F32)],
-        10**9,
-    )(seen, weight, cell, slot, cell.reshape(nobs // 128, 128), factors)
-
-
 def three_products(parts_ref, loc_ref, low_ref, lines):
     both = dot(parts_ref[...], loc_ref[...], NN)
     rest = dot(parts_ref[0:lines].astype(BF16), low_ref[...], NN)
     return both[0:lines] + both[lines : 2 * lines] + rest
 
 
-def adjoint_kernel(
-    weighted_ref, edge_ref, cell_ref, slot_ref, factor_ref, loc_ref, low_ref, pert_ref, dir_ref,
-    img_ref, state_ref, force_ref, parts_ref,
+def finish_kernel(
+    seen_ref, weight_ref, cell_ref, slot_ref, inner_ref, outer_ref, factor_ref, loc_ref, low_ref,
+    pert_ref, dir_ref, res_ref, img_ref, sums_ref, state_ref, force_ref, parts_ref, halo_ref,
 ):
     members, cols, rows = dir_ref.shape
     nobs = cell_ref.shape[1]
-    count = cols - 2 * PAD
+    spots = STEPS * cols
     chunk = 512
+    tiles = rows // 128
+    base = nobs // 128
+    seen = jnp.sum(seen_ref[...], axis=0)
+    for first, height in ((0, 8), (8, 4)):
+        lines = [base + first * tiles + height * i for i in range(tiles)]
+        halo_ref[first : first + height] = jnp.concatenate(
+            [seen[i : i + height] for i in lines], axis=1
+        )
+    tail = slice(3 * REACH, 3 * REACH + CORNER)
+    west, east = from_sides(inner_ref[tail], outer_ref[tail])
+    halo_ref[0:CORNER] *= west
+    halo_ref[CORNER : 2 * CORNER] *= east
     for start in range(0, nobs, chunk):
         here = slice(start, start + chunk)
         row, slot, col = rows_and_spots(cell_ref[:, here], slot_ref[:, here], cols)
-        within = (col >= PAD) & (col < cols - PAD)
-        spot = jnp.where(within, slot * count + (col - PAD), -1)
-        hot = placed(STEPS * count, spot, weighted_ref[:, here])
+        lines = range(start // 128, (start + chunk) // 128)
+        weighted = weight_ref[:, here] * jnp.concatenate([seen[i : i + 1] for i in lines], axis=1)
+        hot = placed(spots, slot * cols + col, weighted)
         gather_force(force_ref, dot(hot, one_hot_rows(row, rows), NT), start)
 
     def add_force(moment):
-        near = 2 * PAD * moment
-        state_ref[0, PAD : 2 * PAD] += edge_ref[near : near + PAD]
-        state_ref[0, 2 * PAD : cols] += force_ref[moment * count : (moment + 1) * count]
-        state_ref[0, cols : PAD + cols] += edge_ref[near + PAD : near + 2 * PAD]
+        at = corner(moment)
+        state_ref[0, PAD - moment - 1 : PAD] += halo_ref[at]
+        state_ref[0, PAD : PAD + cols] += force_ref[moment * cols : (moment + 1) * cols]
+        state_ref[0, PAD + cols : PAD + cols + moment + 1] += halo_ref[
+            CORNER + at.start : CORNER + at.stop
+        ]
 
     backward_steps(state_ref, factor_ref, add_force)
     lines = members * cols
@@ -404,58 +431,11 @@
         parts_ref[lines + m * cols : lines + (m + 1) * cols] = remainder(projected)
     pulled = three_products(parts_ref, loc_ref, low_ref, lines)
     img_ref[...] = dir_ref[...] + pulled.reshape(members, cols, rows)
-
-
-def own_image(weighted, edge, cell, slot, factors, loc, low, pert, direction):
-    members, cols, rows = direction.shape
-    return call(
-        adjoint_kernel,
-        "adjoint",
-        floats(members, cols, rows),
-        [
-            pltpu.VMEM((3, cols + 2 * PAD, rows), F32),
-            pltpu.VMEM((STEPS * (cols - 2 * PAD), rows), F32),
-            pltpu.VMEM((2 * members * cols, rows), F32),
-        ],
-        4 * 10**9,
-    )(weighted, edge, cell, slot, factors, loc, low, pert, direction)
-
-
-def closing_kernel(
-    loc_ref, low_ref, own_ref, inner_ref, outer_ref, pert_ref, dir_ref, res_ref, img_ref, sums_ref,
-    edge_ref, parts_ref,
-):
-    members, cols, rows = dir_ref.shape
-    near = 2 * PAD
-    lines = members * near
-    odd = on_odd_tile()
-    edge_ref[...] = jnp.zeros(edge_ref.shape, F32)
-    for field in range(3):
-        inner, outer = get_edge(inner_ref, field), get_edge(outer_ref, field)
-        edge_ref[field, 0:HALO] = jnp.where(odd, inner, outer)
-        edge_ref[field, near - HALO : near] = jnp.where(odd, outer, inner)
-    for m in range(members):
-        west = jnp.zeros((PAD, rows), F32)
-        east = jnp.zeros((PAD, rows), F32)
-        for field in range(3):
-            west += pert_ref[m, field, 0:PAD].astype(F32) * edge_ref[field, 0:PAD]
-            east += pert_ref[m, field, cols - PAD : cols].astype(F32) * edge_ref[field, PAD:near]
-        projected = jnp.concatenate([west, east], axis=0)
-        parts_ref[m * near : (m + 1) * near] = projected
-        parts_ref[lines + m * near : lines + (m + 1) * near] = remainder(projected)
-    pulled = three_products(parts_ref, loc_ref, low_ref, lines)
     totals = [jnp.zeros((8, rows), F32) for _ in range(4)]
     for m in range(members):
-        for start in range(0, cols, PAD):
-            here = slice(start, start + PAD)
-            image = own_ref[m, here]
-            if start == 0:
-                image = image + pulled[m * near : m * near + PAD]
-            if start == cols - PAD:
-                image = image + pulled[m * near + PAD : (m + 1) * near]
-            img_ref[m, here] = image
-            way = dir_ref[m, here]
-            left = res_ref[m, here]
+        for start in range(0, cols, 8):
+            here = slice(start, start + 8)
+            image, way, left = img_ref[m, here], dir_ref[m, here], res_ref[m, here]
             totals[0] += left * left
             totals[1] += way * image
             totals[2] += left * image
@@ -468,18 +448,22 @@
     sums_ref[...] = jnp.broadcast_to(packed, sums_ref.shape)
 
 
-def image_and_sums(loc, low, own, inner, outer, pert, direction, residual, copies):
+def image_and_sums(
+    seen, weight, cell, slot, inner, outer, factors, loc, low, pert, direction, residual, copies
+):
     members, cols, rows = direction.shape
     return call(
-        closing_kernel,
-        "closing",
+        finish_kernel,
+        "finish",
         [floats(members, cols, rows), floats(copies, 128)],
         [
-            pltpu.VMEM((3, 2 * PAD, rows), F32),
-            pltpu.VMEM((4 * members * PAD, rows), F32),
+            pltpu.VMEM((3, cols + 2 * PAD, rows), F32),
+            pltpu.VMEM((STEPS * cols, rows), F32),
+            pltpu.VMEM((2 * members * cols, rows), F32),
+            pltpu.VMEM((16, rows), F32),
         ],
-        5 * 10**8,
-    )(loc, low, own, inner, outer, pert, direction, residual)
+        4 * 10**9,
+    )(seen, weight, cell, slot, inner, outer, factors, loc, low, pert, direction, residual)
 
 
 def update_kernel(
@@ -538,18 +522,15 @@
     control_t, residual_t, direction_t = turned(control), turned(residual), turned(direction)
     pert = jnp.swapaxes(ens_perturb, 2, 3)
     cell, slot, weight = obs_cell[None], obs_slot[None], obs_weight[None]
-    inc, inner, outer, loc, low = partial_increment(localize, direction_t, pert)
+    lists = [x.reshape(-1, 128) for x in (obs_cell, obs_slot, obs_weight)]
+    inc, inner, outer, loc, low = partial_increment(localize, direction_t, pert, lists)
     inner, outer = swapped(inner, outer)
     seen = inner_observed(inc, factors, cell, slot)
     seen = observed_parts(seen, inc, inner, outer, factors, cell, slot, lax.axis_size(ENS))
     seen = lax.all_to_all(seen, ENS, 0, 0, tiled=True)
-    weighted, edge, inner, outer = edge_adjoint(seen, weight, cell, slot, factors, cols)
-    inner, outer = swapped(inner, outer)
-    image = own_image(
-        weighted, edge, cell, slot, factors, loc, low, pert, direction_t
-    )
     image, sums = image_and_sums(
-        loc, low, image, inner, outer, pert, direction_t, residual_t, lax.axis_size(ENS_LON)
+        seen, weight, cell, slot, inner, outer, factors, loc, low, pert, direction_t, residual_t,
+        lax.axis_size(ENS_LON),
     )
     sums = lax.all_to_all(sums, ENS_LON, 0, 0, tiled=True)
     results = updated(sums, control_t, residual_t, direction_t, image)

time: 62.1 us -> 62.9 us (1.013)
  blocking collectives: 32.1 us -> 40.6 us
  starting transfers between devices: 10.5 us -> 3.29 us
  Pallas kernels: 18.3 us -> 17.4 us
    ppermute x2 -> x1, starting transfers between devices: 10.5 us -> 3.29 us  [swapped(): lax.ppermute(inner, LON, inner_pairs)]
    all_to_all x1, blocking collectives: 19.4 us -> 26.4 us  [body(): sums = lax.all_to_all(sums, ENS_LON, 0, 0, tiled=True)]
    pallas_call x4 -> x2, Pallas kernels: 9.4 us -> 7.67 us  [the longest x1 5.66 us: image_and_sums(): call(finish_kernel, 'finish', [floats(members, cols, rows), floats(copies...]
    all_to_all x1, blocking collectives: 12.7 us -> 14.2 us  [body(): seen = lax.all_to_all(seen, ENS, 0, 0, tiled=True)]
    pallas_call x1, Pallas kernels: 4.18 us -> 4.9 us  [partial_increment(): call(increment_kernel, 'increment', [floats(3, cols, rows), edge_floats(r...]
  transfers between devices with their start and end apart: 4 -> 2, of which waited for: 0 -> 1; matrix products, arithmetic and copies ran while one was open for 0% -> 0% of each run, Pallas kernels for 13% -> 5%
where the time goes in v6:
time: 62.9 us; the launch traced here: 62.8 us
  blocking collectives  40.6 us (65%)
  Pallas kernels  17.4 us (28%)
  starting transfers between devices  3.29 us (5%)
  between operations  0.92 us (1%)
    all_to_all x1, blocking collectives, body(): sums = lax.all_to_all(sums, ENS_LON, 0, 0, tiled=True)  26.4 us
    all_to_all x1, blocking collectives, body(): seen = lax.all_to_all(seen, ENS, 0, 0, tiled=True)  14.2 us
    pallas_call x1, Pallas kernels, image_and_sums(): call(finish_kernel, 'finish', [floats(members, cols, rows), floats(copies...  5.66 us
    pallas_call x1, Pallas kernels, partial_increment(): call(increment_kernel, 'increment', [floats(3, cols, rows), edge_floats(r...  4.9 us
    pallas_call x1, Pallas kernels, inner_observed(): call(forward_kernel, 'forward', floats(1, cell.shape[1]), [pltpu.VMEM((3,...  3.36 us
    ppermute x1, starting transfers between devices, swapped(): lax.ppermute(inner, LON, inner_pairs)  3.29 us
    pallas_call x1, Pallas kernels, observed_parts(): call(border_kernel, 'border', floats(copies, (cell.shape[1] + 2 * CORNER...  2.01 us
    pallas_call x1, Pallas kernels, updated(): call(update_kernel, 'update', [floats(*control.shape)] * 3, [pltpu.VMEM((...  1.43 us
  transfers between devices with their start and end apart: 2, of which 1 were waited for; matrix products, arithmetic and copies ran while one was open for 0% of the time, Pallas kernels for 5%

profile of v6, /device:TPU:1, one launch (start us, length us, event | category | flops | bytes accessed | tf_op | source)
XLA Modules:
  0.0 62.8 jit_solution(17653490318042086858)
XLA Ops:
  0.6 0.0 copy-start.7
  0.6 0.0 copy-start.4
  0.7 0.0 copy-start.5
  0.7 4.9 %increment.1 = (f32[3,64,1024]{2,1,0:T(8,128)S(1)}, f32[24,1024]{1,0:T(8,128)S(1)}, f32[24,1024]{1,0:T(8,128)S(1)}, f32[1024,1024]{1,0:T(8,128)S(1)}, bf16[1024,1024]{1,0:T(8,128)(2,1)S(1)}) custom-call(f32[1024,1024]{1,0:T(8,128)} %loc_hbm.1, f32[2,64,1024]{2,1,0:T(8,128)} %bitcast.17, bf16[2,3,64,1024]{3,2,1,0:T(8,128)(2,1)} %bitcast.20, ...), custom_call_target="tpu_custom_call" | custom-call | flops 1000000000 | bytes 1048576 | tf_op jit(solution)/shard_map/increment/pallas_call | solution.py:230
  5.6 3.3 %collective-permute-start = (f32[24,1024]{1,0:T(8,128)S(1)}, f32[24,1024]{1,0:T(8,128)S(1)}, u32[]{:S(2)}, u32[]{:S(2)}) collective-permute-start(f32[24,1024]{1,0:T(8,128)S(1)} %get-tuple-element.14), channel_id=1, source_target_pairs={{0,1},{1,0},{2,3},{3,2},{4,5},{5,4},{6,7},{7,6},{8,9},{9,8},{10,11... | collective-permute-start | bytes 294920 | tf_op jit(solution)/shard_map/ppermute | solution.py:515
  8.9 0.0 collective-permute-start.1
  8.9 0.0 copy-done.7
  8.9 0.0 copy-done.4
  8.9 0.0 copy-done.5
  8.9 3.4 %forward.1.seen_ref = f32[1,4096]{1,0:T(1,128)S(1)} custom-call(f32[3,64,1024]{2,1,0:T(8,128)S(1)} %get-tuple-element.13.inc_ref, f32[2,1024]{1,0:T(2,128)S(1)} %copy-done.7, s32[1,4096]{1,0:T(1,128)S(1)} %bitcast.28, s32[1,4096]{1,0:T(1,128)S(1)} %bitcast.32), custom_call_target="tpu_custom_call" | custom-call | flops 4000000000 | bytes 1048576 | tf_op jit(solution)/shard_map/forward/pallas_call | solution.py:296
  12.2 0.0 copy-start
  12.3 0.0 copy-start.1
  12.3 0.0 copy-start.2
  12.3 0.0 copy-start.6
  12.3 0.0 collective-permute-done.inner_ref
  12.3 0.6 collective-permute-done.1.outer_ref
  12.9 2.0 %border.1 = f32[8,128,128]{2,1,0:T(8,128)S(1)} custom-call(f32[1,4096]{1,0:T(1,128)S(1)} %forward.1.seen_ref, f32[3,64,1024]{2,1,0:T(8,128)S(1)} %get-tuple-element.13.inc_ref, f32[24,1024]{1,0:T(8,128)S(1)} %collective-permute-done.inner_ref, f32[24,1024]{1,0:T(8,128)S(1)} %collective-permute-done.1.outer_ref, f32[2,1024]{1,0:T(2,128)S(1)} %copy-done.7, ...), custom_call_target="tpu_custom_call" | custom-call | flops 1000000000 | bytes 1048576 | tf_op jit(solution)/shard_map/border/pallas_call | solution.py:354
  14.9 14.2 %all_to_all.16.seen_ref = f32[8,128,128]{2,1,0:T(8,128)S(1)} all-to-all(f32[8,128,128]{2,1,0:T(8,128)S(1)} %border.1), channel_id=1, replica_groups=mesh['ens_0'=2,'ens_1'=4,'lon_0'=8,'lon_1'=2,'lon_2'=2] {'ens_0','ens_1'}, dimensions={0} | all-to-all | bytes 1048576 | tf_op jit(solution)/shard_map/all_to_all | solution.py:530
  29.1 0.0 copy-done
  29.1 0.0 copy-done.1
  29.1 0.0 copy-done.2
  29.1 0.0 copy-done.6
  29.1 0.0 copy-start.3
  29.1 5.7 %finish.1 = (f32[2,64,1024]{2,1,0:T(8,128)S(1)}, f32[256,128]{1,0:T(8,128)S(1)}) custom-call(f32[8,128,128]{2,1,0:T(8,128)S(1)} %all_to_all.16.seen_ref, f32[1,4096]{1,0:T(1,128)S(1)} %bitcast.36, s32[1,4096]{1,0:T(1,128)S(1)} %bitcast.30, s32[1,4096]{1,0:T(1,128)S(1)} %bitcast.34, f32[24,1024]{1,0:T(8,128)S(1)} %collective-permute-done.inner_ref, ...), custom_call_target="tpu_custom_call" | custom-call | flops 4000000000 | bytes 1048576 | tf_op jit(solution)/shard_map/finish/pallas_call | solution.py:455
  34.8 26.4 %all_to_all.17 = f32[256,1,128]{2,1,0:T(1,128)S(1)} all-to-all(f32[256,1,128]{2,1,0:T(1,128)S(1)} %bitcast.26), channel_id=1, replica_groups=mesh['ens_0'=2,'ens_1'=4,'lon_0'=8,'lon_1'=2,'lon_2'=2] {'ens_0','ens_1'..., dimensions={0} | all-to-all | bytes 262144 | tf_op jit(solution)/shard_map/all_to_all | solution.py:535
  61.2 0.0 copy-done.3
  61.2 1.4 %update.1 = (f32[2,64,1024]{2,1,0:T(8,128)}, f32[2,64,1024]{2,1,0:T(8,128)}, f32[2,64,1024]{2,1,0:T(8,128)}) custom-call(f32[256,128]{1,0:T(8,128)S(1)} %bitcast.25, f32[2,64,1024]{2,1,0:T(8,128)S(1)} %bitcast.24, f32[2,64,1024]{2,1,0:T(8,128)S(1)} %bitcast.23, f32[2,64,1024]{2,1,0:T(8,128)S(1)} %bitcast.19, f32[2,64,1024]{2,1,0:T(8,128)S(1)} %get-tuple-element.19.img_ref), custom_call_target="tpu_custom_call" | custom-call | flops 10000000 | bytes 1048576 | tf_op jit(solution)/shard_map/update/pallas_call | solution.py:500
Async XLA Ops:
  0.6 8.2 %copy-start.7 = (f32[2,1024]{1,0:T(2,128)S(1)}, f32[2,1024]{1,0:T(2,128)}, u32[]{:S(2)}) copy-start(f32[2,1024]{1,0:T(2,128)} %constant.2.clone.factor_ref) | copy-start | bytes 24580
  0.6 8.2 %copy-start.4 = (s32[4096]{0:T(1024)S(1)}, s32[4096]{0:T(1024)}, u32[]{:S(2)}) copy-start(s32[4096]{0:T(1024)} %param.14) | copy-start | bytes 49156
  0.7 8.2 %copy-start.5 = (s32[4096]{0:T(1024)S(1)}, s32[4096]{0:T(1024)}, u32[]{:S(2)}) copy-start(s32[4096]{0:T(1024)} %param.15) | copy-start | bytes 49156
  5.6 6.7 %collective-permute-start = (f32[24,1024]{1,0:T(8,128)S(1)}, f32[24,1024]{1,0:T(8,128)S(1)}, u32[]{:S(2)}, u32[]{:S(2)}) collective-permute-start(f32[24,1024]{1,0:T(8,128)S(1)} %get-tuple-element.14), channel_id=1, source_target_pairs={{0,1},{1,0},{2,3},{3,2},{4,5},{5,4},{6,7},{7,6},{8,9},{9,8},{10,11... | collective-permute-start | bytes 294920 | tf_op jit(solution)/shard_map/ppermute | solution.py:515
  8.9 4.0 %collective-permute-start.1 = (f32[24,1024]{1,0:T(8,128)S(1)}, f32[24,1024]{1,0:T(8,128)S(1)}, u32[]{:S(2)}, u32[]{:S(2)}) collective-permute-start(f32[24,1024]{1,0:T(8,128)S(1)} %get-tuple-element.15), channel_id=1, source_target_pairs={{0,31},{1,2},{2,1},{3,4},{4,3},{5,6},{6,5},{7,8},{8,7},{9,10},{10,... | collective-permute-start | bytes 294920 | tf_op jit(solution)/shard_map/ppermute | solution.py:515
  12.2 16.9 %copy-start = (f32[2,1024,64]{1,2,0:T(8,128)S(1)}, f32[2,1024,64]{1,2,0:T(8,128)}, u32[]{:S(2)}) copy-start(f32[2,1024,64]{1,2,0:T(8,128)} %param.11) | copy-start | bytes 1572868
  12.3 16.8 %copy-start.1 = (bf16[2,3,1024,64]{2,3,1,0:T(8,128)(2,1)S(1)}, bf16[2,3,1024,64]{2,3,1,0:T(8,128)(2,1)}, u32[]{:S(2)}) copy-start(bf16[2,3,1024,64]{2,3,1,0:T(8,128)(2,1)} %param.12) | copy-start | bytes 2359300
  12.3 16.8 %copy-start.2 = (f32[2,1024,64]{1,2,0:T(8,128)S(1)}, f32[2,1024,64]{1,2,0:T(8,128)}, u32[]{:S(2)}) copy-start(f32[2,1024,64]{1,2,0:T(8,128)} %param.10) | copy-start | bytes 1572868
  12.3 16.8 %copy-start.6 = (f32[4096]{0:T(1024)S(1)}, f32[4096]{0:T(1024)}, u32[]{:S(2)}) copy-start(f32[4096]{0:T(1024)} %param.16) | copy-start | bytes 49156
  29.1 32.1 %copy-start.3 = (f32[2,1024,64]{1,2,0:T(8,128)S(1)}, f32[2,1024,64]{1,2,0:T(8,128)}, u32[]{:S(2)}) copy-start(f32[2,1024,64]{1,2,0:T(8,128)} %param.9) | copy-start | bytes 1572868

commit v7 on v5

--- a/solution.py
+++ b/solution.py
@@ -373,10 +373,9 @@
 
 
 def adjoint_kernel(
-    weighted_ref, edge_ref, cell_ref, slot_ref, factor_ref, loc_ref, low_ref, pert_ref, dir_ref,
-    img_ref, state_ref, force_ref, parts_ref,
+    weighted_ref, edge_ref, cell_ref, slot_ref, factor_ref, adj_ref, state_ref, force_ref
 ):
-    members, cols, rows = dir_ref.shape
+    _, cols, rows = adj_ref.shape
     nobs = cell_ref.shape[1]
     count = cols - 2 * PAD
     chunk = 512
@@ -395,67 +394,49 @@
         state_ref[0, cols : PAD + cols] += edge_ref[near + PAD : near + 2 * PAD]
 
     backward_steps(state_ref, factor_ref, add_force)
+    for field in range(3):
+        adj_ref[field] = state_ref[field, PAD : PAD + cols]
+
+
+def tile_adjoint(weighted, edge, cell, slot, factors, cols):
+    rows = factors.shape[1]
+    return call(
+        adjoint_kernel,
+        "adjoint",
+        floats(3, cols, rows),
+        [
+            pltpu.VMEM((3, cols + 2 * PAD, rows), F32),
+            pltpu.VMEM((STEPS * (cols - 2 * PAD), rows), F32),
+        ],
+        4 * 10**9,
+    )(weighted, edge, cell, slot, factors)
+
+
+def image_kernel(
+    loc_ref, low_ref, adj_ref, inner_ref, outer_ref, pert_ref, dir_ref, res_ref,
+    img_ref, sums_ref, full_ref, parts_ref,
+):
+    members, cols, rows = dir_ref.shape
     lines = members * cols
+    odd = on_odd_tile()
+    full_ref[...] = adj_ref[...]
+    for field in range(3):
+        inner, outer = get_edge(inner_ref, field), get_edge(outer_ref, field)
+        full_ref[field, 0:HALO] += jnp.where(odd, inner, outer)
+        full_ref[field, cols - HALO : cols] += jnp.where(odd, outer, inner)
     for m in range(members):
-        projected = pert_ref[m, 0].astype(F32) * state_ref[0, PAD : PAD + cols]
-        projected += pert_ref[m, 1].astype(F32) * state_ref[1, PAD : PAD + cols]
-        projected += pert_ref[m, 2].astype(F32) * state_ref[2, PAD : PAD + cols]
+        projected = pert_ref[m, 0].astype(F32) * full_ref[0]
+        projected += pert_ref[m, 1].astype(F32) * full_ref[1]
+        projected += pert_ref[m, 2].astype(F32) * full_ref[2]
         parts_ref[m * cols : (m + 1) * cols] = projected
         parts_ref[lines + m * cols : lines + (m + 1) * cols] = remainder(projected)
     pulled = three_products(parts_ref, loc_ref, low_ref, lines)
     img_ref[...] = dir_ref[...] + pulled.reshape(members, cols, rows)
-
-
-def own_image(weighted, edge, cell, slot, factors, loc, low, pert, direction):
-    members, cols, rows = direction.shape
-    return call(
-        adjoint_kernel,
-        "adjoint",
-        floats(members, cols, rows),
-        [
-            pltpu.VMEM((3, cols + 2 * PAD, rows), F32),
-            pltpu.VMEM((STEPS * (cols - 2 * PAD), rows), F32),
-            pltpu.VMEM((2 * members * cols, rows), F32),
-        ],
-        4 * 10**9,
-    )(weighted, edge, cell, slot, factors, loc, low, pert, direction)
-
-
-def closing_kernel(
-    loc_ref, low_ref, own_ref, inner_ref, outer_ref, pert_ref, dir_ref, res_ref, img_ref, sums_ref,
-    edge_ref, parts_ref,
-):
-    members, cols, rows = dir_ref.shape
-    near = 2 * PAD
-    lines = members * near
-    odd = on_odd_tile()
-    edge_ref[...] = jnp.zeros(edge_ref.shape, F32)
-    for field in range(3):
-        inner, outer = get_edge(inner_ref, field), get_edge(outer_ref, field)
-        edge_ref[field, 0:HALO] = jnp.where(odd, inner, outer)
-        edge_ref[field, near - HALO : near] = jnp.where(odd, outer, inner)
-    for m in range(members):
-        west = jnp.zeros((PAD, rows), F32)
-        east = jnp.zeros((PAD, rows), F32)
-        for field in range(3):
-            west += pert_ref[m, field, 0:PAD].astype(F32) * edge_ref[field, 0:PAD]
-            east += pert_ref[m, field, cols - PAD : cols].astype(F32) * edge_ref[field, PAD:near]
-        projected = jnp.concatenate([west, east], axis=0)
-        parts_ref[m * near : (m + 1) * near] = projected
-        parts_ref[lines + m * near : lines + (m + 1) * near] = remainder(projected)
-    pulled = three_products(parts_ref, loc_ref, low_ref, lines)
     totals = [jnp.zeros((8, rows), F32) for _ in range(4)]
     for m in range(members):
-        for start in range(0, cols, PAD):
-            here = slice(start, start + PAD)
-            image = own_ref[m, here]
-            if start == 0:
-                image = image + pulled[m * near : m * near + PAD]
-            if start == cols - PAD:
-                image = image + pulled[m * near + PAD : (m + 1) * near]
-            img_ref[m, here] = image
-            way = dir_ref[m, here]
-            left = res_ref[m, here]
+        for start in range(0, cols, 8):
+            here = slice(start, start + 8)
+            image, way, left = img_ref[m, here], dir_ref[m, here], res_ref[m, here]
             totals[0] += left * left
             totals[1] += way * image
             totals[2] += left * image
@@ -468,18 +449,18 @@
     sums_ref[...] = jnp.broadcast_to(packed, sums_ref.shape)
 
 
-def image_and_sums(loc, low, own, inner, outer, pert, direction, residual, copies):
+def image_and_sums(loc, low, adj, inner, outer, pert, direction, residual, copies):
     members, cols, rows = direction.shape
     return call(
-        closing_kernel,
-        "closing",
+        image_kernel,
+        "image",
         [floats(members, cols, rows), floats(copies, 128)],
         [
-            pltpu.VMEM((3, 2 * PAD, rows), F32),
-            pltpu.VMEM((4 * members * PAD, rows), F32),
+            pltpu.VMEM((3, cols, rows), F32),
+            pltpu.VMEM((2 * members * cols, rows), F32),
         ],
-        5 * 10**8,
-    )(loc, low, own, inner, outer, pert, direction, residual)
+        10**9,
+    )(loc, low, adj, inner, outer, pert, direction, residual)
 
 
 def update_kernel(
@@ -545,11 +526,9 @@
     seen = lax.all_to_all(seen, ENS, 0, 0, tiled=True)
     weighted, edge, inner, outer = edge_adjoint(seen, weight, cell, slot, factors, cols)
     inner, outer = swapped(inner, outer)
-    image = own_image(
-        weighted, edge, cell, slot, factors, loc, low, pert, direction_t
-    )
+    adj = tile_adjoint(weighted, edge, cell, slot, factors, cols)
     image, sums = image_and_sums(
-        loc, low, image, inner, outer, pert, direction_t, residual_t, lax.axis_size(ENS_LON)
+        loc, low, adj, inner, outer, pert, direction_t, residual_t, lax.axis_size(ENS_LON)
     )
     sums = lax.all_to_all(sums, ENS_LON, 0, 0, tiled=True)
     results = updated(sums, control_t, residual_t, direction_t, image)

time: 62.1 us -> 62.3 us (level)
  blocking collectives: 32.1 us -> 33 us
  Pallas kernels: 18.3 us -> 17.6 us
    all_to_all x1, blocking collectives: 19.4 us -> 20.4 us  [body(): sums = lax.all_to_all(sums, ENS_LON, 0, 0, tiled=True)]
    pallas_call x2, Pallas kernels: 5.53 us -> 4.72 us  [the longest x1 3.37 us: tile_adjoint(): call(adjoint_kernel, 'adjoint', floats(3, cols, rows), [pltpu.VMEM((3, co...]
  transfers between devices with their start and end apart: 4 -> 4, of which waited for: 0 -> 0; matrix products, arithmetic and copies ran while one was open for 0% -> 0% of each run, Pallas kernels for 13% -> 11%
where the time goes in v7:
time: 62.3 us; the launch traced here: 62.1 us
  blocking collectives  33 us (53%)
  Pallas kernels  17.6 us (28%)
  starting transfers between devices  10.5 us (17%)
  between operations  0.96 us (2%)
    all_to_all x1, blocking collectives, body(): sums = lax.all_to_all(sums, ENS_LON, 0, 0, tiled=True)  20.4 us
    all_to_all x1, blocking collectives, body(): seen = lax.all_to_all(seen, ENS, 0, 0, tiled=True)  12.7 us
    ppermute x2, starting transfers between devices, swapped(): lax.ppermute(inner, LON, inner_pairs)  10.5 us
    pallas_call x1, Pallas kernels, partial_increment(): call(increment_kernel, 'increment', [floats(3, cols, rows), edge_floats(r...  4.18 us
    pallas_call x1, Pallas kernels, tile_adjoint(): call(adjoint_kernel, 'adjoint', floats(3, cols, rows), [pltpu.VMEM((3, co...  3.37 us
    pallas_call x1, Pallas kernels, inner_observed(): call(forward_kernel, 'forward', floats(1, cell.shape[1]), [pltpu.VMEM((3,...  3.36 us
    pallas_call x1, Pallas kernels, observed_parts(): call(border_kernel, 'border', floats(copies, cell.shape[1] // 128, 128),...  1.96 us
    pallas_call x1, Pallas kernels, edge_adjoint(): call(lambda *refs: edge_adjoint_kernel(*refs, cols=cols), 'edge_adjoint',...  1.93 us
  transfers between devices with their start and end apart: 4, of which 0 were waited for; matrix products, arithmetic and copies ran while one was open for 0% of the time, Pallas kernels for 11%

profile of v7, /device:TPU:1, one launch (start us, length us, event | category | flops | bytes accessed | tf_op | source)
XLA Modules:
  0.0 62.1 jit_solution(3612389967620980955)
XLA Ops:
  0.6 0.0 copy-start.7
  0.6 0.0 copy-start.5
  0.7 0.0 copy-start.6
  0.7 4.2 %increment.1 = (f32[3,64,1024]{2,1,0:T(8,128)S(1)}, f32[72,128]{1,0:T(8,128)S(1)}, f32[72,128]{1,0:T(8,128)S(1)}, f32[1024,1024]{1,0:T(8,128)S(1)}, bf16[1024,1024]{1,0:T(8,128)(2,1)S(1)}) custom-call(f32[1024,1024]{1,0:T(8,128)} %loc_hbm.1, f32[2,64,1024]{2,1,0:T(8,128)} %bitcast.15, bf16[2,3,64,1024]{3,2,1,0:T(8,128)(2,1)} %bitcast.18), custom_call_target="tpu_custom_call" | custom-call | flops 1000000000 | bytes 1048576 | tf_op jit(solution)/shard_map/increment/pallas_call | solution.py:178
  4.9 3.3 %collective-permute-start = (f32[72,128]{1,0:T(8,128)S(1)}, f32[72,128]{1,0:T(8,128)S(1)}, u32[]{:S(2)}, u32[]{:S(2)}) collective-permute-start(f32[72,128]{1,0:T(8,128)S(1)} %get-tuple-element.20), channel_id=1, source_target_pairs={{0,1},{1,0},{2,3},{3,2},{4,5},{5,4},{6,7},{7,6},{8,9},{9,8},{10,11... | collective-permute-start | bytes 110600 | tf_op jit(solution)/shard_map/ppermute | solution.py:512
  8.1 0.0 collective-permute-start.1
  8.1 0.0 copy-done.7
  8.1 0.0 copy-done.5
  8.1 0.0 copy-done.6
  8.2 0.0 copy-start.4
  8.2 3.4 %forward.1.seen_ref = f32[1,4096]{1,0:T(1,128)S(1)} custom-call(f32[3,64,1024]{2,1,0:T(8,128)S(1)} %get-tuple-element.19.inc_ref, f32[2,1024]{1,0:T(2,128)S(1)} %copy-done.7, s32[1,4096]{1,0:T(1,128)S(1)} %bitcast.26, s32[1,4096]{1,0:T(1,128)S(1)} %bitcast.31), custom_call_target="tpu_custom_call" | custom-call | flops 4000000000 | bytes 1048576 | tf_op jit(solution)/shard_map/forward/pallas_call | solution.py:235
  11.5 0.0 collective-permute-done.inner_ref
  11.6 0.0 collective-permute-done.1.outer_ref
  11.6 2.0 %border.1 = f32[8,32,128]{2,1,0:T(8,128)S(1)} custom-call(f32[1,4096]{1,0:T(1,128)S(1)} %forward.1.seen_ref, f32[3,64,1024]{2,1,0:T(8,128)S(1)} %get-tuple-element.19.inc_ref, f32[72,128]{1,0:T(8,128)S(1)} %collective-permute-done.inner_ref, f32[72,128]{1,0:T(8,128)S(1)} %collective-permute-done.1.outer_ref, f32[2,1024]{1,0:T(2,128)S(1)} %copy-done.7, ...), custom_call_target="tpu_custom_call" | custom-call | flops 1000000000 | bytes 1048576 | tf_op jit(solution)/shard_map/border/pallas_call | solution.py:277
  13.5 12.7 %all_to_all.16.refs_0_ = f32[8,32,128]{2,1,0:T(8,128)S(1)} all-to-all(f32[8,32,128]{2,1,0:T(8,128)S(1)} %border.1), channel_id=1, replica_groups=mesh['ens_0'=2,'ens_1'=4,'lon_0'=8,'lon_1'=2,'lon_2'=2] {'ens_0','ens_1'}, dimensions={0} | all-to-all | bytes 262144 | tf_op jit(solution)/shard_map/all_to_all | solution.py:526
  26.2 0.0 copy-done.4
  26.2 1.9 %edge_adjoint.1 = (f32[1,4096]{1,0:T(1,128)S(1)}, f32[48,1024]{1,0:T(8,128)S(1)}, f32[72,128]{1,0:T(8,128)S(1)}, f32[72,128]{1,0:T(8,128)S(1)}) custom-call(f32[8,32,128]{2,1,0:T(8,128)S(1)} %all_to_all.16.refs_0_, f32[1,4096]{1,0:T(1,128)S(1)} %bitcast.25, s32[1,4096]{1,0:T(1,128)S(1)} %bitcast.28, s32[1,4096]{1,0:T(1,128)S(1)} %bitcast.33, ...), custom_call_target="tpu_custom_call" | custom-call | flops 1000000000 | bytes 1048576 | tf_op jit(solution)/shard_map/edge_adjoint/pallas_call | solution.py:360
  28.1 7.2 %collective-permute-start.2 = (f32[72,128]{1,0:T(8,128)S(1)}, f32[72,128]{1,0:T(8,128)S(1)}, u32[]{:S(2)}, u32[]{:S(2)}) collective-permute-start(f32[72,128]{1,0:T(8,128)S(1)} %get-tuple-element.24), channel_id=1, source_target_pairs={{0,1},{1,0},{2,3},{3,2},{4,5},{5,4},{6,7},{7,6},{8,9},{9,8},{10,11... | collective-permute-start | bytes 110600 | tf_op jit(solution)/shard_map/ppermute | solution.py:512
  35.3 0.0 collective-permute-start.3
  35.3 0.0 copy-start
  35.3 0.0 copy-start.1
  35.3 0.0 copy-start.2
  35.3 3.4 %adjoint.1.adj_ref = f32[3,64,1024]{2,1,0:T(8,128)S(1)} custom-call(f32[1,4096]{1,0:T(1,128)S(1)} %get-tuple-element.22.weighted_ref, f32[48,1024]{1,0:T(8,128)S(1)} %get-tuple-element.23.edge_ref, s32[1,4096]{1,0:T(1,128)S(1)} %bitcast.30, s32[1,4096]{1,0:T(1,128)S(1)} %bitcast.34, f32[2,1024]{1,0:T(2,128)S(1)} %copy-done.7), custom_call_target="tpu_custom_call" | custom-call | flops 4000000000 | bytes 1048576 | tf_op jit(solution)/shard_map/adjoint/pallas_call | solution.py:403
  38.7 0.0 collective-permute-done.2.inner_ref
  38.7 0.0 collective-permute-done.3.outer_ref
  38.7 0.0 copy-done
  38.8 0.0 copy-done.1
  38.8 0.0 copy-done.2
  38.8 0.0 copy-start.3
  38.8 1.3 %image.1 = (f32[2,64,1024]{2,1,0:T(8,128)S(1)}, f32[256,128]{1,0:T(8,128)S(1)}) custom-call(f32[1024,1024]{1,0:T(8,128)S(1)} %get-tuple-element.17.loc_ref, bf16[1024,1024]{1,0:T(8,128)(2,1)S(1)} %get-tuple-element.18.low_ref, f32[3,64,1024]{2,1,0:T(8,128)S(1)} %adjoint.1.adj_ref, f32[72,128]{1,0:T(8,128)S(1)} %collective-permute-done.2.inner_ref, ...), custom_call_target="tpu_custom_call" | custom-call | flops 1000000000 | bytes 1048576 | tf_op jit(solution)/shard_map/image/pallas_call | solution.py:454
  40.2 20.4 %all_to_all.17 = f32[256,1,128]{2,1,0:T(1,128)S(1)} all-to-all(f32[256,1,128]{2,1,0:T(1,128)S(1)} %bitcast.24), channel_id=1, replica_groups=mesh['ens_0'=2,'ens_1'=4,'lon_0'=8,'lon_1'=2,'lon_2'=2] {'ens_0','ens_1'..., dimensions={0} | all-to-all | bytes 262144 | tf_op jit(solution)/shard_map/all_to_all | solution.py:533
  60.5 0.0 copy-done.3
  60.5 1.4 %update.1 = (f32[2,64,1024]{2,1,0:T(8,128)}, f32[2,64,1024]{2,1,0:T(8,128)}, f32[2,64,1024]{2,1,0:T(8,128)}) custom-call(f32[256,128]{1,0:T(8,128)S(1)} %bitcast.23, f32[2,64,1024]{2,1,0:T(8,128)S(1)} %bitcast.22, f32[2,64,1024]{2,1,0:T(8,128)S(1)} %bitcast.21, f32[2,64,1024]{2,1,0:T(8,128)S(1)} %bitcast.17, f32[2,64,1024]{2,1,0:T(8,128)S(1)} %get-tuple-element.27.img_ref), custom_call_target="tpu_custom_call" | custom-call | flops 10000000 | bytes 1048576 | tf_op jit(solution)/shard_map/update/pallas_call | solution.py:497
Async XLA Ops:
  0.6 7.5 %copy-start.7 = (f32[2,1024]{1,0:T(2,128)S(1)}, f32[2,1024]{1,0:T(2,128)}, u32[]{:S(2)}) copy-start(f32[2,1024]{1,0:T(2,128)} %constant.2.clone.factor_ref.refs_5_) | copy-start | bytes 24580
  0.6 7.5 %copy-start.5 = (s32[4096]{0:T(1024)S(1)}, s32[4096]{0:T(1024)}, u32[]{:S(2)}) copy-start(s32[4096]{0:T(1024)} %param.14) | copy-start | bytes 49156
  0.7 7.5 %copy-start.6 = (s32[4096]{0:T(1024)S(1)}, s32[4096]{0:T(1024)}, u32[]{:S(2)}) copy-start(s32[4096]{0:T(1024)} %param.15) | copy-start | bytes 49156
  4.9 6.7 %collective-permute-start = (f32[72,128]{1,0:T(8,128)S(1)}, f32[72,128]{1,0:T(8,128)S(1)}, u32[]{:S(2)}, u32[]{:S(2)}) collective-permute-start(f32[72,128]{1,0:T(8,128)S(1)} %get-tuple-element.20), channel_id=1, source_target_pairs={{0,1},{1,0},{2,3},{3,2},{4,5},{5,4},{6,7},{7,6},{8,9},{9,8},{10,11... | collective-permute-start | bytes 110600 | tf_op jit(solution)/shard_map/ppermute | solution.py:512
  8.1 3.4 %collective-permute-start.1 = (f32[72,128]{1,0:T(8,128)S(1)}, f32[72,128]{1,0:T(8,128)S(1)}, u32[]{:S(2)}, u32[]{:S(2)}) collective-permute-start(f32[72,128]{1,0:T(8,128)S(1)} %get-tuple-element.21), channel_id=1, source_target_pairs={{0,31},{1,2},{2,1},{3,4},{4,3},{5,6},{6,5},{7,8},{8,7},{9,10},{10,... | collective-permute-start | bytes 110600 | tf_op jit(solution)/shard_map/ppermute | solution.py:512
  8.2 18.0 %copy-start.4 = (f32[4096]{0:T(1024)S(1)}, f32[4096]{0:T(1024)}, u32[]{:S(2)}) copy-start(f32[4096]{0:T(1024)} %param.16) | copy-start | bytes 49156
  28.1 10.6 %collective-permute-start.2 = (f32[72,128]{1,0:T(8,128)S(1)}, f32[72,128]{1,0:T(8,128)S(1)}, u32[]{:S(2)}, u32[]{:S(2)}) collective-permute-start(f32[72,128]{1,0:T(8,128)S(1)} %get-tuple-element.24), channel_id=1, source_target_pairs={{0,1},{1,0},{2,3},{3,2},{4,5},{5,4},{6,7},{7,6},{8,9},{9,8},{10,11... | collective-permute-start | bytes 110600 | tf_op jit(solution)/shard_map/ppermute | solution.py:512
  35.3 3.4 %collective-permute-start.3 = (f32[72,128]{1,0:T(8,128)S(1)}, f32[72,128]{1,0:T(8,128)S(1)}, u32[]{:S(2)}, u32[]{:S(2)}) collective-permute-start(f32[72,128]{1,0:T(8,128)S(1)} %get-tuple-element.25), channel_id=1, source_target_pairs={{0,31},{1,2},{2,1},{3,4},{4,3},{5,6},{6,5},{7,8},{8,7},{9,10},{10,... | collective-permute-start | bytes 110600 | tf_op jit(solution)/shard_map/ppermute | solution.py:512
  35.3 3.4 %copy-start = (f32[2,1024,64]{1,2,0:T(8,128)S(1)}, f32[2,1024,64]{1,2,0:T(8,128)}, u32[]{:S(2)}) copy-start(f32[2,1024,64]{1,2,0:T(8,128)} %param.11) | copy-start | bytes 1572868
  35.3 3.4 %copy-start.1 = (bf16[2,3,1024,64]{2,3,1,0:T(8,128)(2,1)S(1)}, bf16[2,3,1024,64]{2,3,1,0:T(8,128)(2,1)}, u32[]{:S(2)}) copy-start(bf16[2,3,1024,64]{2,3,1,0:T(8,128)(2,1)} %param.12) | copy-start | bytes 2359300
  35.3 3.4 %copy-start.2 = (f32[2,1024,64]{1,2,0:T(8,128)S(1)}, f32[2,1024,64]{1,2,0:T(8,128)}, u32[]{:S(2)}) copy-start(f32[2,1024,64]{1,2,0:T(8,128)} %param.10) | copy-start | bytes 1572868
  38.8 21.8 %copy-start.3 = (f32[2,1024,64]{1,2,0:T(8,128)S(1)}, f32[2,1024,64]{1,2,0:T(8,128)}, u32[]{:S(2)}) copy-start(f32[2,1024,64]{1,2,0:T(8,128)} %param.9) | copy-start | bytes 1572868

commit v8 on v5

--- a/solution.py
+++ b/solution.py
@@ -76,10 +76,9 @@
     return h, -lon_diff(h), -lat_diff(h)
 
 
-def call(kernel, name, out_shape, scratch, flops, limit_mib=24, **options):
+def call(kernel, out_shape, scratch, flops, limit_mib=24, **options):
     return pl.pallas_call(
         kernel,
-        name=name,
         out_shape=out_shape,
         scratch_shapes=scratch,
         compiler_params=pltpu.CompilerParams(vmem_limit_bytes=limit_mib << 20),
@@ -177,7 +176,6 @@
     low = jax.ShapeDtypeStruct((rows, rows), BF16)
     return call(
         increment_kernel,
-        "increment",
         [floats(3, cols, rows), edge_floats(rows), edge_floats(rows), floats(rows, rows), low],
         [
             pltpu.VMEM(direction.shape, F32),
@@ -234,7 +232,6 @@
     _, cols, rows = inc.shape
     return call(
         forward_kernel,
-        "forward",
         floats(1, cell.shape[1]),
         [
             pltpu.VMEM((3, cols, rows), F32),
@@ -276,7 +273,6 @@
     rows = inc.shape[2]
     return call(
         border_kernel,
-        "border",
         floats(copies, cell.shape[1] // 128, 128),
         [
             pltpu.VMEM((3, 6 * PAD, rows), F32),
@@ -359,7 +355,6 @@
     nobs = cell.shape[1]
     return call(
         lambda *refs: edge_adjoint_kernel(*refs, cols=cols),
-        "edge_adjoint",
         [floats(1, nobs), floats(2 * STEPS * PAD, rows), edge_floats(rows), edge_floats(rows)],
         [pltpu.VMEM((3, 4 * PAD, rows), F32)],
         10**9,
@@ -410,7 +405,6 @@
     members, cols, rows = direction.shape
     return call(
         adjoint_kernel,
-        "adjoint",
         floats(members, cols, rows),
         [
             pltpu.VMEM((3, cols + 2 * PAD, rows), F32),
@@ -472,7 +466,6 @@
     members, cols, rows = direction.shape
     return call(
         closing_kernel,
-        "closing",
         [floats(members, cols, rows), floats(copies, 128)],
         [
             pltpu.VMEM((3, 2 * PAD, rows), F32),
@@ -485,7 +478,7 @@
 def update_kernel(
     sums_ref, control_ref, res_ref, dir_ref, img_ref, control_out, res_out, dir_out, new_ref, sems
 ):
-    members, cols, rows = dir_ref.shape
+    members, _, _ = dir_ref.shape
     total = jnp.sum(sums_ref[...], axis=0, keepdims=True)
     lane = lax.broadcasted_iota(jnp.int32, (1, 128), 1)
 
@@ -515,7 +508,6 @@
     members = control.shape[0]
     return call(
         update_kernel,
-        "update",
         [floats(*control.shape)] * 3,
         [pltpu.VMEM((3, *control.shape), F32), pltpu.SemaphoreType.DMA((3 * members,))],
         10**7,
@@ -528,7 +520,9 @@
     inner_pairs = [(i, i ^ 1) for i in range(count)]
     outer_pairs = [(i, ((i + 1) ^ 1) - 1) for i in range(count)]
     outer_pairs = [(source, target % count) for source, target in outer_pairs]
-    return lax.ppermute(inner, LON, inner_pairs), lax.ppermute(outer, LON, outer_pairs)
+    outer = lax.ppermute(outer, LON, outer_pairs)
+    inner = lax.ppermute(inner, LON, inner_pairs)
+    return inner, outer
 
 
 def body(control, residual, direction, ens_perturb, localize, obs_cell, obs_slot, obs_weight):

time: 62.1 us -> 62.1 us (level)
  no operation moved by 1% of the time
where the time goes in v8:
time: 62.1 us; the launch traced here: 61.9 us
  blocking collectives  32.1 us (52%)
  Pallas kernels  18.3 us (29%)
  starting transfers between devices  10.5 us (17%)
  between operations  0.95 us (2%)
    all_to_all x1, blocking collectives, body(): sums = lax.all_to_all(sums, ENS_LON, 0, 0, tiled=True)  19.4 us
    all_to_all x1, blocking collectives, body(): seen = lax.all_to_all(seen, ENS, 0, 0, tiled=True)  12.7 us
    ppermute x2, starting transfers between devices, swapped(): inner = lax.ppermute(inner, LON, inner_pairs)  10.5 us
    pallas_call x1, Pallas kernels, own_image(): call(adjoint_kernel, floats(members, cols, rows), [pltpu.VMEM((3, cols +...  4.51 us
    pallas_call x1, Pallas kernels, partial_increment(): call(increment_kernel, [floats(3, cols, rows), edge_floats(rows), edge_fl...  4.18 us
    pallas_call x1, Pallas kernels, inner_observed(): call(forward_kernel, floats(1, cell.shape[1]), [pltpu.VMEM((3, cols, rows...  3.32 us
    pallas_call x1, Pallas kernels, edge_adjoint(): call(lambda *refs: edge_adjoint_kernel(*refs, cols=cols), [floats(1, nobs...  1.94 us
    pallas_call x1, Pallas kernels, observed_parts(): call(border_kernel, floats(copies, cell.shape[1] // 128, 128), [pltpu.VME...  1.94 us
  transfers between devices with their start and end apart: 4, of which 0 were waited for; matrix products, arithmetic and copies ran while one was open for 0% of the time, Pallas kernels for 13%

profile of v8, /device:TPU:1, one launch (start us, length us, event | category | flops | bytes accessed | tf_op | source)
XLA Modules:
  0.0 61.9 jit_solution(13684412514404956517)
XLA Ops:
  0.6 0.0 copy-start.7
  0.6 0.0 copy-start.5
  0.7 0.0 copy-start.6
  0.7 4.2 %shard_map.112 = (f32[3,64,1024]{2,1,0:T(8,128)S(1)}, f32[72,128]{1,0:T(8,128)S(1)}, f32[72,128]{1,0:T(8,128)S(1)}, f32[1024,1024]{1,0:T(8,128)S(1)}, bf16[1024,1024]{1,0:T(8,128)(2,1)S(1)}) custom-call(f32[1024,1024]{1,0:T(8,128)} %loc_hbm.1, f32[2,64,1024]{2,1,0:T(8,128)} %bitcast.15, bf16[2,3,64,1024]{3,2,1,0:T(8,128)(2,1)} %bitcast.19), custom_call_target="tpu_custom_call" | custom-call | flops 1000000000 | bytes 1048576 | tf_op jit(solution)/shard_map/pallas_call | solution.py:177
  4.8 3.3 %collective-permute-start = (f32[72,128]{1,0:T(8,128)S(1)}, f32[72,128]{1,0:T(8,128)S(1)}, u32[]{:S(2)}, u32[]{:S(2)}) collective-permute-start(f32[72,128]{1,0:T(8,128)S(1)} %get-tuple-element.20), channel_id=1, source_target_pairs={{0,1},{1,0},{2,3},{3,2},{4,5},{5,4},{6,7},{7,6},{8,9},{9,8},{10,11... | collective-permute-start | bytes 110600 | tf_op jit(solution)/shard_map/ppermute | solution.py:524
  8.1 0.0 collective-permute-start.1
  8.1 0.0 copy-done.7
  8.1 0.0 copy-done.5
  8.1 0.0 copy-done.6
  8.2 0.0 copy-start.4
  8.2 3.3 %shard_map.113.seen_ref = f32[1,4096]{1,0:T(1,128)S(1)} custom-call(f32[3,64,1024]{2,1,0:T(8,128)S(1)} %get-tuple-element.19.inc_ref, f32[2,1024]{1,0:T(2,128)S(1)} %copy-done.7, s32[1,4096]{1,0:T(1,128)S(1)} %bitcast.28, s32[1,4096]{1,0:T(1,128)S(1)} %bitcast.33), custom_call_target="tpu_custom_call" | custom-call | flops 4000000000 | bytes 1048576 | tf_op jit(solution)/shard_map/pallas_call | solution.py:233
  11.5 0.0 copy-start
  11.5 0.0 copy-start.1
  11.5 0.0 collective-permute-done.inner_ref
  11.5 0.0 collective-permute-done.1.outer_ref
  11.5 1.9 %shard_map.114 = f32[8,32,128]{2,1,0:T(8,128)S(1)} custom-call(f32[1,4096]{1,0:T(1,128)S(1)} %shard_map.113.seen_ref, f32[3,64,1024]{2,1,0:T(8,128)S(1)} %get-tuple-element.19.inc_ref, f32[72,128]{1,0:T(8,128)S(1)} %collective-permute-done.inner_ref, f32[72,128]{1,0:T(8,128)S(1)} %collective-permute-done.1.outer_ref, f32[2,1024]{1,0:T(2,128)S(1)} %copy-done.7, ...), custom_call_target="tpu_custom_call" | custom-call | flops 1000000000 | bytes 1048576 | tf_op jit(solution)/shard_map/pallas_call | solution.py:274
  13.5 12.7 %all_to_all.16.refs_0_ = f32[8,32,128]{2,1,0:T(8,128)S(1)} all-to-all(f32[8,32,128]{2,1,0:T(8,128)S(1)} %shard_map.114), channel_id=1, replica_groups=mesh['ens_0'=2,'ens_1'=4,'lon_0'=8,'lon_1'=2,'lon_2'=2] {'ens_0','ens_1'}, dimensions={0} | all-to-all | bytes 262144 | tf_op jit(solution)/shard_map/all_to_all | solution.py:539
  26.1 0.0 copy-done.4
  26.1 1.9 %shard_map.115 = (f32[1,4096]{1,0:T(1,128)S(1)}, f32[48,1024]{1,0:T(8,128)S(1)}, f32[72,128]{1,0:T(8,128)S(1)}, f32[72,128]{1,0:T(8,128)S(1)}) custom-call(f32[8,32,128]{2,1,0:T(8,128)S(1)} %all_to_all.16.refs_0_, f32[1,4096]{1,0:T(1,128)S(1)} %bitcast.27, s32[1,4096]{1,0:T(1,128)S(1)} %bitcast.30, s32[1,4096]{1,0:T(1,128)S(1)} %bitcast.35, ...), custom_call_target="tpu_custom_call" | custom-call | flops 1000000000 | bytes 1048576 | tf_op jit(solution)/shard_map/pallas_call | solution.py:356
  28.1 7.2 %collective-permute-start.2 = (f32[72,128]{1,0:T(8,128)S(1)}, f32[72,128]{1,0:T(8,128)S(1)}, u32[]{:S(2)}, u32[]{:S(2)}) collective-permute-start(f32[72,128]{1,0:T(8,128)S(1)} %get-tuple-element.24), channel_id=1, source_target_pairs={{0,1},{1,0},{2,3},{3,2},{4,5},{5,4},{6,7},{7,6},{8,9},{9,8},{10,11... | collective-permute-start | bytes 110600 | tf_op jit(solution)/shard_map/ppermute | solution.py:524
  35.3 0.0 collective-permute-start.3
  35.3 0.0 copy-done
  35.3 0.0 copy-done.1
  35.3 0.0 copy-start.2
  35.3 4.5 %shard_map.116.own_ref = f32[2,64,1024]{2,1,0:T(8,128)S(1)} custom-call(f32[1,4096]{1,0:T(1,128)S(1)} %get-tuple-element.22.weighted_ref, f32[48,1024]{1,0:T(8,128)S(1)} %get-tuple-element.23.edge_ref, s32[1,4096]{1,0:T(1,128)S(1)} %bitcast.32, s32[1,4096]{1,0:T(1,128)S(1)} %bitcast.36, f32[2,1024]{1,0:T(2,128)S(1)} %copy-done.7, ...), custom_call_target="tpu_custom_call" | custom-call | flops 4000000000 | bytes 1048576 | tf_op jit(solution)/shard_map/pallas_call | solution.py:406
  39.8 0.0 collective-permute-done.2.inner_ref
  39.9 0.0 collective-permute-done.3.outer_ref
  39.9 0.0 copy-done.2
  39.9 0.0 copy-start.3
  39.9 1.0 %shard_map.117 = (f32[2,64,1024]{2,1,0:T(8,128)S(1)}, f32[256,128]{1,0:T(8,128)S(1)}) custom-call(f32[1024,1024]{1,0:T(8,128)S(1)} %get-tuple-element.17.loc_ref, bf16[1024,1024]{1,0:T(8,128)(2,1)S(1)} %get-tuple-element.18.low_ref, f32[2,64,1024]{2,1,0:T(8,128)S(1)} %shard_map.116.own_ref, f32[72,128]{1,0:T(8,128)S(1)} %collective-permute-done.2.inner_ref, ...), custom_call_target="tpu_custom_call" | custom-call | flops 500000000 | bytes 1048576 | tf_op jit(solution)/shard_map/pallas_call | solution.py:467
  40.9 19.4 %all_to_all.17 = f32[256,1,128]{2,1,0:T(1,128)S(1)} all-to-all(f32[256,1,128]{2,1,0:T(1,128)S(1)} %bitcast.26), channel_id=1, replica_groups=mesh['ens_0'=2,'ens_1'=4,'lon_0'=8,'lon_1'=2,'lon_2'=2] {'ens_0','ens_1'..., dimensions={0} | all-to-all | bytes 262144 | tf_op jit(solution)/shard_map/all_to_all | solution.py:548
  60.3 0.0 copy-done.3
  60.3 1.4 %shard_map.118 = (f32[2,64,1024]{2,1,0:T(8,128)}, f32[2,64,1024]{2,1,0:T(8,128)}, f32[2,64,1024]{2,1,0:T(8,128)}) custom-call(f32[256,128]{1,0:T(8,128)S(1)} %bitcast.25, f32[2,64,1024]{2,1,0:T(8,128)S(1)} %bitcast.24, f32[2,64,1024]{2,1,0:T(8,128)S(1)} %bitcast.23, f32[2,64,1024]{2,1,0:T(8,128)S(1)} %bitcast.18, f32[2,64,1024]{2,1,0:T(8,128)S(1)} %get-tuple-element.27.img_ref), custom_call_target="tpu_custom_call" | custom-call | flops 10000000 | bytes 1048576 | tf_op jit(solution)/shard_map/pallas_call | solution.py:509
Async XLA Ops:
  0.6 7.5 %copy-start.7 = (f32[2,1024]{1,0:T(2,128)S(1)}, f32[2,1024]{1,0:T(2,128)}, u32[]{:S(2)}) copy-start(f32[2,1024]{1,0:T(2,128)} %constant.2.clone.factor_ref.refs_5_) | copy-start | bytes 24580
  0.6 7.5 %copy-start.5 = (s32[4096]{0:T(1024)S(1)}, s32[4096]{0:T(1024)}, u32[]{:S(2)}) copy-start(s32[4096]{0:T(1024)} %param.14) | copy-start | bytes 49156
  0.7 7.5 %copy-start.6 = (s32[4096]{0:T(1024)S(1)}, s32[4096]{0:T(1024)}, u32[]{:S(2)}) copy-start(s32[4096]{0:T(1024)} %param.15) | copy-start | bytes 49156
  4.8 6.7 %collective-permute-start = (f32[72,128]{1,0:T(8,128)S(1)}, f32[72,128]{1,0:T(8,128)S(1)}, u32[]{:S(2)}, u32[]{:S(2)}) collective-permute-start(f32[72,128]{1,0:T(8,128)S(1)} %get-tuple-element.20), channel_id=1, source_target_pairs={{0,1},{1,0},{2,3},{3,2},{4,5},{5,4},{6,7},{7,6},{8,9},{9,8},{10,11... | collective-permute-start | bytes 110600 | tf_op jit(solution)/shard_map/ppermute | solution.py:524
  8.1 3.4 %collective-permute-start.1 = (f32[72,128]{1,0:T(8,128)S(1)}, f32[72,128]{1,0:T(8,128)S(1)}, u32[]{:S(2)}, u32[]{:S(2)}) collective-permute-start(f32[72,128]{1,0:T(8,128)S(1)} %get-tuple-element.21), channel_id=1, source_target_pairs={{0,31},{1,2},{2,1},{3,4},{4,3},{5,6},{6,5},{7,8},{8,7},{9,10},{10,... | collective-permute-start | bytes 110600 | tf_op jit(solution)/shard_map/ppermute | solution.py:523
  8.2 18.0 %copy-start.4 = (f32[4096]{0:T(1024)S(1)}, f32[4096]{0:T(1024)}, u32[]{:S(2)}) copy-start(f32[4096]{0:T(1024)} %param.16) | copy-start | bytes 49156
  11.5 23.8 %copy-start = (f32[2,1024,64]{1,2,0:T(8,128)S(1)}, f32[2,1024,64]{1,2,0:T(8,128)}, u32[]{:S(2)}) copy-start(f32[2,1024,64]{1,2,0:T(8,128)} %param.11) | copy-start | bytes 1572868
  11.5 23.8 %copy-start.1 = (bf16[2,3,1024,64]{2,3,1,0:T(8,128)(2,1)S(1)}, bf16[2,3,1024,64]{2,3,1,0:T(8,128)(2,1)}, u32[]{:S(2)}) copy-start(bf16[2,3,1024,64]{2,3,1,0:T(8,128)(2,1)} %param.12) | copy-start | bytes 2359300
  28.1 11.8 %collective-permute-start.2 = (f32[72,128]{1,0:T(8,128)S(1)}, f32[72,128]{1,0:T(8,128)S(1)}, u32[]{:S(2)}, u32[]{:S(2)}) collective-permute-start(f32[72,128]{1,0:T(8,128)S(1)} %get-tuple-element.24), channel_id=1, source_target_pairs={{0,1},{1,0},{2,3},{3,2},{4,5},{5,4},{6,7},{7,6},{8,9},{9,8},{10,11... | collective-permute-start | bytes 110600 | tf_op jit(solution)/shard_map/ppermute | solution.py:524
  35.3 4.6 %collective-permute-start.3 = (f32[72,128]{1,0:T(8,128)S(1)}, f32[72,128]{1,0:T(8,128)S(1)}, u32[]{:S(2)}, u32[]{:S(2)}) collective-permute-start(f32[72,128]{1,0:T(8,128)S(1)} %get-tuple-element.25), channel_id=1, source_target_pairs={{0,31},{1,2},{2,1},{3,4},{4,3},{5,6},{6,5},{7,8},{8,7},{9,10},{10,... | collective-permute-start | bytes 110600 | tf_op jit(solution)/shard_map/ppermute | solution.py:523
  35.3 4.6 %copy-start.2 = (f32[2,1024,64]{1,2,0:T(8,128)S(1)}, f32[2,1024,64]{1,2,0:T(8,128)}, u32[]{:S(2)}) copy-start(f32[2,1024,64]{1,2,0:T(8,128)} %param.10) | copy-start | bytes 1572868
  39.9 20.5 %copy-start.3 = (f32[2,1024,64]{1,2,0:T(8,128)S(1)}, f32[2,1024,64]{1,2,0:T(8,128)}, u32[]{:S(2)}) copy-start(f32[2,1024,64]{1,2,0:T(8,128)} %param.9) | copy-start | bytes 1572868
